TPU v7x, 32 devices: a whole 2x2x4 slice. The times are simulated.
32 devices in a mesh: leaf: 8 (over z, y), sub: 4 (over x, core).
Axes of the slice: x: 2, y: 2, z: 4, core: 2. Of those that a mesh axis runs over, the one named last changes fastest.
Arguments:
- signal: bfloat16 [32, 65536], P(None, ('leaf', 'sub')), may hold values from -6 to 6
- row_basis: bfloat16 [64, 65536], P(None, ('leaf', 'sub')), may hold values from -0.375 to 0.375
- transfer: bfloat16 [512, 9, 32, 128], P(('leaf', 'sub')), may hold values from -0.5 to 0.5
- column_basis: bfloat16 [64, 65536], P(None, ('leaf', 'sub')), may hold values from -0.75 to 0.75
- near_blocks: bfloat16 [768, 128, 256], P(('leaf', 'sub')), may hold values from -0.375 to 0.375
- near_list: int32 [768, 2], P(('leaf', 'sub')), may hold values from -1 to 31, as said below
Outputs:
- result: float32 [32, 65536], P(None, ('leaf', 'sub'))
Inputs may be any that keep to these rules, and one draw needn't show every extreme that they name: `near_list`: on each device the live entries (column >= 0) fill a leading run of its 24 slots, 2 or more of them, and empty slots hold -1 in both places; a live entry has 0 <= column < 24 and column <= row <= column + 8. Devices 2m and 2m + 1 hold at most 24 live entries together, and some such pair holds 24.
All inputs are finite; a program needn't handle non-finite values.
Results may differ from a plain program's by a relative error of at most 0.0003.
Values may be sent and summed in bfloat16 or wider, within the bound.
No kernel may reach another device: no remote copies, remote signals or barrier semaphores. Data moves between devices by JAX's collectives and lax.ppermute only.
A program may use at most 128 MiB of HBM per device.

v0:
```python
import jax
import jax.numpy as jnp
from jax import lax
from jax.sharding import PartitionSpec as P

LEAF = 128


highest = lax.Precision.HIGHEST


def with_halo(cells, sides, width):
    for axis, dim in sides:
        count = lax.axis_size(axis)
        head = lax.slice_in_dim(cells, 0, width, axis=dim)
        tail = lax.slice_in_dim(cells, cells.shape[dim] - width, cells.shape[dim], axis=dim)
        cells = jnp.concatenate(
            [
                lax.ppermute(tail, axis, [(i, (i + 1) % count) for i in range(count)]),
                cells,
                lax.ppermute(head, axis, [((i + 1) % count, i) for i in range(count)]),
            ],
            axis=dim,
        )
    return cells


def swapped(shard, axis, distance):
    return lax.ppermute(shard, axis, [(i, i ^ 1 << distance) for i in range(lax.axis_size(axis))])


def from_behind(value, axis, steps):
    count = lax.axis_size(axis)
    pairs = [(source, (source + steps) % count) for source in range(count)]
    return lax.ppermute(value, axis, pairs)


def project(signal, row_basis):
    rhs_count = signal.shape[0] // 2
    rank_width = row_basis.shape[0] // 2
    leaves = signal.shape[1] // LEAF
    samples = signal.reshape(2, rhs_count, leaves, LEAF)
    basis_rows = row_basis.reshape(2, rank_width, leaves, LEAF)
    products = jnp.einsum(
        "xrlp,yqlp->xylrq", samples, basis_rows, preferred_element_type=jnp.float32
    )
    real_part = products[0, 0] + products[1, 1]
    imag_part = products[1, 0] - products[0, 1]
    return jnp.transpose(jnp.concatenate([real_part, imag_part], axis=-1), (1, 0, 2))


def block_form(weights):
    matrices = weights.astype(jnp.float32)
    rank_width = matrices.shape[1]
    pieces = []
    for offspring in range(2):
        real_part = matrices[:, :, 2 * offspring * rank_width : (2 * offspring + 1) * rank_width]
        imag_part = matrices[
            :, :, (2 * offspring + 1) * rank_width : (2 * offspring + 2) * rank_width
        ]
        upper_rows = jnp.concatenate([real_part, -imag_part], axis=2)
        lower_rows = jnp.concatenate([imag_part, real_part], axis=2)
        pieces.append(jnp.concatenate([upper_rows, lower_rows], axis=1))
    return jnp.concatenate(pieces, axis=1)


def apply_level(paired, weights):
    return jnp.einsum("rsm,smn->rsn", paired, block_form(weights), precision=highest)


def pair_local(coeffs, height):
    rhs_count, slot_count, doubled = coeffs.shape
    half_span = 2 ** (height - 1)
    grouped = coeffs.reshape(rhs_count, slot_count // (2 * half_span), 2, half_span, doubled)
    joined = jnp.concatenate([grouped[:, :, 0], grouped[:, :, 1]], axis=-1)
    twice = jnp.stack([joined, joined], axis=2)
    return twice.reshape(rhs_count, slot_count, 2 * doubled)


def swap_level(owned, partner_box, upper_bit, weights):
    low_side = jnp.where(upper_bit == 0, owned, partner_box)
    high_side = jnp.where(upper_bit == 0, partner_box, owned)
    return apply_level(jnp.concatenate([low_side, high_side], axis=-1), weights)


def evaluate(coeffs, column_basis):
    rhs_count, leaves, doubled = coeffs.shape
    rank_width = doubled // 2
    basis_rows = column_basis.astype(jnp.float32).reshape(2, rank_width, leaves, LEAF)
    real_coefficient = coeffs[:, :, :rank_width]
    imag_coef = coeffs[:, :, rank_width:]
    real_out = jnp.einsum(
        "rlq,qlp->rlp", real_coefficient, basis_rows[0], precision=highest
    ) - jnp.einsum("rlq,qlp->rlp", imag_coef, basis_rows[1], precision=highest)
    imag_out = jnp.einsum("rlq,qlp->rlp", imag_coef, basis_rows[0], precision=highest) + jnp.einsum(
        "rlq,qlp->rlp", real_coefficient, basis_rows[1], precision=highest
    )
    return jnp.concatenate([real_out, imag_out], axis=0).reshape(2 * rhs_count, leaves * LEAF)


def near_products(picked, blocks):
    products = jnp.einsum("scp,spj->scj", picked, blocks, preferred_element_type=jnp.float32)
    rhs_count = picked.shape[1] // 2
    real_part = products[:, :rhs_count, :LEAF] + products[:, rhs_count:, LEAF:]
    imag_part = products[:, rhs_count:, :LEAF] - products[:, :rhs_count, LEAF:]
    return jnp.concatenate([real_part, imag_part], axis=1)


def accumulate(output_values, col_index, box_count):
    selector = (col_index[:, None] == jnp.arange(box_count, dtype=jnp.int32)[None, :]).astype(
        jnp.float32
    )
    return jnp.einsum("sw,scj->cwj", selector, output_values, precision=highest)


def shards(signal, row_basis, transfer, column_basis, near_blocks, near_list):
    channels = signal.shape[0]
    box_count = signal.shape[1] // LEAF
    reach_boxes = box_count // 4
    local_levels = box_count.bit_length() - 1
    sub_bits = lax.axis_size("sub").bit_length() - 1
    count_of_leaves = lax.axis_size("leaf")
    leaf_bits = count_of_leaves.bit_length() - 1
    sub_index = lax.axis_index("sub")
    leaf_index = lax.axis_index("leaf")
    window = with_halo(signal, ((("leaf", "sub"), 1),), 2 * reach_boxes * LEAF)
    coeffs = project(signal, row_basis)
    for height in range(1, local_levels + 1):
        coeffs = apply_level(pair_local(coeffs, height), transfer[:, height - 1])
    for bit_place in range(sub_bits):
        partner_box = swapped(coeffs, "sub", bit_place)
        coeffs = swap_level(
            coeffs, partner_box, sub_index >> bit_place & 1, transfer[:, local_levels + bit_place]
        )
    for bit_place in range(leaf_bits):
        partner_box = swapped(coeffs, "leaf", bit_place)
        coeffs = swap_level(
            coeffs,
            partner_box,
            leaf_index >> bit_place & 1,
            transfer[:, local_levels + sub_bits + bit_place],
        )
    far_field = evaluate(coeffs, column_basis)
    leaf_tiles = window.reshape(channels, -1, LEAF)
    row_index = near_list[:, 0]
    col_index = near_list[:, 1]
    picked = jnp.transpose(jnp.take(leaf_tiles, jnp.maximum(row_index, 0), axis=1), (1, 0, 2))
    out_boxes = box_count + 2 * reach_boxes
    near_field = accumulate(near_products(picked, near_blocks), col_index, out_boxes)
    from_next = from_behind(near_field[:, :reach_boxes], ("leaf", "sub"), -1)
    from_prev = from_behind(near_field[:, box_count + reach_boxes :], ("leaf", "sub"), 1)
    center = near_field[:, reach_boxes : reach_boxes + box_count]
    center = center.at[:, :reach_boxes].add(from_prev)
    center = center.at[:, box_count - reach_boxes :].add(from_next)
    return far_field + center.reshape(channels, box_count * LEAF)


def solution(mesh):
    return jax.shard_map(
        shards,
        mesh=mesh,
        in_specs=(
            P(None, ("leaf", "sub")),
            P(None, ("leaf", "sub")),
            P(("leaf", "sub"), None, None, None),
            P(None, ("leaf", "sub")),
            P(("leaf", "sub"), None, None),
            P(("leaf", "sub"), None),
        ),
        out_specs=P(None, ("leaf", "sub")),
        check_vma=False,
    )
```

profile of v0, /device:TPU:0, one launch (start us, length us, event | category | flops | bytes accessed | tf_op | source)
XLA Modules:
  0.0 60.2 jit_solution(17310740215272328099)
XLA Ops:
  0.0 1.1 %copy.105 = bf16[8,8,16,128]{3,2,1,0:T(8,128)(2,1)S(1)} copy(bf16[8,8,16,128]{3,1,2,0:T(8,128)(2,1)} %bitcast.167) | data formatting | bytes 524288
  1.2 0.9 %copy.106 = bf16[4,8,16,128]{3,2,1,0:T(8,128)(2,1)S(1)} copy(bf16[4,8,16,128]{3,1,2,0:T(8,128)(2,1)} %bitcast.163) | data formatting | bytes 262144
  2.1 0.5 convolution_bitcast_fusion
  2.7 0.2 fusion.197
  2.9 0.3 copy.95
  3.3 0.2 slice_negate_fusion.1
  3.8 1.3 %fusion.124 = f32[16,64,16]{1,2,0:T(8,128)S(1)} fusion(f32[16,16,128]{2,0,1:T(8,128)S(1)} %bitcast.174, f32[16,32,32]{1,2,0:T(8,128)S(1)} %get-tuple-element.59, f32[16,32,32]{1,2,0:T(8,128)S(1)} %get-tuple-element.58, f32[16,32,32]{1,2,0:T(8,128)S(1)} %get-tuple-element.57, f32[16,32,32]{1,2,0:T(8,128)S(1)} %get-tuple-element.61, ...), kind=kOutput, calls=%fused_computation.134 | convolution fusion | flops 26083328 | bytes 589824 | tf_op jit(solution)/shard_map/rsm,smn->rsn/dot_general | solution.py:68
  5.2 0.3 copy.94
  5.7 1.3 %fusion.108 = f32[16,64,16]{1,2,0:T(8,128)S(1)} fusion(f32[16,16,128]{2,0,1:T(8,128)S(1)} %bitcast.169, f32[16,32,32]{1,2,0:T(8,128)S(1)} %get-tuple-element.53, f32[16,32,32]{1,2,0:T(8,128)S(1)} %get-tuple-element.52, f32[16,32,32]{1,2,0:T(8,128)S(1)} %get-tuple-element.51, f32[16,32,32]{1,2,0:T(8,128)S(1)} %get-tuple-element.55, ...), kind=kOutput, calls=%fused_computation.118 | convolution fusion | flops 26083328 | bytes 589824 | tf_op jit(solution)/shard_map/rsm,smn->rsn/dot_general | solution.py:68
  7.2 0.3 copy.93
  7.7 1.3 %fusion.92 = f32[16,64,16]{1,2,0:T(8,128)S(1)} fusion(f32[16,16,128]{2,0,1:T(8,128)S(1)} %bitcast.170, f32[16,32,32]{1,2,0:T(8,128)S(1)} %get-tuple-element.47, f32[16,32,32]{1,2,0:T(8,128)S(1)} %get-tuple-element.46, f32[16,32,32]{1,2,0:T(8,128)S(1)} %get-tuple-element.45, f32[16,32,32]{1,2,0:T(8,128)S(1)} %get-tuple-element.49, ...), kind=kOutput, calls=%fused_computation.102 | convolution fusion | flops 26083328 | bytes 589824 | tf_op jit(solution)/shard_map/rsm,smn->rsn/dot_general | solution.py:68
  9.1 0.3 copy.92
  9.7 1.3 %convolution_bitcast_fusion.6 = f32[16,16,64]{2,0,1:T(8,128)S(1)} fusion(f32[16,16,128]{2,0,1:T(8,128)S(1)} %bitcast.168, f32[16,32,32]{1,2,0:T(8,128)S(1)} %get-tuple-element.41, f32[16,32,32]{1,2,0:T(8,128)S(1)} %get-tuple-element.40, f32[16,32,32]{1,2,0:T(8,128)S(1)} %get-tuple-element.39, f32[16,32,32]{1,2,0:T(8,128)S(1)} %get-tuple-element.43, ...), kind=kOutput, calls=%fused_computation.7 | convolution fusion | flops 26083328 | bytes 589824 | tf_op jit(solution)/shard_map/rsm,smn->rsn/dot_general | solution.py:68
  11.0 0.5 collective-permute-start
  11.5 0.6 %fusion.199 = (bf16[32,1024]{1,0:T(8,128)(2,1)}, bf16[32,1024]{1,0:T(8,128)(2,1)S(1)}) fusion(bf16[32,2048]{1,0:T(8,128)(2,1)S(1)} %copy-done.2), kind=kLoop, calls=%fused_computation.284 | loop fusion | bytes 262144 | tf_op jit(solution)/shard_map/slice | solution.py:16
  12.2 6.6 %collective-permute-start.6 = (bf16[32,1024]{1,0:T(8,128)(2,1)S(1)}, bf16[32,1024]{1,0:T(8,128)(2,1)}, u32[]{:S(2)}, u32[]{:S(2)}) collective-permute-start(bf16[32,1024]{1,0:T(8,128)(2,1)S(1)} %get-tuple-element.117), channel_id=1, source_target_pairs={{1,0},{2,1},{3,2},{4,3},{5,4},{6,5},{7,6},{8,7},{9,8},{10,9},{11,1... | collective-permute-start | bytes 196616 | tf_op jit(solution)/shard_map/ppermute | solution.py:21
  18.7 0.3 copy.91
  19.1 1.2 %slice_negate_fusion.9 = (f32[16,32,32]{1,2,0:T(8,128)}, f32[16,32,32]{1,2,0:T(8,128)}, f32[16,32,32]{1,2,0:T(8,128)}, f32[16,32,32]{1,2,0:T(8,128)}, f32[16,32,32]{1,2,0:T(8,128)}, /*index=5*/f32[16,32,32]{1,2,0:T(8,128)}) fusion(f32[16,32,128]{1,2,0:T(8,128)S(1)} %bitcast_convert_fusion.4), kind=kLoop, calls=%fused_computation.273 | loop fusion | flops 32768 | bytes 655360 | tf_op jit(solution)/shard_map/neg | solution.py:61
  20.4 0.3 copy.90
  20.8 1.3 %slice_negate_fusion.11 = (f32[16,32,32]{1,2,0:T(8,128)}, f32[16,32,32]{1,2,0:T(8,128)}, f32[16,32,32]{1,2,0:T(8,128)}, f32[16,32,32]{1,2,0:T(8,128)}, f32[16,32,32]{1,2,0:T(8,128)}, /*index=5*/f32[16,32,32]{1,2,0:T(8,128)}) fusion(f32[16,32,128]{1,2,0:T(8,128)S(1)} %bitcast_convert_fusion.5), kind=kLoop, calls=%fused_computation.275 | loop fusion | flops 32768 | bytes 655360 | tf_op jit(solution)/shard_map/neg | solution.py:61
  22.0 0.3 copy.89
  22.4 1.2 %slice_negate_fusion.13 = (f32[16,32,32]{1,2,0:T(8,128)}, f32[16,32,32]{1,2,0:T(8,128)}, f32[16,32,32]{1,2,0:T(8,128)}, f32[16,32,32]{1,2,0:T(8,128)}, f32[16,32,32]{1,2,0:T(8,128)}, /*index=5*/f32[16,32,32]{1,2,0:T(8,128)}) fusion(f32[16,32,128]{1,2,0:T(8,128)S(1)} %bitcast_convert_fusion.6), kind=kLoop, calls=%fused_computation.277 | loop fusion | flops 32768 | bytes 655360 | tf_op jit(solution)/shard_map/neg | solution.py:61
  23.7 0.3 copy.88
  24.1 1.2 %slice_negate_fusion.15 = (f32[16,32,32]{1,2,0:T(8,128)}, f32[16,32,32]{1,2,0:T(8,128)}, f32[16,32,32]{1,2,0:T(8,128)}, f32[16,32,32]{1,2,0:T(8,128)}, f32[16,32,32]{1,2,0:T(8,128)}, /*index=5*/f32[16,32,32]{1,2,0:T(8,128)}) fusion(f32[16,32,128]{1,2,0:T(8,128)S(1)} %bitcast_convert_fusion.7), kind=kLoop, calls=%fused_computation.279 | loop fusion | flops 32768 | bytes 655360 | tf_op jit(solution)/shard_map/neg | solution.py:61
  25.3 0.3 copy.87
  25.8 1.0 %slice_negate_fusion.17 = (f32[16,32,32]{1,2,0:T(8,128)S(1)}, f32[16,32,32]{1,2,0:T(8,128)S(1)}, f32[16,32,32]{1,2,0:T(8,128)S(1)}, f32[16,32,32]{1,2,0:T(8,128)...) fusion(f32[16,32,128]{1,2,0:T(8,128)S(1)} %bitcast_convert_fusion.8), kind=kLoop, calls=%fused_computation.281 | loop fusion | flops 32768 | bytes 655360 | tf_op jit(solution)/shard_map/neg | solution.py:61
  26.8 0.9 %broadcast_select_fusion.1 = (f32[16,16,64]{2,0,1:T(8,128)S(1)}, f32[16,16,64]{2,0,1:T(8,128)S(1)}) fusion(f32[16,16,64]{2,0,1:T(8,128)S(1)} %convolution_bitcast_fusion.6, f32[16,16,64]{2,0,1:T(8,128)} %collective-permute-done, pred[]{:T(512)S(6)} %eq.39), kind=kLoop, calls=%fused_computation.237 | loop fusion | flops 32768 | bytes 262145 | tf_op jit(solution)/shard_map/jit(_where)/select_n | solution.py:81
  27.8 1.3 %convolution_bitcast_fusion.5 = f32[16,16,64]{2,0,1:T(8,128)S(1)} fusion(f32[16,32,32]{1,2,0:T(8,128)S(1)} %copy-done.26, f32[16,32,32]{1,2,0:T(8,128)S(1)} %copy-done.25, f32[16,32,32]{1,2,0:T(8,128)S(1)} %copy-done.24, f32[16,32,32]{1,2,0:T(8,128)S(1)} %copy-done.28, f32[16,32,32]{1,2,0:T(8,128)S(1)} %copy-done.27, f32[16,32,32]{1,2,0:T(8,128)S(1)} %copy-done.23, ...), kind=kOutput, calls=%fused_computation.6 | convolution fusion | flops 26116096 | bytes 589824 | tf_op jit(solution)/shard_map/rsm,smn->rsn/dot_general | solution.py:68
  29.2 0.9 %copy_bitcast_fusion.2 = bf16[32,32,128]{2,0,1:T(8,128)(2,1)S(1)} fusion(bf16[32,1024]{1,0:T(8,128)(2,1)} %collective-permute-done.6, bf16[32,2048]{1,0:T(8,128)(2,1)S(1)} %copy-done.2, bf16[32,1024]{1,0:T(8,128)(2,1)} %collective-permute-done.5), kind=kLoop, calls=%fused_computation.165 | loop fusion | flops 786432 | bytes 524288 | tf_op jit(solution)/shard_map/reshape | solution.py:144
  30.2 0.6 gather_fusion
  30.8 0.4 fusion.144
  31.3 0.5 fusion.140
  31.9 2.3 %collective-permute-done.1 = f32[16,16,64]{2,0,1:T(8,128)} collective-permute-done((f32[16,16,64]{2,0,1:T(8,128)S(1)}, f32[16,16,64]{2,0,1:T(8,128)}, u32[]{:S(2)}, u32[]{:S(2)}) %collective-permute-start.1) | collective-permute-done | bytes 65568 | tf_op jit(solution)/shard_map/ppermute | solution.py:29
  34.3 0.9 %broadcast_select_fusion.3 = (f32[16,16,64]{2,0,1:T(8,128)S(1)}, f32[16,16,64]{2,0,1:T(8,128)S(1)}) fusion(f32[16,16,64]{2,0,1:T(8,128)S(1)} %convolution_bitcast_fusion.5, f32[16,16,64]{2,0,1:T(8,128)} %collective-permute-done.1, pred[]{:T(512)S(6)} %eq.38), kind=kLoop, calls=%fused_computation.239 | loop fusion | flops 32768 | bytes 262145 | tf_op jit(solution)/shard_map/jit(_where)/select_n | solution.py:81
  35.3 1.3 %convolution_bitcast_fusion.4 = f32[16,16,64]{2,0,1:T(8,128)S(1)} fusion(f32[16,32,32]{1,2,0:T(8,128)S(1)} %copy-done.20, f32[16,32,32]{1,2,0:T(8,128)S(1)} %copy-done.19, f32[16,32,32]{1,2,0:T(8,128)S(1)} %copy-done.18, f32[16,32,32]{1,2,0:T(8,128)S(1)} %copy-done.22, f32[16,32,32]{1,2,0:T(8,128)S(1)} %copy-done.21, f32[16,32,32]{1,2,0:T(8,128)S(1)} %copy-done.17, ...), kind=kOutput, calls=%fused_computation.5 | convolution fusion | flops 26116096 | bytes 589824 | tf_op jit(solution)/shard_map/rsm,smn->rsn/dot_general | solution.py:68
  36.9 5.4 %collective-permute-start.8 = (f32[32,4,128]{2,0,1:T(8,128)S(1)}, f32[32,4,128]{2,0,1:T(8,128)S(1)}, u32[]{:S(2)}, u32[]{:S(2)}) collective-permute-start(f32[32,4,128]{2,0,1:T(8,128)S(1)} %get-tuple-element.94), channel_id=1, source_target_pairs={{0,31},{1,0},{2,1},{3,2},{4,3},{5,4},{6,5},{7,6},{8,7},{9,8},{10,9... | collective-permute-start | bytes 196616 | tf_op jit(solution)/shard_map/ppermute | solution.py:35
  42.3 1.3 %convolution_bitcast_fusion.3 = f32[16,16,64]{2,0,1:T(8,128)S(1)} fusion(f32[16,32,32]{1,2,0:T(8,128)S(1)} %copy-done.14, f32[16,32,32]{1,2,0:T(8,128)S(1)} %copy-done.13, f32[16,32,32]{1,2,0:T(8,128)S(1)} %copy-done.12, f32[16,32,32]{1,2,0:T(8,128)S(1)} %copy-done.16, f32[16,32,32]{1,2,0:T(8,128)S(1)} %copy-done.15, f32[16,32,32]{1,2,0:T(8,128)S(1)} %copy-done.11, ...), kind=kOutput, calls=%fused_computation.4 | convolution fusion | flops 26116096 | bytes 589824 | tf_op jit(solution)/shard_map/rsm,smn->rsn/dot_general | solution.py:68
  43.7 0.5 collective-permute-done.7
  44.2 4.4 %collective-permute-done.3 = f32[16,16,64]{2,0,1:T(8,128)S(1)} collective-permute-done((f32[16,16,64]{2,0,1:T(8,128)S(1)}, f32[16,16,64]{2,0,1:T(8,128)S(1)}, u32[]{:S(2)}, u32[]{:S(2)}) %collective-permute-start.3) | collective-permute-done | bytes 65568 | tf_op jit(solution)/shard_map/ppermute | solution.py:29
  48.7 1.3 %convolution_bitcast_fusion.2 = f32[16,16,64]{2,0,1:T(8,128)S(1)} fusion(f32[16,32,32]{1,2,0:T(8,128)S(1)} %copy-done.8, f32[16,32,32]{1,2,0:T(8,128)S(1)} %copy-done.7, f32[16,32,32]{1,2,0:T(8,128)S(1)} %copy-done.6, f32[16,32,32]{1,2,0:T(8,128)S(1)} %copy-done.10, f32[16,32,32]{1,2,0:T(8,128)S(1)} %copy-done.9, f32[16,32,32]{1,2,0:T(8,128)S(1)} %copy-done.5, ...), kind=kOutput, calls=%fused_computation.3 | convolution fusion | flops 26116096 | bytes 589824 | tf_op jit(solution)/shard_map/rsm,smn->rsn/dot_general | solution.py:68
  50.0 0.4 collective-permute-start.4
  50.4 6.6 %collective-permute-done.4 = f32[16,16,64]{2,0,1:T(8,128)S(1)} collective-permute-done((f32[16,16,64]{2,0,1:T(8,128)S(1)}, f32[16,16,64]{2,0,1:T(8,128)S(1)}, u32[]{:S(2)}, u32[]{:S(2)}) %collective-permute-start.4) | collective-permute-done | bytes 65568 | tf_op jit(solution)/shard_map/ppermute | solution.py:29
  57.1 1.3 %convolution_bitcast_fusion.1 = f32[16,16,64]{2,0,1:T(8,128)S(1)} fusion(f32[16,32,32]{1,2,0:T(8,128)S(1)} %get-tuple-element.89, f32[16,32,32]{1,2,0:T(8,128)S(1)} %get-tuple-element.88, f32[16,32,32]{1,2,0:T(8,128)S(1)} %get-tuple-element.87, f32[16,32,32]{1,2,0:T(8,128)S(1)} %copy-done.4, f32[16,32,32]{1,2,0:T(8,128)S(1)} %copy-done.3, ...), kind=kOutput, calls=%fused_computation.2 | convolution fusion | flops 26116096 | bytes 589824 | tf_op jit(solution)/shard_map/rsm,smn->rsn/dot_general | solution.py:68
  58.4 0.2 fusion.151
  58.6 0.3 fusion.149
  58.9 0.3 fusion.1
  59.2 0.2 fusion
  59.5 0.7 %copy_bitcast_fusion.1 = f32[32,2048]{1,0:T(8,128)} fusion(f32[32,16,128]{2,0,1:T(8,128)S(1)} %fusion.181, f32[16,16,128]{2,0,1:T(8,128)S(1)} %fusion, f32[16,16,128]{2,0,1:T(8,128)S(1)} %fusion.1), kind=kLoop, calls=%fused_computation.164 | loop fusion | flops 131072 | bytes 786432 | tf_op jit(solution)/shard_map/add | solution.py:155
  (118 shorter events, 2.7 us)
Async XLA Ops:
  0.0 30.7 %copy-start = (bf16[24,128,256]{2,1,0:T(8,128)(2,1)S(1)}, bf16[24,128,256]{2,1,0:T(8,128)(2,1)}, u32[]{:S(2)}) copy-start(bf16[24,128,256]{2,1,0:T(8,128)(2,1)} %param.14) | copy-start | bytes 4718596
  0.0 2.7 %copy-start.1 = (bf16[16,9,32,128]{3,2,1,0:T(8,128)(2,1)S(1)}, bf16[16,9,32,128]{3,2,1,0:T(8,128)(2,1)}, u32[]{:S(2)}) copy-start(bf16[16,9,32,128]{3,2,1,0:T(8,128)(2,1)} %param.12) | copy-start | bytes 3538948
  9.7 1.9 %copy-start.2 = (bf16[32,2048]{1,0:T(8,128)(2,1)S(1)}, bf16[32,2048]{1,0:T(8,128)(2,1)}, u32[]{:S(2)}) copy-start(bf16[32,2048]{1,0:T(8,128)(2,1)} %param.10) | copy-start | bytes 393220
  9.7 9.1 %copy-start.30 = (s32[24,2]{0,1:T(2,128)S(1)}, s32[24,2]{0,1:T(2,128)}, u32[]{:S(2)}) copy-start(s32[24,2]{0,1:T(2,128)} %param.15) | copy-start | bytes 580
  11.0 15.9 %collective-permute-start = (f32[16,16,64]{2,0,1:T(8,128)S(1)}, f32[16,16,64]{2,0,1:T(8,128)}, u32[]{:S(2)}, u32[]{:S(2)}) collective-permute-start(f32[16,16,64]{2,0,1:T(8,128)S(1)} %convolution_bitcast_fusion.6), channel_id=1, source_target_pairs={{0,1},{1,0},{2,3},{3,2},{4,5},{5,4},{6,7},{7,6},{8,9},{9,8},{10,11... | collective-permute-start | bytes 196616 | tf_op jit(solution)/shard_map/ppermute | solution.py:29
  12.1 17.1 %collective-permute-start.5 = (bf16[32,1024]{1,0:T(8,128)(2,1)}, bf16[32,1024]{1,0:T(8,128)(2,1)}, u32[]{:S(2)}, u32[]{:S(2)}) collective-permute-start(bf16[32,1024]{1,0:T(8,128)(2,1)} %get-tuple-element.116), channel_id=1, source_target_pairs={{0,1},{1,2},{2,3},{3,4},{4,5},{5,6},{6,7},{7,8},{8,9},{9,10},{10,1... | collective-permute-start | bytes 196616 | tf_op jit(solution)/shard_map/ppermute | solution.py:19
  12.2 17.1 %collective-permute-start.6 = (bf16[32,1024]{1,0:T(8,128)(2,1)S(1)}, bf16[32,1024]{1,0:T(8,128)(2,1)}, u32[]{:S(2)}, u32[]{:S(2)}) collective-permute-start(bf16[32,1024]{1,0:T(8,128)(2,1)S(1)} %get-tuple-element.117), channel_id=1, source_target_pairs={{1,0},{2,1},{3,2},{4,3},{5,4},{6,5},{7,6},{8,7},{9,8},{10,9},{11,1... | collective-permute-start | bytes 196616 | tf_op jit(solution)/shard_map/ppermute | solution.py:21
  25.7 1.1 %copy-start.29 = (bf16[64,2048]{1,0:T(8,128)(2,1)S(1)}, bf16[64,2048]{1,0:T(8,128)(2,1)}, u32[]{:S(2)}) copy-start(bf16[64,2048]{1,0:T(8,128)(2,1)} %param.13) | copy-start | bytes 786436
  25.7 2.1 %copy-start.23 = (f32[16,32,32]{1,2,0:T(8,128)S(1)}, f32[16,32,32]{1,2,0:T(8,128)}, u32[]{:S(2)}) copy-start(f32[16,32,32]{1,2,0:T(8,128)} %get-tuple-element.62) | copy-start | bytes 196612
  25.7 2.1 %copy-start.24 = (f32[16,32,32]{1,2,0:T(8,128)S(1)}, f32[16,32,32]{1,2,0:T(8,128)}, u32[]{:S(2)}) copy-start(f32[16,32,32]{1,2,0:T(8,128)} %get-tuple-element.63) | copy-start | bytes 196612
  25.7 2.1 %copy-start.25 = (f32[16,32,32]{1,2,0:T(8,128)S(1)}, f32[16,32,32]{1,2,0:T(8,128)}, u32[]{:S(2)}) copy-start(f32[16,32,32]{1,2,0:T(8,128)} %get-tuple-element.64) | copy-start | bytes 196612
  25.7 2.1 %copy-start.26 = (f32[16,32,32]{1,2,0:T(8,128)S(1)}, f32[16,32,32]{1,2,0:T(8,128)}, u32[]{:S(2)}) copy-start(f32[16,32,32]{1,2,0:T(8,128)} %get-tuple-element.65) | copy-start | bytes 196612
  25.8 2.1 %copy-start.27 = (f32[16,32,32]{1,2,0:T(8,128)S(1)}, f32[16,32,32]{1,2,0:T(8,128)}, u32[]{:S(2)}) copy-start(f32[16,32,32]{1,2,0:T(8,128)} %get-tuple-element.66) | copy-start | bytes 196612
  25.8 2.1 %copy-start.28 = (f32[16,32,32]{1,2,0:T(8,128)S(1)}, f32[16,32,32]{1,2,0:T(8,128)}, u32[]{:S(2)}) copy-start(f32[16,32,32]{1,2,0:T(8,128)} %get-tuple-element.67) | copy-start | bytes 196612
  29.1 5.1 %collective-permute-start.1 = (f32[16,16,64]{2,0,1:T(8,128)S(1)}, f32[16,16,64]{2,0,1:T(8,128)}, u32[]{:S(2)}, u32[]{:S(2)}) collective-permute-start(f32[16,16,64]{2,0,1:T(8,128)S(1)} %convolution_bitcast_fusion.5), channel_id=1, source_target_pairs={{0,2},{1,3},{2,0},{3,1},{4,6},{5,7},{6,4},{7,5},{8,10},{9,11},{10,... | collective-permute-start | bytes 196616 | tf_op jit(solution)/shard_map/ppermute | solution.py:29
  31.2 4.0 %copy-start.17 = (f32[16,32,32]{1,2,0:T(8,128)S(1)}, f32[16,32,32]{1,2,0:T(8,128)}, u32[]{:S(2)}) copy-start(f32[16,32,32]{1,2,0:T(8,128)} %get-tuple-element.68) | copy-start | bytes 196612
  31.2 4.0 %copy-start.18 = (f32[16,32,32]{1,2,0:T(8,128)S(1)}, f32[16,32,32]{1,2,0:T(8,128)}, u32[]{:S(2)}) copy-start(f32[16,32,32]{1,2,0:T(8,128)} %get-tuple-element.69) | copy-start | bytes 196612
  31.2 4.0 %copy-start.19 = (f32[16,32,32]{1,2,0:T(8,128)S(1)}, f32[16,32,32]{1,2,0:T(8,128)}, u32[]{:S(2)}) copy-start(f32[16,32,32]{1,2,0:T(8,128)} %get-tuple-element.70) | copy-start | bytes 196612
  31.2 4.0 %copy-start.20 = (f32[16,32,32]{1,2,0:T(8,128)S(1)}, f32[16,32,32]{1,2,0:T(8,128)}, u32[]{:S(2)}) copy-start(f32[16,32,32]{1,2,0:T(8,128)} %get-tuple-element.71) | copy-start | bytes 196612
  31.2 4.0 %copy-start.21 = (f32[16,32,32]{1,2,0:T(8,128)S(1)}, f32[16,32,32]{1,2,0:T(8,128)}, u32[]{:S(2)}) copy-start(f32[16,32,32]{1,2,0:T(8,128)} %get-tuple-element.72) | copy-start | bytes 196612
  31.3 4.0 %copy-start.22 = (f32[16,32,32]{1,2,0:T(8,128)S(1)}, f32[16,32,32]{1,2,0:T(8,128)}, u32[]{:S(2)}) copy-start(f32[16,32,32]{1,2,0:T(8,128)} %get-tuple-element.73) | copy-start | bytes 196612
  35.3 7.0 %copy-start.11 = (f32[16,32,32]{1,2,0:T(8,128)S(1)}, f32[16,32,32]{1,2,0:T(8,128)}, u32[]{:S(2)}) copy-start(f32[16,32,32]{1,2,0:T(8,128)} %get-tuple-element.74) | copy-start | bytes 196612
  35.3 7.0 %copy-start.12 = (f32[16,32,32]{1,2,0:T(8,128)S(1)}, f32[16,32,32]{1,2,0:T(8,128)}, u32[]{:S(2)}) copy-start(f32[16,32,32]{1,2,0:T(8,128)} %get-tuple-element.75) | copy-start | bytes 196612
  35.3 7.0 %copy-start.13 = (f32[16,32,32]{1,2,0:T(8,128)S(1)}, f32[16,32,32]{1,2,0:T(8,128)}, u32[]{:S(2)}) copy-start(f32[16,32,32]{1,2,0:T(8,128)} %get-tuple-element.76) | copy-start | bytes 196612
  35.3 7.0 %copy-start.14 = (f32[16,32,32]{1,2,0:T(8,128)S(1)}, f32[16,32,32]{1,2,0:T(8,128)}, u32[]{:S(2)}) copy-start(f32[16,32,32]{1,2,0:T(8,128)} %get-tuple-element.77) | copy-start | bytes 196612
  35.3 7.0 %copy-start.15 = (f32[16,32,32]{1,2,0:T(8,128)S(1)}, f32[16,32,32]{1,2,0:T(8,128)}, u32[]{:S(2)}) copy-start(f32[16,32,32]{1,2,0:T(8,128)} %get-tuple-element.78) | copy-start | bytes 196612
  35.3 7.0 %copy-start.16 = (f32[16,32,32]{1,2,0:T(8,128)S(1)}, f32[16,32,32]{1,2,0:T(8,128)}, u32[]{:S(2)}) copy-start(f32[16,32,32]{1,2,0:T(8,128)} %get-tuple-element.79) | copy-start | bytes 196612
  36.6 5.6 %collective-permute-start.2 = (f32[16,16,64]{2,0,1:T(8,128)S(1)}, f32[16,16,64]{2,0,1:T(8,128)S(1)}, u32[]{:S(2)}, u32[]{:S(2)}) collective-permute-start(f32[16,16,64]{2,0,1:T(8,128)S(1)} %convolution_bitcast_fusion.4), channel_id=1, source_target_pairs={{0,4},{4,0},{8,12},{12,8},{16,20},{20,16},{24,28},{28,24},{1,5},{5... | collective-permute-start | bytes 196616 | tf_op jit(solution)/shard_map/ppermute | solution.py:29
  36.7 7.4 %collective-permute-start.7 = (f32[32,4,128]{2,0,1:T(8,128)S(1)}, f32[32,4,128]{2,0,1:T(8,128)S(1)}, u32[]{:S(2)}, u32[]{:S(2)}) collective-permute-start(f32[32,4,128]{2,0,1:T(8,128)S(1)} %get-tuple-element.95), channel_id=1, source_target_pairs={{0,1},{1,2},{2,3},{3,4},{4,5},{5,6},{6,7},{7,8},{8,9},{9,10},{10,1... | collective-permute-start | bytes 196616 | tf_op jit(solution)/shard_map/ppermute | solution.py:35
  36.8 11.9 %copy-start.5 = (f32[16,32,32]{1,2,0:T(8,128)S(1)}, f32[16,32,32]{1,2,0:T(8,128)}, u32[]{:S(2)}) copy-start(f32[16,32,32]{1,2,0:T(8,128)} %get-tuple-element.80) | copy-start | bytes 196612
  36.8 11.9 %copy-start.6 = (f32[16,32,32]{1,2,0:T(8,128)S(1)}, f32[16,32,32]{1,2,0:T(8,128)}, u32[]{:S(2)}) copy-start(f32[16,32,32]{1,2,0:T(8,128)} %get-tuple-element.81) | copy-start | bytes 196612
  36.8 11.9 %copy-start.7 = (f32[16,32,32]{1,2,0:T(8,128)S(1)}, f32[16,32,32]{1,2,0:T(8,128)}, u32[]{:S(2)}) copy-start(f32[16,32,32]{1,2,0:T(8,128)} %get-tuple-element.82) | copy-start | bytes 196612
  36.8 11.9 %copy-start.8 = (f32[16,32,32]{1,2,0:T(8,128)S(1)}, f32[16,32,32]{1,2,0:T(8,128)}, u32[]{:S(2)}) copy-start(f32[16,32,32]{1,2,0:T(8,128)} %get-tuple-element.83) | copy-start | bytes 196612
  36.8 11.9 %copy-start.9 = (f32[16,32,32]{1,2,0:T(8,128)S(1)}, f32[16,32,32]{1,2,0:T(8,128)}, u32[]{:S(2)}) copy-start(f32[16,32,32]{1,2,0:T(8,128)} %get-tuple-element.84) | copy-start | bytes 196612
  36.9 11.9 %copy-start.10 = (f32[16,32,32]{1,2,0:T(8,128)S(1)}, f32[16,32,32]{1,2,0:T(8,128)}, u32[]{:S(2)}) copy-start(f32[16,32,32]{1,2,0:T(8,128)} %get-tuple-element.85) | copy-start | bytes 196612
  36.9 13.5 %collective-permute-start.8 = (f32[32,4,128]{2,0,1:T(8,128)S(1)}, f32[32,4,128]{2,0,1:T(8,128)S(1)}, u32[]{:S(2)}, u32[]{:S(2)}) collective-permute-start(f32[32,4,128]{2,0,1:T(8,128)S(1)} %get-tuple-element.94), channel_id=1, source_target_pairs={{0,31},{1,0},{2,1},{3,2},{4,3},{5,4},{6,5},{7,6},{8,7},{9,8},{10,9... | collective-permute-start | bytes 196616 | tf_op jit(solution)/shard_map/ppermute | solution.py:35
  43.6 5.0 %collective-permute-start.3 = (f32[16,16,64]{2,0,1:T(8,128)S(1)}, f32[16,16,64]{2,0,1:T(8,128)S(1)}, u32[]{:S(2)}, u32[]{:S(2)}) collective-permute-start(f32[16,16,64]{2,0,1:T(8,128)S(1)} %convolution_bitcast_fusion.3), channel_id=1, source_target_pairs={{0,8},{4,12},{8,0},{12,4},{16,24},{20,28},{24,16},{28,20},{1,9},{5... | collective-permute-start | bytes 196616 | tf_op jit(solution)/shard_map/ppermute | solution.py:29
  44.2 12.9 %copy-start.3 = (f32[16,32,32]{1,2,0:T(8,128)S(1)}, f32[16,32,32]{1,2,0:T(8,128)}, u32[]{:S(2)}) copy-start(f32[16,32,32]{1,2,0:T(8,128)} %get-tuple-element.90) | copy-start | bytes 196612
  44.2 12.9 %copy-start.4 = (f32[16,32,32]{1,2,0:T(8,128)S(1)}, f32[16,32,32]{1,2,0:T(8,128)}, u32[]{:S(2)}) copy-start(f32[16,32,32]{1,2,0:T(8,128)} %get-tuple-element.91) | copy-start | bytes 196612
  50.0 7.0 %collective-permute-start.4 = (f32[16,16,64]{2,0,1:T(8,128)S(1)}, f32[16,16,64]{2,0,1:T(8,128)S(1)}, u32[]{:S(2)}, u32[]{:S(2)}) collective-permute-start(f32[16,16,64]{2,0,1:T(8,128)S(1)} %convolution_bitcast_fusion.2), channel_id=1, source_target_pairs={{0,16},{4,20},{8,24},{12,28},{16,0},{20,4},{24,8},{28,12},{1,17},{... | collective-permute-start | bytes 196616 | tf_op jit(solution)/shard_map/ppermute | solution.py:29
where the time goes:
time: 60.4 us; the launch traced here: 60.2 us
  matrix products  14.1 us (23%)
  waiting for transfers between devices  13.9 us (23%)
  starting transfers between devices  13.1 us (22%)
  other arithmetic  11.7 us (19%)
  local copies, waits for them, and re-layouts  6.45 us (11%)
  between operations  0.98 us (2%)
    ppermute x5, waiting for transfers between devices, swapped(): lax.ppermute(shard, axis, [(i, i ^ 1 << distance) for i in range(lax.axis...  13.4 us
    dot_general x9, matrix products, apply_level(): jnp.einsum('rsm,smn->rsn', paired, block_form(weights), precision=highest)  11.6 us
    ppermute x1, starting transfers between devices, with_halo(): lax.ppermute(head, axis, [((i + 1) % count, i) for i in range(count)])  6.56 us
    neg x9, other arithmetic, block_form(): upper_rows = jnp.concatenate([real_part, -imag_part], axis=2)  6.54 us
    ppermute x2, starting transfers between devices, from_behind(): return lax.ppermute(value, axis, pairs)  5.41 us
    unnamed x74, local copies, waits for them, and re-layouts  4.77 us
    select_n x5, other arithmetic, swap_level(): low_side = jnp.where(upper_bit == 0, owned, partner_box)  1.92 us
  transfers between devices with their start and end apart: 9, of which 4 were waited for; matrix products, arithmetic and copies ran while one was open for 27% of the time, Pallas kernels for 0%

commit v1 on v0

v1 whole, which is shorter than its diff:
```python
import functools

import jax
import jax.numpy as jnp
from jax import lax
from jax.experimental import pallas as pl
from jax.experimental.pallas import tpu as pltpu
from jax.sharding import PartitionSpec as P

LEAF = 128
AXES = ("leaf", "sub")
F32 = jnp.float32
BF16 = jnp.bfloat16


def lanes_like(x):
    return lax.broadcasted_iota(jnp.int32, x.shape, x.ndim - 1)


def dot(a, b):
    return lax.dot_general(a, b, (((1,), (0,)), ((), ())), preferred_element_type=F32)


def dot_t(a, b):
    return lax.dot_general(a, b, (((1,), (1,)), ((), ())), preferred_element_type=F32)


def half_roll(x):
    return pltpu.roll(x, x.shape[1] // 2, 1)


def pick_low(x, y):
    return jnp.where(lanes_like(x) < x.shape[1] // 2, x, y)


def split_rows(x):
    top = x.astype(BF16)
    rest = (x - top.astype(F32)).astype(BF16)
    return [top, rest]


def level_matrix(first, second):
    a = first.astype(F32)
    b = second.astype(F32)
    width = a.shape[1]
    quarter = width // 4
    low = pick_low(a, half_roll(b))
    high = pick_low(half_roll(a), b)
    is_real = lanes_like(a) % (2 * quarter) < quarter
    rows = []
    for part in (low, high):
        rows.append(jnp.where(is_real, part, -part))
        rows.append(jnp.where(is_real, pltpu.roll(part, width - quarter, 1), pltpu.roll(part, quarter, 1)))
    return jnp.concatenate(rows, axis=0).astype(BF16)


def project_pair(signal_ref, basis_ref, first, second):
    rhs = signal_ref.shape[0] // 2
    rank = basis_ref.shape[0] // 2
    left = []
    right = []
    for box in (first, second):
        cols = pl.ds(box * LEAF, LEAF)
        x = signal_ref[:, cols]
        u = basis_ref[:, cols]
        left.append(jnp.concatenate([x[:rhs], x[rhs:]], axis=1))
        right.append(jnp.concatenate([u[:rank], u[rank:]], axis=1))
        right.append(jnp.concatenate([-u[rank:], u[:rank]], axis=1))
    out = dot_t(jnp.concatenate(left, axis=0), jnp.concatenate(right, axis=0))
    return pick_low(out[:rhs], out[rhs:])


def local_kernel(signal_ref, basis_ref, transfer_ref, out_ref):
    boxes = transfer_ref.shape[0]
    rhs = signal_ref.shape[0] // 2
    levels = boxes.bit_length() - 1
    state = {}
    for box in range(0, boxes, 2):
        state[box] = project_pair(signal_ref, basis_ref, box, box + 1)
    for level in range(levels):
        bit = 1 << level
        done = {}
        for box, pair in state.items():
            matrix = level_matrix(transfer_ref[box, level], transfer_ref[box + bit, level])
            both = dot(jnp.concatenate(split_rows(pair), axis=0), matrix)
            done[box] = both[:rhs] + both[rhs:]
        state = done
        if level + 1 < levels:
            state = {}
            for box in done:
                if box & (2 * bit):
                    continue
                other = box + 2 * bit
                state[box] = pick_low(done[box], half_roll(done[other]))
                state[box + bit] = pick_low(half_roll(done[box]), done[other])
    for box, pair in state.items():
        out_ref[box] = pair


def matrices_kernel(transfer_ref, out_ref, *, first_level):
    half = transfer_ref.shape[0] // 2
    for level in range(out_ref.shape[0]):
        for box in range(half):
            out_ref[level, box] = level_matrix(
                transfer_ref[box, first_level + level], transfer_ref[box + half, first_level + level]
            )


def crossed(own_ref, other_ref, matrices_ref, level, upper, box):
    own = own_ref[box]
    other = other_ref[box]
    rhs = own.shape[0]
    low = jnp.where(upper, other, own)
    high = jnp.where(upper, own, other)
    first = pick_low(low, half_roll(high))
    second = pick_low(half_roll(low), high)
    rows = jnp.concatenate(split_rows(first) + split_rows(second), axis=0)
    out = dot(rows, matrices_ref[level, box])
    return pick_low(out[:rhs] + out[rhs : 2 * rhs], out[2 * rhs : 3 * rhs] + out[3 * rhs :])


def device_index():
    return lax.axis_index("leaf") * lax.axis_size("sub") + lax.axis_index("sub")


def cross_kernel(index_ref, own_ref, other_ref, matrices_ref, out_ref, *, level):
    upper = (index_ref[0] >> level & 1) == 1
    for box in range(own_ref.shape[0]):
        out_ref[box] = crossed(own_ref, other_ref, matrices_ref, level, upper, box)


def final_kernel(
    index_ref, own_ref, other_ref, matrices_ref, basis_ref, center_ref, pair_ref, ring_ref, out_ref, *, level
):
    upper = (index_ref[0] >> level & 1) == 1
    odd = (index_ref[0] & 1) == 1
    half, rhs, width = own_ref.shape
    rank = width // 4
    edge = pair_ref.shape[1] // LEAF
    for box in range(half):
        pair = crossed(own_ref, other_ref, matrices_ref, level, upper, box)
        is_low = lanes_like(pair) < width // 2
        rows = []
        for part in (jnp.where(is_low, pair, 0.0), jnp.where(is_low, 0.0, pair)):
            rows += split_rows(part)
        right = []
        for place in (box, box + half):
            v = basis_ref[:, pl.ds(place * LEAF, LEAF)]
            right.append(jnp.concatenate([v[:rank], v[rank:]], axis=1))
            right.append(jnp.concatenate([-v[rank:], v[:rank]], axis=1))
        out = dot(jnp.concatenate(rows, axis=0), jnp.concatenate(right, axis=0))
        for k, place in enumerate((box, box + half)):
            far = out[2 * k * rhs : (2 * k + 1) * rhs] + out[(2 * k + 1) * rhs : (2 * k + 2) * rhs]
            total = center_ref[place] + jnp.concatenate([far[:, :LEAF], far[:, LEAF:]], axis=0)
            if place < edge:
                cols = pl.ds(place * LEAF, LEAF)
                total = total + jnp.where(odd, pair_ref[:, cols], ring_ref[:, cols])
            if place >= 2 * half - edge:
                cols = pl.ds((place - 2 * half + edge) * LEAF, LEAF)
                total = total + jnp.where(odd, ring_ref[:, cols], pair_ref[:, cols])
            out_ref[:, pl.ds(place * LEAF, LEAF)] = total


def near_kernel(
    index_ref, list_ref, signal_ref, pair_ref, ring_ref, blocks_ref, center_ref, to_pair_ref, to_ring_ref, window, sums
):
    odd = (index_ref[0] & 1) == 1
    channels = signal_ref.shape[0]
    rhs = channels // 2
    boxes = signal_ref.shape[1] // LEAF
    halo = pair_ref.shape[1] // LEAF
    edge = to_pair_ref.shape[1] // LEAF
    for box in range(halo):
        cols = pl.ds(box * LEAF, LEAF)
        window[box] = jnp.where(odd, pair_ref[:, cols], ring_ref[:, cols])
        window[halo + boxes + box] = jnp.where(odd, ring_ref[:, cols], pair_ref[:, cols])
    for box in range(boxes):
        window[halo + box] = signal_ref[:, pl.ds(box * LEAF, LEAF)]
    sums[...] = jnp.zeros_like(sums)
    for slot in range(blocks_ref.shape[0]):
        row = jnp.maximum(list_ref[slot, 0], 0)
        col = list_ref[slot, 1]
        col = jnp.where(col < 0, sums.shape[0] - 1, col)
        out = dot(window[row], blocks_ref[slot])
        real = out[:rhs, :LEAF] + out[rhs:, LEAF:]
        imag = out[rhs:, :LEAF] - out[:rhs, LEAF:]
        sums[col] = sums[col] + jnp.concatenate([real, imag], axis=0)
    for box in range(boxes):
        center_ref[box] = sums[edge + box]
    for box in range(edge):
        cols = pl.ds(box * LEAF, LEAF)
        before = sums[box]
        after = sums[edge + boxes + box]
        to_pair_ref[:, cols] = jnp.where(odd, before, after)
        to_ring_ref[:, cols] = jnp.where(odd, after, before)


VMEM = pl.BlockSpec(memory_space=pltpu.VMEM)
SMEM = pl.BlockSpec(memory_space=pltpu.SMEM)


def shards(signal, row_basis, transfer, column_basis, near_blocks, near_list):
    channels = signal.shape[0]
    rhs = channels // 2
    boxes, levels, rank, width = transfer.shape
    half = boxes // 2
    reach = boxes // 4
    local_levels = boxes.bit_length() - 1
    devices = lax.axis_size("leaf") * lax.axis_size("sub")
    index = device_index()
    index_word = index.astype(jnp.int32).reshape(1)
    odd = index & 1

    pairs = [(i, i ^ 1) for i in range(devices)]
    ring = [(i, (i + 1) % devices if i & 1 else (i - 1) % devices) for i in range(devices)]

    halo = 2 * reach * LEAF
    far_end = signal.shape[1] - halo
    to_pair = lax.dynamic_slice_in_dim(signal, jnp.where(odd == 1, 0, far_end), halo, 1)
    to_ring = lax.dynamic_slice_in_dim(signal, jnp.where(odd == 1, far_end, 0), halo, 1)
    with jax.named_scope("halo_pair"):
        from_pair = lax.ppermute(to_pair, AXES, pairs)
    with jax.named_scope("halo_ring"):
        from_ring = lax.ppermute(to_ring, AXES, ring)

    state_type = jax.ShapeDtypeStruct((half, rhs, width), F32)
    coeffs = pl.pallas_call(
        local_kernel, out_shape=state_type, in_specs=[VMEM] * 3, out_specs=VMEM, name="local"
    )(signal, row_basis, transfer)
    cross_levels = levels - local_levels
    matrices = pl.pallas_call(
        functools.partial(matrices_kernel, first_level=local_levels),
        out_shape=jax.ShapeDtypeStruct((cross_levels, half, width, width), BF16),
        in_specs=[VMEM],
        out_specs=VMEM,
        name="matrices",
    )(transfer)
    center, rim_pair, rim_ring = pl.pallas_call(
        near_kernel,
        out_shape=(
            jax.ShapeDtypeStruct((boxes, channels, LEAF), F32),
            jax.ShapeDtypeStruct((channels, reach * LEAF), F32),
            jax.ShapeDtypeStruct((channels, reach * LEAF), F32),
        ),
        in_specs=[SMEM, SMEM, VMEM, VMEM, VMEM, VMEM],
        out_specs=(VMEM, VMEM, VMEM),
        scratch_shapes=[
            pltpu.VMEM((boxes + 4 * reach, channels, LEAF), BF16),
            pltpu.VMEM((boxes + 2 * reach + 1, channels, LEAF), F32),
        ],
        name="near",
    )(index_word, near_list, signal, from_pair, from_ring, near_blocks)
    with jax.named_scope("rim_pair"):
        rim_from_pair = lax.ppermute(rim_pair, AXES, pairs)
    with jax.named_scope("rim_ring"):
        rim_from_ring = lax.ppermute(rim_ring, AXES, ring)

    for level in range(cross_levels):
        with jax.named_scope(f"swap_{level}"):
            other = lax.ppermute(coeffs, AXES, [(i, i ^ 1 << level) for i in range(devices)])
        if level + 1 < cross_levels:
            coeffs = pl.pallas_call(
                functools.partial(cross_kernel, level=level),
                out_shape=state_type,
                in_specs=[SMEM, VMEM, VMEM, VMEM],
                out_specs=VMEM,
                name=f"cross_{level}",
            )(index_word, coeffs, other, matrices)
    return pl.pallas_call(
        functools.partial(final_kernel, level=cross_levels - 1),
        out_shape=jax.ShapeDtypeStruct((channels, boxes * LEAF), F32),
        in_specs=[SMEM] + [VMEM] * 7,
        out_specs=VMEM,
        name="final",
    )(index_word, coeffs, other, matrices, column_basis, center, rim_from_pair, rim_from_ring)


def solution(mesh):
    return jax.shard_map(
        shards,
        mesh=mesh,
        in_specs=(
            P(None, AXES),
            P(None, AXES),
            P(AXES, None, None, None),
            P(None, AXES),
            P(AXES, None, None),
            P(AXES, None),
        ),
        out_specs=P(None, AXES),
        check_vma=False,
    )
```

time: 60.4 us -> 50.5 us (0.84)
  Pallas kernels: 0 us -> 23 us
  matrix products: 14.1 us -> 0 us
  other arithmetic: 11.7 us -> 0 us
  waiting for transfers between devices: 13.9 us -> 8.34 us
  local copies, waits for them, and re-layouts: 6.45 us -> 5.06 us
  between operations: 0.98 us -> 0.04 us
    pallas_call x0 -> x8, Pallas kernels: none -> 23 us  [the longest x4 9.15 us: shards(): pl.pallas_call(functools.partial(cross_kernel, level=level), out_shape=st...]
    dot_general x16 -> x0, matrix products: 14.1 us -> none  [the longest x9 11.6 us: apply_level(): jnp.einsum('rsm,smn->rsn', paired, block_form(weights), precision=highest)]
    neg x9 -> x0, other arithmetic: 6.54 us -> none  [block_form(): upper_rows = jnp.concatenate([real_part, -imag_part], axis=2)]
    ppermute x9, waiting for transfers between devices: 13.9 us -> 8.34 us  [the longest x5 8.23 us: shards(): lax.ppermute(coeffs, AXES, [(i, i ^ 1 << level) for i in range(devices)])]
    select_n x5 -> x0, other arithmetic: 1.92 us -> none  [swap_level(): low_side = jnp.where(upper_bit == 0, owned, partner_box)]
    convert_element_type x9 -> x0, other arithmetic: 0.93 us -> none  [block_form(): matrices = weights.astype(jnp.float32)]
    reshape x1 -> x0, other arithmetic: 0.92 us -> none  [shards(): leaf_tiles = window.reshape(channels, -1, LEAF)]
    slice x4 -> x0, local copies, waits for them, and re-layouts: 0.9 us -> none  [the longest x1 0.63 us: with_halo(): lax.slice_in_dim(cells, cells.shape[dim] - width, cells.shape[dim], axis=...]
  transfers between devices with their start and end apart: 9 -> 9, of which waited for: 4 -> 3; matrix products, arithmetic and copies ran while one was open for 27% -> 1% of each run, Pallas kernels for 0% -> 25%
where the time goes in v1:
time: 50.5 us; the launch traced here: 50.2 us
  Pallas kernels  23 us (46%)
  starting transfers between devices  13.7 us (27%)
  waiting for transfers between devices  8.34 us (17%)
  local copies, waits for them, and re-layouts  5.06 us (10%)
    pallas_call x4, Pallas kernels, shards(): pl.pallas_call(functools.partial(cross_kernel, level=level), out_shape=st...  9.15 us
    ppermute x5, waiting for transfers between devices, shards(): lax.ppermute(coeffs, AXES, [(i, i ^ 1 << level) for i in range(devices)])  8.23 us
    ppermute x5, starting transfers between devices, shards(): lax.ppermute(coeffs, AXES, [(i, i ^ 1 << level) for i in range(devices)])  5.75 us
    pallas_call x1, Pallas kernels, shards(): pl.pallas_call(functools.partial(matrices_kernel, first_level=local_level...  5.07 us
    unnamed x23, local copies, waits for them, and re-layouts  5.05 us
    ppermute x1, starting transfers between devices, shards(): rim_from_ring = lax.ppermute(rim_ring, AXES, ring)  4.47 us
    ppermute x1, starting transfers between devices, shards(): from_ring = lax.ppermute(to_ring, AXES, ring)  3.51 us
    pallas_call x1, Pallas kernels, shards(): pl.pallas_call(local_kernel, out_shape=state_type, in_specs=[VMEM] * 3, o...  3.36 us
  transfers between devices with their start and end apart: 9, of which 3 were waited for; matrix products, arithmetic and copies ran while one was open for 1% of the time, Pallas kernels for 25%

profile of v1, /device:TPU:0, one launch (start us, length us, event | category | flops | bytes accessed | tf_op | source)
XLA Modules:
  0.0 50.2 jit_solution(7899736044999298827)
XLA Ops:
  0.0 3.4 %local.1.own_ref = f32[8,16,128]{2,1,0:T(8,128)} custom-call(bf16[32,2048]{1,0:T(8,128)(2,1)} %signal_ref.3, bf16[64,2048]{1,0:T(8,128)(2,1)} %basis_ref.2, bf16[16,9,32,128]{3,2,1,0:T(8,128)(2,1)} %transfer_ref.3), custom_call_target="tpu_custom_call" | custom-call | tf_op jit(solution)/shard_map/local/pallas_call | solution.py:227
  3.4 0.5 collective-permute-start
  3.9 5.1 %matrices.1.matrices_ref = bf16[5,8,128,128]{3,2,1,0:T(8,128)(2,1)} custom-call(bf16[16,9,32,128]{3,2,1,0:T(8,128)(2,1)} %transfer_ref.3), custom_call_target="tpu_custom_call" | custom-call | tf_op jit(solution)/shard_map/matrices/pallas_call | solution.py:231
  8.9 0.0 collective-permute-done.other_ref
  8.9 0.0 copy-start.5
  8.9 0.6 %copy-done.5 = f32[8,16,128]{2,1,0:T(8,128)} copy-done((f32[8,16,128]{2,1,0:T(8,128)}, f32[8,16,128]{2,1,0:T(8,128)S(1)}, u32[]{:S(2)}) %copy-start.5) | copy-done | bytes 65560
  9.6 0.0 copy-start
  9.6 2.3 %cross_0.1.own_ref = f32[8,16,128]{2,1,0:T(8,128)} custom-call(s32[1]{0:T(128)} %bitcast.index_ref, f32[8,16,128]{2,1,0:T(8,128)} %local.1.own_ref, f32[8,16,128]{2,1,0:T(8,128)} %copy-done.5, bf16[5,8,128,128]{3,2,1,0:T(8,128)(2,1)} %matrices.1.matrices_ref), custom_call_target="tpu_custom_call" | custom-call | tf_op jit(solution)/shard_map/cross_0/pallas_call | solution.py:262
  11.9 2.5 %collective-permute-start.1 = (f32[8,16,128]{2,1,0:T(8,128)}, f32[8,16,128]{2,1,0:T(8,128)S(1)}, u32[]{:S(2)}, u32[]{:S(2)}) collective-permute-start(f32[8,16,128]{2,1,0:T(8,128)} %cross_0.1.own_ref), channel_id=1, source_target_pairs={{0,2},{1,3},{2,0},{3,1},{4,6},{5,7},{6,4},{7,5},{8,10},{9,11},{10,... | collective-permute-start | bytes 196616 | tf_op jit(solution)/shard_map/swap_1/ppermute | solution.py:260
  14.4 0.0 copy-start.10
  14.4 3.0 %collective-permute-done.1.other_ref = f32[8,16,128]{2,1,0:T(8,128)S(1)} collective-permute-done((f32[8,16,128]{2,1,0:T(8,128)}, f32[8,16,128]{2,1,0:T(8,128)S(1)}, u32[]{:S(2)}, u32[]{:S(2)}) %collective-permute-start.1) | collective-permute-done | bytes 65568 | tf_op jit(solution)/shard_map/swap_1/ppermute | solution.py:260
  17.3 0.0 copy-start.9
  17.3 0.6 %copy-done.9 = f32[8,16,128]{2,1,0:T(8,128)} copy-done((f32[8,16,128]{2,1,0:T(8,128)}, f32[8,16,128]{2,1,0:T(8,128)S(1)}, u32[]{:S(2)}) %copy-start.9) | copy-done | bytes 65560
  17.9 2.3 %cross_1.1.own_ref = f32[8,16,128]{2,1,0:T(8,128)} custom-call(s32[1]{0:T(128)} %bitcast.index_ref, f32[8,16,128]{2,1,0:T(8,128)} %cross_0.1.own_ref, f32[8,16,128]{2,1,0:T(8,128)} %copy-done.9, bf16[5,8,128,128]{3,2,1,0:T(8,128)(2,1)} %matrices.1.matrices_ref), custom_call_target="tpu_custom_call" | custom-call | tf_op jit(solution)/shard_map/cross_1/pallas_call | solution.py:262
  20.2 1.8 %collective-permute-start.2 = (f32[8,16,128]{2,1,0:T(8,128)}, f32[8,16,128]{2,1,0:T(8,128)S(1)}, u32[]{:S(2)}, u32[]{:S(2)}) collective-permute-start(f32[8,16,128]{2,1,0:T(8,128)} %cross_1.1.own_ref), channel_id=1, source_target_pairs={{0,4},{1,5},{2,6},{3,7},{4,0},{5,1},{6,2},{7,3},{8,12},{9,13},{10,... | collective-permute-start | bytes 196616 | tf_op jit(solution)/shard_map/swap_2/ppermute | solution.py:260
  22.0 0.0 copy-done
  22.0 3.5 %collective-permute-start.6 = (bf16[32,1024]{1,0:T(8,128)(2,1)S(1)}, bf16[32,1024]{1,0:T(8,128)(2,1)S(1)}, u32[]{:S(2)}, u32[]{:S(2)}) collective-permute-start(bf16[32,1024]{1,0:T(8,128)(2,1)S(1)} %get-tuple-element.11), channel_id=1, source_target_pairs={{0,31},{1,2},{2,1},{3,4},{4,3},{5,6},{6,5},{7,8},{8,7},{9,10},{10,... | collective-permute-start | bytes 196616 | tf_op jit(solution)/shard_map/halo_ring/ppermute | solution.py:224
  25.5 0.0 collective-permute-start.5
  25.5 0.0 collective-permute-done.2.other_ref
  25.5 0.0 copy-start.7
  25.5 0.6 %copy-done.7 = f32[8,16,128]{2,1,0:T(8,128)} copy-done((f32[8,16,128]{2,1,0:T(8,128)}, f32[8,16,128]{2,1,0:T(8,128)S(1)}, u32[]{:S(2)}) %copy-start.7) | copy-done | bytes 65560
  26.2 2.3 %cross_2.1.own_ref = f32[8,16,128]{2,1,0:T(8,128)} custom-call(s32[1]{0:T(128)} %bitcast.index_ref, f32[8,16,128]{2,1,0:T(8,128)} %cross_1.1.own_ref, f32[8,16,128]{2,1,0:T(8,128)} %copy-done.7, bf16[5,8,128,128]{3,2,1,0:T(8,128)(2,1)} %matrices.1.matrices_ref), custom_call_target="tpu_custom_call" | custom-call | tf_op jit(solution)/shard_map/cross_2/pallas_call | solution.py:262
  28.4 1.0 %collective-permute-start.3 = (f32[8,16,128]{2,1,0:T(8,128)}, f32[8,16,128]{2,1,0:T(8,128)S(1)}, u32[]{:S(2)}, u32[]{:S(2)}) collective-permute-start(f32[8,16,128]{2,1,0:T(8,128)} %cross_2.1.own_ref), channel_id=1, source_target_pairs={{0,8},{1,9},{2,10},{3,11},{4,12},{5,13},{6,14},{7,15},{8,0},{9,1},... | collective-permute-start | bytes 196616 | tf_op jit(solution)/shard_map/swap_3/ppermute | solution.py:260
  29.4 0.0 copy-done.10
  29.4 0.7 %copy.7.list_ref = s32[24,2]{1,0:T(8,128)} copy(s32[24,2]{0,1:T(2,128)S(1)} %copy-done.10) | data formatting | bytes 384 | tf_op args[5]
  30.1 0.0 collective-permute-done.6.ring_ref
  30.1 0.0 copy-start.3
  30.1 0.0 collective-permute-done.5.pair_ref
  30.1 0.6 %copy-done.3 = bf16[32,1024]{1,0:T(8,128)(2,1)} copy-done((bf16[32,1024]{1,0:T(8,128)(2,1)}, bf16[32,1024]{1,0:T(8,128)(2,1)S(1)}, u32[]{:S(2)}) %copy-start.3) | copy-done | bytes 65560
  30.7 0.0 copy-start.6
  30.7 0.6 %copy-done.6 = bf16[32,1024]{1,0:T(8,128)(2,1)} copy-done((bf16[32,1024]{1,0:T(8,128)(2,1)}, bf16[32,1024]{1,0:T(8,128)(2,1)S(1)}, u32[]{:S(2)}) %copy-start.6) | copy-done | bytes 65560
  31.4 2.7 %near.1 = (f32[16,32,128]{2,1,0:T(8,128)}, f32[32,512]{1,0:T(8,128)}, f32[32,512]{1,0:T(8,128)}) custom-call(s32[1]{0:T(128)} %bitcast.index_ref, s32[24,2]{1,0:T(8,128)} %copy.7.list_ref, bf16[32,2048]{1,0:T(8,128)(2,1)} %signal_ref.3, bf16[32,1024]{1,0:T(8,128)(2,1)} %copy-done.6, bf16[32,1024]{1,0:T(8,128)(2,1)} %copy-done.3, bf16[24,128,256]{2,1,0:T(8,128)(2,1)} %blocks_ref.1), custom_call_target="tpu_custom_call" | custom-call | tf_op jit(solution)/shard_map/near/pallas_call | solution.py:238
  34.1 0.0 collective-permute-start.7
  34.1 4.5 %collective-permute-start.8 = (f32[32,512]{1,0:T(8,128)}, f32[32,512]{1,0:T(8,128)S(1)}, u32[]{:S(2)}, u32[]{:S(2)}) collective-permute-start(f32[32,512]{1,0:T(8,128)} %get-tuple-element.10), channel_id=1, source_target_pairs={{0,31},{1,2},{2,1},{3,4},{4,3},{5,6},{6,5},{7,8},{8,7},{9,10},{10,... | collective-permute-start | bytes 196616 | tf_op jit(solution)/shard_map/rim_ring/ppermute | solution.py:256
  38.6 0.0 collective-permute-done.3.other_ref
  38.6 0.0 copy-start.2
  38.6 0.6 %copy-done.2 = f32[8,16,128]{2,1,0:T(8,128)} copy-done((f32[8,16,128]{2,1,0:T(8,128)}, f32[8,16,128]{2,1,0:T(8,128)S(1)}, u32[]{:S(2)}) %copy-start.2) | copy-done | bytes 65560
  39.2 2.3 %cross_3.1.own_ref = f32[8,16,128]{2,1,0:T(8,128)} custom-call(s32[1]{0:T(128)} %bitcast.index_ref, f32[8,16,128]{2,1,0:T(8,128)} %cross_2.1.own_ref, f32[8,16,128]{2,1,0:T(8,128)} %copy-done.2, bf16[5,8,128,128]{3,2,1,0:T(8,128)(2,1)} %matrices.1.matrices_ref), custom_call_target="tpu_custom_call" | custom-call | tf_op jit(solution)/shard_map/cross_3/pallas_call | solution.py:262
  41.5 0.0 collective-permute-start.4
  41.5 0.0 collective-permute-done.7.pair_ref
  41.5 0.1 collective-permute-done.8.ring_ref
  41.6 0.0 copy-start.4
  41.6 5.3 %collective-permute-done.4.other_ref = f32[8,16,128]{2,1,0:T(8,128)S(1)} collective-permute-done((f32[8,16,128]{2,1,0:T(8,128)}, f32[8,16,128]{2,1,0:T(8,128)S(1)}, u32[]{:S(2)}, u32[]{:S(2)}) %collective-permute-start.4) | collective-permute-done | bytes 65568 | tf_op jit(solution)/shard_map/swap_4/ppermute | solution.py:260
  46.9 0.0 copy-start.8
  46.9 0.0 copy-done.1
  46.9 0.0 copy-done.4
  46.9 0.6 %copy-done.8 = f32[8,16,128]{2,1,0:T(8,128)} copy-done((f32[8,16,128]{2,1,0:T(8,128)}, f32[8,16,128]{2,1,0:T(8,128)S(1)}, u32[]{:S(2)}) %copy-start.8) | copy-done | bytes 65560
  47.5 2.7 %final.1 = f32[32,2048]{1,0:T(8,128)} custom-call(s32[1]{0:T(128)} %bitcast.index_ref, f32[8,16,128]{2,1,0:T(8,128)} %cross_3.1.own_ref, f32[8,16,128]{2,1,0:T(8,128)} %copy-done.8, bf16[5,8,128,128]{3,2,1,0:T(8,128)(2,1)} %matrices.1.matrices_ref, bf16[64,2048]{1,0:T(8,128)(2,1)} %basis_ref.3, f32[16,32,128]{2,1,0:T(8,128)} %get-tuple-element.8.center_ref, ...), custom_call_target="tpu_custom_call" | custom-call | tf_op jit(solution)/shard_map/final/pallas_call | solution.py:269
  (2 shorter events, 0.0 us)
Async XLA Ops:
  3.4 5.6 %collective-permute-start = (f32[8,16,128]{2,1,0:T(8,128)}, f32[8,16,128]{2,1,0:T(8,128)S(1)}, u32[]{:S(2)}, u32[]{:S(2)}) collective-permute-start(f32[8,16,128]{2,1,0:T(8,128)} %local.1.own_ref), channel_id=1, source_target_pairs={{0,1},{1,0},{2,3},{3,2},{4,5},{5,4},{6,7},{7,6},{8,9},{9,8},{10,11... | collective-permute-start | bytes 196616 | tf_op jit(solution)/shard_map/swap_0/ppermute | solution.py:260
  8.9 0.6 %copy-start.5 = (f32[8,16,128]{2,1,0:T(8,128)}, f32[8,16,128]{2,1,0:T(8,128)S(1)}, u32[]{:S(2)}) copy-start(f32[8,16,128]{2,1,0:T(8,128)S(1)} %collective-permute-done.other_ref) | copy-start | bytes 196612
  9.6 12.5 %copy-start = (bf16[32,2048]{1,0:T(8,128)(2,1)S(1)}, bf16[32,2048]{1,0:T(8,128)(2,1)}, u32[]{:S(2)}) copy-start(bf16[32,2048]{1,0:T(8,128)(2,1)} %signal_ref.3) | copy-start | bytes 393220
  11.9 5.5 %collective-permute-start.1 = (f32[8,16,128]{2,1,0:T(8,128)}, f32[8,16,128]{2,1,0:T(8,128)S(1)}, u32[]{:S(2)}, u32[]{:S(2)}) collective-permute-start(f32[8,16,128]{2,1,0:T(8,128)} %cross_0.1.own_ref), channel_id=1, source_target_pairs={{0,2},{1,3},{2,0},{3,1},{4,6},{5,7},{6,4},{7,5},{8,10},{9,11},{10,... | collective-permute-start | bytes 196616 | tf_op jit(solution)/shard_map/swap_1/ppermute | solution.py:260
  14.4 15.1 %copy-start.10 = (s32[24,2]{0,1:T(2,128)S(1)}, s32[24,2]{0,1:T(2,128)}, u32[]{:S(2)}) copy-start(s32[24,2]{0,1:T(2,128)} %param.11) | copy-start | bytes 580
  17.3 0.6 %copy-start.9 = (f32[8,16,128]{2,1,0:T(8,128)}, f32[8,16,128]{2,1,0:T(8,128)S(1)}, u32[]{:S(2)}) copy-start(f32[8,16,128]{2,1,0:T(8,128)S(1)} %collective-permute-done.1.other_ref) | copy-start | bytes 196612
  20.2 5.3 %collective-permute-start.2 = (f32[8,16,128]{2,1,0:T(8,128)}, f32[8,16,128]{2,1,0:T(8,128)S(1)}, u32[]{:S(2)}, u32[]{:S(2)}) collective-permute-start(f32[8,16,128]{2,1,0:T(8,128)} %cross_1.1.own_ref), channel_id=1, source_target_pairs={{0,4},{1,5},{2,6},{3,7},{4,0},{5,1},{6,2},{7,3},{8,12},{9,13},{10,... | collective-permute-start | bytes 196616 | tf_op jit(solution)/shard_map/swap_2/ppermute | solution.py:260
  22.0 8.1 %collective-permute-start.6 = (bf16[32,1024]{1,0:T(8,128)(2,1)S(1)}, bf16[32,1024]{1,0:T(8,128)(2,1)S(1)}, u32[]{:S(2)}, u32[]{:S(2)}) collective-permute-start(bf16[32,1024]{1,0:T(8,128)(2,1)S(1)} %get-tuple-element.11), channel_id=1, source_target_pairs={{0,31},{1,2},{2,1},{3,4},{4,3},{5,6},{6,5},{7,8},{8,7},{9,10},{10,... | collective-permute-start | bytes 196616 | tf_op jit(solution)/shard_map/halo_ring/ppermute | solution.py:224
  25.5 4.6 %collective-permute-start.5 = (bf16[32,1024]{1,0:T(8,128)(2,1)S(1)}, bf16[32,1024]{1,0:T(8,128)(2,1)S(1)}, u32[]{:S(2)}, u32[]{:S(2)}) collective-permute-start(bf16[32,1024]{1,0:T(8,128)(2,1)S(1)} %get-tuple-element.12), channel_id=1, source_target_pairs={{0,1},{1,0},{2,3},{3,2},{4,5},{5,4},{6,7},{7,6},{8,9},{9,8},{10,11... | collective-permute-start | bytes 196616 | tf_op jit(solution)/shard_map/halo_pair/ppermute | solution.py:222
  25.5 0.6 %copy-start.7 = (f32[8,16,128]{2,1,0:T(8,128)}, f32[8,16,128]{2,1,0:T(8,128)S(1)}, u32[]{:S(2)}) copy-start(f32[8,16,128]{2,1,0:T(8,128)S(1)} %collective-permute-done.2.other_ref) | copy-start | bytes 196612
  28.4 10.1 %collective-permute-start.3 = (f32[8,16,128]{2,1,0:T(8,128)}, f32[8,16,128]{2,1,0:T(8,128)S(1)}, u32[]{:S(2)}, u32[]{:S(2)}) collective-permute-start(f32[8,16,128]{2,1,0:T(8,128)} %cross_2.1.own_ref), channel_id=1, source_target_pairs={{0,8},{1,9},{2,10},{3,11},{4,12},{5,13},{6,14},{7,15},{8,0},{9,1},... | collective-permute-start | bytes 196616 | tf_op jit(solution)/shard_map/swap_3/ppermute | solution.py:260
  30.1 0.6 %copy-start.3 = (bf16[32,1024]{1,0:T(8,128)(2,1)}, bf16[32,1024]{1,0:T(8,128)(2,1)S(1)}, u32[]{:S(2)}) copy-start(bf16[32,1024]{1,0:T(8,128)(2,1)S(1)} %collective-permute-done.6.ring_ref) | copy-start | bytes 196612
  30.7 0.6 %copy-start.6 = (bf16[32,1024]{1,0:T(8,128)(2,1)}, bf16[32,1024]{1,0:T(8,128)(2,1)S(1)}, u32[]{:S(2)}) copy-start(bf16[32,1024]{1,0:T(8,128)(2,1)S(1)} %collective-permute-done.5.pair_ref) | copy-start | bytes 196612
  34.1 7.4 %collective-permute-start.7 = (f32[32,512]{1,0:T(8,128)}, f32[32,512]{1,0:T(8,128)S(1)}, u32[]{:S(2)}, u32[]{:S(2)}) collective-permute-start(f32[32,512]{1,0:T(8,128)} %get-tuple-element.9), channel_id=1, source_target_pairs={{0,1},{1,0},{2,3},{3,2},{4,5},{5,4},{6,7},{7,6},{8,9},{9,8},{10,11... | collective-permute-start | bytes 196616 | tf_op jit(solution)/shard_map/rim_pair/ppermute | solution.py:254
  34.1 7.5 %collective-permute-start.8 = (f32[32,512]{1,0:T(8,128)}, f32[32,512]{1,0:T(8,128)S(1)}, u32[]{:S(2)}, u32[]{:S(2)}) collective-permute-start(f32[32,512]{1,0:T(8,128)} %get-tuple-element.10), channel_id=1, source_target_pairs={{0,31},{1,2},{2,1},{3,4},{4,3},{5,6},{6,5},{7,8},{8,7},{9,10},{10,... | collective-permute-start | bytes 196616 | tf_op jit(solution)/shard_map/rim_ring/ppermute | solution.py:256
  38.6 0.6 %copy-start.2 = (f32[8,16,128]{2,1,0:T(8,128)}, f32[8,16,128]{2,1,0:T(8,128)S(1)}, u32[]{:S(2)}) copy-start(f32[8,16,128]{2,1,0:T(8,128)S(1)} %collective-permute-done.3.other_ref) | copy-start | bytes 196612
  41.5 5.4 %collective-permute-start.4 = (f32[8,16,128]{2,1,0:T(8,128)}, f32[8,16,128]{2,1,0:T(8,128)S(1)}, u32[]{:S(2)}, u32[]{:S(2)}) collective-permute-start(f32[8,16,128]{2,1,0:T(8,128)} %cross_3.1.own_ref), channel_id=1, source_target_pairs={{0,16},{1,17},{2,18},{3,19},{4,20},{5,21},{6,22},{7,23},{8,24},{9,... | collective-permute-start | bytes 196616 | tf_op jit(solution)/shard_map/swap_4/ppermute | solution.py:260
  41.5 5.4 %copy-start.1 = (f32[32,512]{1,0:T(8,128)}, f32[32,512]{1,0:T(8,128)S(1)}, u32[]{:S(2)}) copy-start(f32[32,512]{1,0:T(8,128)S(1)} %collective-permute-done.7.pair_ref) | copy-start | bytes 196612
  41.6 5.3 %copy-start.4 = (f32[32,512]{1,0:T(8,128)}, f32[32,512]{1,0:T(8,128)S(1)}, u32[]{:S(2)}) copy-start(f32[32,512]{1,0:T(8,128)S(1)} %collective-permute-done.8.ring_ref) | copy-start | bytes 196612
  46.9 0.6 %copy-start.8 = (f32[8,16,128]{2,1,0:T(8,128)}, f32[8,16,128]{2,1,0:T(8,128)S(1)}, u32[]{:S(2)}) copy-start(f32[8,16,128]{2,1,0:T(8,128)S(1)} %collective-permute-done.4.other_ref) | copy-start | bytes 196612

commit v2 on v1

--- a/solution.py
+++ b/solution.py
@@ -178,8 +178,8 @@
         window[halo + box] = signal_ref[:, pl.ds(box * LEAF, LEAF)]
     sums[...] = jnp.zeros_like(sums)
     for slot in range(blocks_ref.shape[0]):
-        row = jnp.maximum(list_ref[slot, 0], 0)
-        col = list_ref[slot, 1]
+        row = jnp.maximum(list_ref[0, slot], 0)
+        col = list_ref[1, slot]
         col = jnp.where(col < 0, sums.shape[0] - 1, col)
         out = dot(window[row], blocks_ref[slot])
         real = out[:rhs, :LEAF] + out[rhs:, LEAF:]
@@ -199,6 +199,21 @@
 SMEM = pl.BlockSpec(memory_space=pltpu.SMEM)
 
 
+def on_chip(kernel, name, outs, scalars, arrays, scratch=(), grant=16 << 20):
+    single = len(outs) == 2 and not isinstance(outs[1], tuple)
+    shapes = tuple(pltpu.VMEM(shape, kind) for shape, kind in ((outs,) if single else outs))
+    call = pl.pallas_call(
+        kernel,
+        out_shape=shapes[0] if single else shapes,
+        in_specs=[SMEM] * len(scalars) + [VMEM] * len(arrays),
+        out_specs=VMEM if single else (VMEM,) * len(shapes),
+        scratch_shapes=list(scratch),
+        compiler_params=pltpu.CompilerParams(vmem_limit_bytes=grant),
+        name=name,
+    )
+    return call(*scalars, *[pltpu.with_memory_space_constraint(x, pltpu.VMEM) for x in arrays])
+
+
 def shards(signal, row_basis, transfer, column_basis, near_blocks, near_list):
     channels = signal.shape[0]
     rhs = channels // 2
@@ -223,33 +238,31 @@
     with jax.named_scope("halo_ring"):
         from_ring = lax.ppermute(to_ring, AXES, ring)
 
-    state_type = jax.ShapeDtypeStruct((half, rhs, width), F32)
-    coeffs = pl.pallas_call(
-        local_kernel, out_shape=state_type, in_specs=[VMEM] * 3, out_specs=VMEM, name="local"
-    )(signal, row_basis, transfer)
+    state = ((half, rhs, width), F32)
+    coeffs = on_chip(local_kernel, "local", state, (), (signal, row_basis, transfer))
     cross_levels = levels - local_levels
-    matrices = pl.pallas_call(
+    matrices = on_chip(
         functools.partial(matrices_kernel, first_level=local_levels),
-        out_shape=jax.ShapeDtypeStruct((cross_levels, half, width, width), BF16),
-        in_specs=[VMEM],
-        out_specs=VMEM,
-        name="matrices",
-    )(transfer)
-    center, rim_pair, rim_ring = pl.pallas_call(
+        "matrices",
+        ((cross_levels, half, width, width), BF16),
+        (),
+        (transfer,),
+    )
+    center, rim_pair, rim_ring = on_chip(
         near_kernel,
-        out_shape=(
-            jax.ShapeDtypeStruct((boxes, channels, LEAF), F32),
-            jax.ShapeDtypeStruct((channels, reach * LEAF), F32),
-            jax.ShapeDtypeStruct((channels, reach * LEAF), F32),
+        "near",
+        (
+            ((boxes, channels, LEAF), F32),
+            ((channels, reach * LEAF), F32),
+            ((channels, reach * LEAF), F32),
         ),
-        in_specs=[SMEM, SMEM, VMEM, VMEM, VMEM, VMEM],
-        out_specs=(VMEM, VMEM, VMEM),
-        scratch_shapes=[
+        (index_word, near_list.T),
+        (signal, from_pair, from_ring, near_blocks),
+        scratch=(
             pltpu.VMEM((boxes + 4 * reach, channels, LEAF), BF16),
             pltpu.VMEM((boxes + 2 * reach + 1, channels, LEAF), F32),
-        ],
-        name="near",
-    )(index_word, near_list, signal, from_pair, from_ring, near_blocks)
+        ),
+    )
     with jax.named_scope("rim_pair"):
         rim_from_pair = lax.ppermute(rim_pair, AXES, pairs)
     with jax.named_scope("rim_ring"):
@@ -259,20 +272,27 @@
         with jax.named_scope(f"swap_{level}"):
             other = lax.ppermute(coeffs, AXES, [(i, i ^ 1 << level) for i in range(devices)])
         if level + 1 < cross_levels:
-            coeffs = pl.pallas_call(
+            coeffs = on_chip(
                 functools.partial(cross_kernel, level=level),
-                out_shape=state_type,
-                in_specs=[SMEM, VMEM, VMEM, VMEM],
-                out_specs=VMEM,
-                name=f"cross_{level}",
-            )(index_word, coeffs, other, matrices)
+                f"cross_{level}",
+                state,
+                (index_word,),
+                (coeffs, other, matrices),
+            )
     return pl.pallas_call(
         functools.partial(final_kernel, level=cross_levels - 1),
         out_shape=jax.ShapeDtypeStruct((channels, boxes * LEAF), F32),
         in_specs=[SMEM] + [VMEM] * 7,
         out_specs=VMEM,
+        compiler_params=pltpu.CompilerParams(vmem_limit_bytes=16 << 20),
         name="final",
-    )(index_word, coeffs, other, matrices, column_basis, center, rim_from_pair, rim_from_ring)
+    )(
+        index_word,
+        *[
+            pltpu.with_memory_space_constraint(x, pltpu.VMEM)
+            for x in (coeffs, other, matrices, column_basis, center, rim_from_pair, rim_from_ring)
+        ],
+    )
 
 
 def solution(mesh):

time: 50.5 us -> 34.8 us (0.69)
  Pallas kernels: 23 us -> 7.2 us
  waiting for transfers between devices: 8.34 us -> 10.7 us
  local copies, waits for them, and re-layouts: 5.06 us -> 3.15 us
    pallas_call x7, Pallas kernels: 20.3 us -> 6.01 us  [on_chip(): call(*scalars, *[pltpu.with_memory_space_constraint(x, pltpu.VMEM) for x...]
    ppermute x5, waiting for transfers between devices: 8.23 us -> 4.2 us  [shards(): lax.ppermute(coeffs, AXES, [(i, i ^ 1 << level) for i in range(devices)])]
    ppermute x1, waiting for transfers between devices: 0.11 us -> 3.69 us  [shards(): rim_from_ring = lax.ppermute(rim_ring, AXES, ring)]
    ppermute x1, waiting for transfers between devices: 0.01 us -> 2.81 us  [shards(): from_ring = lax.ppermute(to_ring, AXES, ring)]
    unnamed x23 -> x14, local copies, waits for them, and re-layouts: 5.05 us -> 3.14 us
    pallas_call x1, Pallas kernels: 2.72 us -> 1.19 us  [shards(): pl.pallas_call(functools.partial(final_kernel, level=cross_levels - 1), o...]
    ppermute x1, starting transfers between devices: 4.47 us -> 3.93 us  [shards(): rim_from_ring = lax.ppermute(rim_ring, AXES, ring)]
  transfers between devices with their start and end apart: 9 -> 9, of which waited for: 3 -> 4; matrix products, arithmetic and copies ran while one was open for 1% -> 0% of each run, Pallas kernels for 25% -> 12%
where the time goes in v2:
time: 34.8 us; the launch traced here: 34.6 us
  starting transfers between devices  13.4 us (39%)
  waiting for transfers between devices  10.7 us (31%)
  Pallas kernels  7.2 us (21%)
  local copies, waits for them, and re-layouts  3.15 us (9%)
    pallas_call x7, Pallas kernels, on_chip(): call(*scalars, *[pltpu.with_memory_space_constraint(x, pltpu.VMEM) for x...  6.01 us
    ppermute x5, starting transfers between devices, shards(): lax.ppermute(coeffs, AXES, [(i, i ^ 1 << level) for i in range(devices)])  5.88 us
    ppermute x5, waiting for transfers between devices, shards(): lax.ppermute(coeffs, AXES, [(i, i ^ 1 << level) for i in range(devices)])  4.2 us
    ppermute x1, starting transfers between devices, shards(): rim_from_ring = lax.ppermute(rim_ring, AXES, ring)  3.93 us
    ppermute x1, waiting for transfers between devices, shards(): rim_from_ring = lax.ppermute(rim_ring, AXES, ring)  3.69 us
    ppermute x1, starting transfers between devices, shards(): from_ring = lax.ppermute(to_ring, AXES, ring)  3.5 us
    unnamed x14, local copies, waits for them, and re-layouts  3.14 us
    ppermute x1, waiting for transfers between devices, shards(): from_ring = lax.ppermute(to_ring, AXES, ring)  2.81 us
  transfers between devices with their start and end apart: 9, of which 4 were waited for; matrix products, arithmetic and copies ran while one was open for 0% of the time, Pallas kernels for 12%

profile of v2, /device:TPU:0, one launch (start us, length us, event | category | flops | bytes accessed | tf_op | source)
XLA Modules:
  0.0 34.6 jit_solution(13463496126542658669)
XLA Ops:
  0.0 0.0 copy-start
  0.0 1.3 %copy-done = bf16[16,9,32,128]{3,2,1,0:T(8,128)(2,1)S(1)} copy-done((bf16[16,9,32,128]{3,2,1,0:T(8,128)(2,1)S(1)}, bf16[16,9,32,128]{3,2,1,0:T(8,128)(2,1)}, u32[]{:S(2)}) %copy-start) | copy-done | bytes 1179672
  1.3 0.0 copy-start.2
  1.3 0.9 %copy-done.2 = bf16[32,2048]{1,0:T(8,128)(2,1)S(1)} copy-done((bf16[32,2048]{1,0:T(8,128)(2,1)S(1)}, bf16[32,2048]{1,0:T(8,128)(2,1)}, u32[]{:S(2)}) %copy-start.2) | copy-done | bytes 131096
  2.2 0.0 copy-start.4
  2.2 0.9 %copy-done.4 = bf16[64,2048]{1,0:T(8,128)(2,1)S(1)} copy-done((bf16[64,2048]{1,0:T(8,128)(2,1)S(1)}, bf16[64,2048]{1,0:T(8,128)(2,1)}, u32[]{:S(2)}) %copy-start.4) | copy-done | bytes 262168
  3.1 1.3 %local.1.own_ref = f32[8,16,128]{2,1,0:T(8,128)S(1)} custom-call(bf16[32,2048]{1,0:T(8,128)(2,1)S(1)} %copy-done.2, bf16[64,2048]{1,0:T(8,128)(2,1)S(1)} %copy-done.4, bf16[16,9,32,128]{3,2,1,0:T(8,128)(2,1)S(1)} %copy-done), custom_call_target="tpu_custom_call" | custom-call | tf_op jit(solution)/shard_map/local/pallas_call | solution.py:214
  4.4 0.6 %collective-permute-start = (f32[8,16,128]{2,1,0:T(8,128)S(1)}, f32[8,16,128]{2,1,0:T(8,128)S(1)}, u32[]{:S(2)}, u32[]{:S(2)}) collective-permute-start(f32[8,16,128]{2,1,0:T(8,128)S(1)} %local.1.own_ref), channel_id=1, source_target_pairs={{0,1},{1,0},{2,3},{3,2},{4,5},{5,4},{6,7},{7,6},{8,9},{9,8},{10,11... | collective-permute-start | bytes 196616 | tf_op jit(solution)/shard_map/swap_0/ppermute | solution.py:273
  5.0 2.7 %matrices.1.matrices_ref = bf16[5,8,128,128]{3,2,1,0:T(8,128)(2,1)S(1)} custom-call(bf16[16,9,32,128]{3,2,1,0:T(8,128)(2,1)S(1)} %copy-done), custom_call_target="tpu_custom_call" | custom-call | tf_op jit(solution)/shard_map/matrices/pallas_call | solution.py:214
  7.7 0.0 collective-permute-done.other_ref
  7.7 0.0 copy-start.3
  7.7 0.3 cross_0.1.own_ref
  8.0 2.6 %collective-permute-start.1 = (f32[8,16,128]{2,1,0:T(8,128)S(1)}, f32[8,16,128]{2,1,0:T(8,128)S(1)}, u32[]{:S(2)}, u32[]{:S(2)}) collective-permute-start(f32[8,16,128]{2,1,0:T(8,128)S(1)} %cross_0.1.own_ref), channel_id=1, source_target_pairs={{0,2},{1,3},{2,0},{3,1},{4,6},{5,7},{6,4},{7,5},{8,10},{9,11},{10,... | collective-permute-start | bytes 196616 | tf_op jit(solution)/shard_map/swap_1/ppermute | solution.py:273
  10.5 0.0 copy-start.1
  10.6 0.0 copy-start.6
  10.6 2.7 %collective-permute-done.1.other_ref = f32[8,16,128]{2,1,0:T(8,128)S(1)} collective-permute-done((f32[8,16,128]{2,1,0:T(8,128)S(1)}, f32[8,16,128]{2,1,0:T(8,128)S(1)}, u32[]{:S(2)}, u32[]{:S(2)}) %collective-permute-start.1) | collective-permute-done | bytes 65568 | tf_op jit(solution)/shard_map/swap_1/ppermute | solution.py:273
  13.3 0.3 cross_1.1.own_ref
  13.6 1.8 %collective-permute-start.2 = (f32[8,16,128]{2,1,0:T(8,128)S(1)}, f32[8,16,128]{2,1,0:T(8,128)S(1)}, u32[]{:S(2)}, u32[]{:S(2)}) collective-permute-start(f32[8,16,128]{2,1,0:T(8,128)S(1)} %cross_1.1.own_ref), channel_id=1, source_target_pairs={{0,4},{1,5},{2,6},{3,7},{4,0},{5,1},{6,2},{7,3},{8,12},{9,13},{10,... | collective-permute-start | bytes 196616 | tf_op jit(solution)/shard_map/swap_2/ppermute | solution.py:273
  15.4 0.0 copy-done.3
  15.4 3.5 %collective-permute-start.6 = (bf16[32,1024]{1,0:T(8,128)(2,1)S(1)}, bf16[32,1024]{1,0:T(8,128)(2,1)S(1)}, u32[]{:S(2)}, u32[]{:S(2)}) collective-permute-start(bf16[32,1024]{1,0:T(8,128)(2,1)S(1)} %get-tuple-element.11), channel_id=1, source_target_pairs={{0,31},{1,2},{2,1},{3,4},{4,3},{5,6},{6,5},{7,8},{8,7},{9,10},{10,... | collective-permute-start | bytes 196616 | tf_op jit(solution)/shard_map/halo_ring/ppermute | solution.py:239
  18.9 0.0 collective-permute-start.5
  18.9 0.0 collective-permute-done.2.other_ref
  18.9 0.3 cross_2.1.own_ref
  19.2 0.9 %collective-permute-start.3 = (f32[8,16,128]{2,1,0:T(8,128)S(1)}, f32[8,16,128]{2,1,0:T(8,128)S(1)}, u32[]{:S(2)}, u32[]{:S(2)}) collective-permute-start(f32[8,16,128]{2,1,0:T(8,128)S(1)} %cross_2.1.own_ref), channel_id=1, source_target_pairs={{0,8},{1,9},{2,10},{3,11},{4,12},{5,13},{6,14},{7,15},{8,0},{9,1},... | collective-permute-start | bytes 196616 | tf_op jit(solution)/shard_map/swap_3/ppermute | solution.py:273
  20.0 2.8 %collective-permute-done.6.ring_ref = bf16[32,1024]{1,0:T(8,128)(2,1)S(1)} collective-permute-done((bf16[32,1024]{1,0:T(8,128)(2,1)S(1)}, bf16[32,1024]{1,0:T(8,128)(2,1)S(1)}, u32[]{:S(2)}, u32[]{:S(2)}) %collective-permute-start.6) | collective-permute-done | bytes 65568 | tf_op jit(solution)/shard_map/halo_ring/ppermute | solution.py:239
  22.9 0.0 collective-permute-done.5.pair_ref
  22.9 0.0 copy-done.1
  22.9 0.0 copy-done.6
  22.9 0.0 copy-start.5
  22.9 1.0 %near.1 = (f32[16,32,128]{2,1,0:T(8,128)S(1)}, f32[32,512]{1,0:T(8,128)S(1)}, f32[32,512]{1,0:T(8,128)S(1)}) custom-call(s32[1]{0:T(128)} %bitcast.index_ref, s32[2,24]{1,0:T(2,128)S(1)} %bitcast.2, bf16[32,2048]{1,0:T(8,128)(2,1)S(1)} %copy-done.3, bf16[32,1024]{1,0:T(8,128)(2,1)S(1)} %collective-permute-done.5.pair_ref, ...), custom_call_target="tpu_custom_call" | custom-call | tf_op jit(solution)/shard_map/near/pallas_call | solution.py:214
  23.9 0.1 collective-permute-start.7
  23.9 3.9 %collective-permute-start.8 = (f32[32,512]{1,0:T(8,128)S(1)}, f32[32,512]{1,0:T(8,128)S(1)}, u32[]{:S(2)}, u32[]{:S(2)}) collective-permute-start(f32[32,512]{1,0:T(8,128)S(1)} %get-tuple-element.10), channel_id=1, source_target_pairs={{0,31},{1,2},{2,1},{3,4},{4,3},{5,6},{6,5},{7,8},{8,7},{9,10},{10,... | collective-permute-start | bytes 196616 | tf_op jit(solution)/shard_map/rim_ring/ppermute | solution.py:269
  27.9 0.0 collective-permute-done.3.other_ref
  27.9 0.3 cross_3.1.own_ref
  28.1 0.1 collective-permute-start.4
  28.2 0.0 collective-permute-done.7.pair_ref
  28.2 3.7 %collective-permute-done.8.ring_ref = f32[32,512]{1,0:T(8,128)S(1)} collective-permute-done((f32[32,512]{1,0:T(8,128)S(1)}, f32[32,512]{1,0:T(8,128)S(1)}, u32[]{:S(2)}, u32[]{:S(2)}) %collective-permute-start.8) | collective-permute-done | bytes 65568 | tf_op jit(solution)/shard_map/rim_ring/ppermute | solution.py:269
  31.9 1.4 %collective-permute-done.4.other_ref = f32[8,16,128]{2,1,0:T(8,128)S(1)} collective-permute-done((f32[8,16,128]{2,1,0:T(8,128)S(1)}, f32[8,16,128]{2,1,0:T(8,128)S(1)}, u32[]{:S(2)}, u32[]{:S(2)}) %collective-permute-start.4) | collective-permute-done | bytes 65568 | tf_op jit(solution)/shard_map/swap_4/ppermute | solution.py:273
  33.4 0.0 copy-done.5
  33.4 1.2 %final.1 = f32[32,2048]{1,0:T(8,128)} custom-call(s32[1]{0:T(128)} %bitcast.index_ref, f32[8,16,128]{2,1,0:T(8,128)S(1)} %cross_3.1.own_ref, f32[8,16,128]{2,1,0:T(8,128)S(1)} %collective-permute-done.4.other_ref, bf16[5,8,128,128]{3,2,1,0:T(8,128)(2,1)S(1)} %matrices.1.matrices_ref, bf16[64,2048]{1,0:T(8,128)(2,1)S(1)} %copy-done.5, ...), custom_call_target="tpu_custom_call" | custom-call | tf_op jit(solution)/shard_map/final/pallas_call | solution.py:282
  (1 shorter events, 0.0 us)
Async XLA Ops:
  0.0 1.3 %copy-start = (bf16[16,9,32,128]{3,2,1,0:T(8,128)(2,1)S(1)}, bf16[16,9,32,128]{3,2,1,0:T(8,128)(2,1)}, u32[]{:S(2)}) copy-start(bf16[16,9,32,128]{3,2,1,0:T(8,128)(2,1)} %transfer_ref.3) | copy-start | bytes 3538948
  1.3 0.9 %copy-start.2 = (bf16[32,2048]{1,0:T(8,128)(2,1)S(1)}, bf16[32,2048]{1,0:T(8,128)(2,1)}, u32[]{:S(2)}) copy-start(bf16[32,2048]{1,0:T(8,128)(2,1)} %signal_ref.3) | copy-start | bytes 393220
  2.2 0.9 %copy-start.4 = (bf16[64,2048]{1,0:T(8,128)(2,1)S(1)}, bf16[64,2048]{1,0:T(8,128)(2,1)}, u32[]{:S(2)}) copy-start(bf16[64,2048]{1,0:T(8,128)(2,1)} %basis_ref.2) | copy-start | bytes 786436
  4.4 3.3 %collective-permute-start = (f32[8,16,128]{2,1,0:T(8,128)S(1)}, f32[8,16,128]{2,1,0:T(8,128)S(1)}, u32[]{:S(2)}, u32[]{:S(2)}) collective-permute-start(f32[8,16,128]{2,1,0:T(8,128)S(1)} %local.1.own_ref), channel_id=1, source_target_pairs={{0,1},{1,0},{2,3},{3,2},{4,5},{5,4},{6,7},{7,6},{8,9},{9,8},{10,11... | collective-permute-start | bytes 196616 | tf_op jit(solution)/shard_map/swap_0/ppermute | solution.py:273
  7.7 7.7 %copy-start.3 = (bf16[32,2048]{1,0:T(8,128)(2,1)S(1)}, bf16[32,2048]{1,0:T(8,128)(2,1)}, u32[]{:S(2)}) copy-start(bf16[32,2048]{1,0:T(8,128)(2,1)} %signal_ref.3) | copy-start | bytes 393220
  8.0 5.3 %collective-permute-start.1 = (f32[8,16,128]{2,1,0:T(8,128)S(1)}, f32[8,16,128]{2,1,0:T(8,128)S(1)}, u32[]{:S(2)}, u32[]{:S(2)}) collective-permute-start(f32[8,16,128]{2,1,0:T(8,128)S(1)} %cross_0.1.own_ref), channel_id=1, source_target_pairs={{0,2},{1,3},{2,0},{3,1},{4,6},{5,7},{6,4},{7,5},{8,10},{9,11},{10,... | collective-permute-start | bytes 196616 | tf_op jit(solution)/shard_map/swap_1/ppermute | solution.py:273
  10.5 12.3 %copy-start.1 = (bf16[24,128,256]{2,1,0:T(8,128)(2,1)S(1)}, bf16[24,128,256]{2,1,0:T(8,128)(2,1)}, u32[]{:S(2)}) copy-start(bf16[24,128,256]{2,1,0:T(8,128)(2,1)} %blocks_ref.1) | copy-start | bytes 4718596
  10.6 12.3 %copy-start.6 = (s32[24,2]{0,1:T(2,128)S(1)}, s32[24,2]{0,1:T(2,128)}, u32[]{:S(2)}) copy-start(s32[24,2]{0,1:T(2,128)} %param.11) | copy-start | bytes 580
  13.6 5.4 %collective-permute-start.2 = (f32[8,16,128]{2,1,0:T(8,128)S(1)}, f32[8,16,128]{2,1,0:T(8,128)S(1)}, u32[]{:S(2)}, u32[]{:S(2)}) collective-permute-start(f32[8,16,128]{2,1,0:T(8,128)S(1)} %cross_1.1.own_ref), channel_id=1, source_target_pairs={{0,4},{1,5},{2,6},{3,7},{4,0},{5,1},{6,2},{7,3},{8,12},{9,13},{10,... | collective-permute-start | bytes 196616 | tf_op jit(solution)/shard_map/swap_2/ppermute | solution.py:273
  15.4 7.5 %collective-permute-start.6 = (bf16[32,1024]{1,0:T(8,128)(2,1)S(1)}, bf16[32,1024]{1,0:T(8,128)(2,1)S(1)}, u32[]{:S(2)}, u32[]{:S(2)}) collective-permute-start(bf16[32,1024]{1,0:T(8,128)(2,1)S(1)} %get-tuple-element.11), channel_id=1, source_target_pairs={{0,31},{1,2},{2,1},{3,4},{4,3},{5,6},{6,5},{7,8},{8,7},{9,10},{10,... | collective-permute-start | bytes 196616 | tf_op jit(solution)/shard_map/halo_ring/ppermute | solution.py:239
  18.9 4.0 %collective-permute-start.5 = (bf16[32,1024]{1,0:T(8,128)(2,1)S(1)}, bf16[32,1024]{1,0:T(8,128)(2,1)S(1)}, u32[]{:S(2)}, u32[]{:S(2)}) collective-permute-start(bf16[32,1024]{1,0:T(8,128)(2,1)S(1)} %get-tuple-element.12), channel_id=1, source_target_pairs={{0,1},{1,0},{2,3},{3,2},{4,5},{5,4},{6,7},{7,6},{8,9},{9,8},{10,11... | collective-permute-start | bytes 196616 | tf_op jit(solution)/shard_map/halo_pair/ppermute | solution.py:237
  19.2 8.7 %collective-permute-start.3 = (f32[8,16,128]{2,1,0:T(8,128)S(1)}, f32[8,16,128]{2,1,0:T(8,128)S(1)}, u32[]{:S(2)}, u32[]{:S(2)}) collective-permute-start(f32[8,16,128]{2,1,0:T(8,128)S(1)} %cross_2.1.own_ref), channel_id=1, source_target_pairs={{0,8},{1,9},{2,10},{3,11},{4,12},{5,13},{6,14},{7,15},{8,0},{9,1},... | collective-permute-start | bytes 196616 | tf_op jit(solution)/shard_map/swap_3/ppermute | solution.py:273
  22.9 10.5 %copy-start.5 = (bf16[64,2048]{1,0:T(8,128)(2,1)S(1)}, bf16[64,2048]{1,0:T(8,128)(2,1)}, u32[]{:S(2)}) copy-start(bf16[64,2048]{1,0:T(8,128)(2,1)} %basis_ref.3) | copy-start | bytes 786436
  23.9 4.4 %collective-permute-start.7 = (f32[32,512]{1,0:T(8,128)S(1)}, f32[32,512]{1,0:T(8,128)S(1)}, u32[]{:S(2)}, u32[]{:S(2)}) collective-permute-start(f32[32,512]{1,0:T(8,128)S(1)} %get-tuple-element.9), channel_id=1, source_target_pairs={{0,1},{1,0},{2,3},{3,2},{4,5},{5,4},{6,7},{7,6},{8,9},{9,8},{10,11... | collective-permute-start | bytes 196616 | tf_op jit(solution)/shard_map/rim_pair/ppermute | solution.py:267
  23.9 8.0 %collective-permute-start.8 = (f32[32,512]{1,0:T(8,128)S(1)}, f32[32,512]{1,0:T(8,128)S(1)}, u32[]{:S(2)}, u32[]{:S(2)}) collective-permute-start(f32[32,512]{1,0:T(8,128)S(1)} %get-tuple-element.10), channel_id=1, source_target_pairs={{0,31},{1,2},{2,1},{3,4},{4,3},{5,6},{6,5},{7,8},{8,7},{9,10},{10,... | collective-permute-start | bytes 196616 | tf_op jit(solution)/shard_map/rim_ring/ppermute | solution.py:269
  28.1 5.2 %collective-permute-start.4 = (f32[8,16,128]{2,1,0:T(8,128)S(1)}, f32[8,16,128]{2,1,0:T(8,128)S(1)}, u32[]{:S(2)}, u32[]{:S(2)}) collective-permute-start(f32[8,16,128]{2,1,0:T(8,128)S(1)} %cross_3.1.own_ref), channel_id=1, source_target_pairs={{0,16},{1,17},{2,18},{3,19},{4,20},{5,21},{6,22},{7,23},{8,24},{9,... | collective-permute-start | bytes 196616 | tf_op jit(solution)/shard_map/swap_4/ppermute | solution.py:273

commit v3 on v2

--- a/solution.py
+++ b/solution.py
@@ -2,6 +2,7 @@
 
 import jax
 import jax.numpy as jnp
+import numpy as np
 from jax import lax
 from jax.experimental import pallas as pl
 from jax.experimental.pallas import tpu as pltpu
@@ -39,19 +40,32 @@
     return [top, rest]
 
 
-def level_matrix(first, second):
-    a = first.astype(F32)
-    b = second.astype(F32)
-    width = a.shape[1]
-    quarter = width // 4
-    low = pick_low(a, half_roll(b))
-    high = pick_low(half_roll(a), b)
-    is_real = lanes_like(a) % (2 * quarter) < quarter
-    rows = []
-    for part in (low, high):
-        rows.append(jnp.where(is_real, part, -part))
-        rows.append(jnp.where(is_real, pltpu.roll(part, width - quarter, 1), pltpu.roll(part, quarter, 1)))
-    return jnp.concatenate(rows, axis=0).astype(BF16)
+def form_table(rank):
+    width = 4 * rank
+    table = np.zeros((2 * width, 4 * width), np.float32)
+    unit = np.eye(rank, dtype=np.float32)
+    for group in range(4):
+        child, imag = divmod(group, 2)
+        for box in range(2):
+            for part in range(2):
+                source = box * width + child * 2 * rank + (part ^ imag) * rank
+                target = group * width + box * 2 * rank + part * rank
+                sign = -1.0 if part and not imag else 1.0
+                table[source : source + rank, target : target + rank] = sign * unit
+    return table
+
+
+def level_matrices(blocks, pairs, table):
+    rows = [jnp.concatenate([blocks[first], blocks[second]], axis=1) for first, second in pairs]
+    rank, width = rows[0].shape
+    width //= 2
+    out = dot(jnp.concatenate(rows, axis=0), table).astype(BF16)
+    return [
+        jnp.concatenate(
+            [out[k * rank : (k + 1) * rank, g * width : (g + 1) * width] for g in range(4)], axis=0
+        )
+        for k in range(len(pairs))
+    ]
 
 
 def project_pair(signal_ref, basis_ref, first, second):
@@ -70,18 +84,33 @@
     return pick_low(out[:rhs], out[rhs:])
 
 
-def local_kernel(signal_ref, basis_ref, transfer_ref, out_ref):
-    boxes = transfer_ref.shape[0]
+def local_kernel(
+    signal_hbm, basis_hbm, transfer_hbm, table_hbm, out_ref, signal_ref, basis_ref, transfer_ref, table_ref, arrived
+):
+    boxes, levels = transfer_ref.shape[:2]
     rhs = signal_ref.shape[0] // 2
-    levels = boxes.bit_length() - 1
+    copies = [
+        pltpu.make_async_copy(signal_hbm, signal_ref, arrived.at[0]),
+        pltpu.make_async_copy(basis_hbm, basis_ref, arrived.at[1]),
+        pltpu.make_async_copy(table_hbm, table_ref, arrived.at[2]),
+        pltpu.make_async_copy(transfer_hbm.at[:, pl.ds(0, levels)], transfer_ref, arrived.at[3]),
+    ]
+    for copy in copies:
+        copy.start()
+    for copy in copies[:2]:
+        copy.wait()
     state = {}
     for box in range(0, boxes, 2):
         state[box] = project_pair(signal_ref, basis_ref, box, box + 1)
+    for copy in copies[2:]:
+        copy.wait()
+    table = table_ref[...]
     for level in range(levels):
         bit = 1 << level
+        blocks = [transfer_ref[box, level] for box in range(boxes)]
+        matrices = level_matrices(blocks, [(box, box + bit) for box in state], table)
         done = {}
-        for box, pair in state.items():
-            matrix = level_matrix(transfer_ref[box, level], transfer_ref[box + bit, level])
+        for matrix, (box, pair) in zip(matrices, state.items()):
             both = dot(jnp.concatenate(split_rows(pair), axis=0), matrix)
             done[box] = both[:rhs] + both[rhs:]
         state = done
@@ -97,13 +126,15 @@
         out_ref[box] = pair
 
 
-def matrices_kernel(transfer_ref, out_ref, *, first_level):
-    half = transfer_ref.shape[0] // 2
+def matrices_kernel(transfer_ref, table_ref, out_ref, *, first_level):
+    boxes = transfer_ref.shape[0]
+    half = boxes // 2
+    table = table_ref[...]
     for level in range(out_ref.shape[0]):
+        blocks = [transfer_ref[box, first_level + level] for box in range(boxes)]
+        matrices = level_matrices(blocks, [(box, box + half) for box in range(half)], table)
         for box in range(half):
-            out_ref[level, box] = level_matrix(
-                transfer_ref[box, first_level + level], transfer_ref[box + half, first_level + level]
-            )
+            out_ref[level, box] = matrices[box]
 
 
 def crossed(own_ref, other_ref, matrices_ref, level, upper, box):
@@ -238,15 +269,30 @@
     with jax.named_scope("halo_ring"):
         from_ring = lax.ppermute(to_ring, AXES, ring)
 
+    table = jnp.asarray(form_table(rank), BF16)
     state = ((half, rhs, width), F32)
-    coeffs = on_chip(local_kernel, "local", state, (), (signal, row_basis, transfer))
+    coeffs = pl.pallas_call(
+        local_kernel,
+        out_shape=pltpu.VMEM(*state),
+        in_specs=[pl.BlockSpec(memory_space=pl.ANY)] * 4,
+        out_specs=VMEM,
+        scratch_shapes=[
+            pltpu.VMEM(signal.shape, BF16),
+            pltpu.VMEM(row_basis.shape, BF16),
+            pltpu.VMEM((boxes, local_levels, rank, width), BF16),
+            pltpu.VMEM(table.shape, BF16),
+            pltpu.SemaphoreType.DMA((4,)),
+        ],
+        compiler_params=pltpu.CompilerParams(vmem_limit_bytes=16 << 20),
+        name="local",
+    )(*[pltpu.with_memory_space_constraint(x, pltpu.HBM) for x in (signal, row_basis, transfer, table)])
     cross_levels = levels - local_levels
     matrices = on_chip(
         functools.partial(matrices_kernel, first_level=local_levels),
         "matrices",
         ((cross_levels, half, width, width), BF16),
         (),
-        (transfer,),
+        (transfer, table),
     )
     center, rim_pair, rim_ring = on_chip(
         near_kernel,

time: 34.8 us -> 30.4 us (0.87)
  local copies, waits for them, and re-layouts: 3.15 us -> 0.03 us
  Pallas kernels: 7.2 us -> 6.2 us
    pallas_call x7 -> x6, Pallas kernels: 6.01 us -> 2.5 us  [on_chip(): call(*scalars, *[pltpu.with_memory_space_constraint(x, pltpu.VMEM) for x...]
    unnamed x14 -> x12, local copies, waits for them, and re-layouts: 3.14 us -> 0.02 us
    pallas_call x0 -> x1, Pallas kernels: none -> 2.5 us  [shards(): pl.pallas_call(local_kernel, out_shape=pltpu.VMEM(*state), in_specs=[pl.B...]
    ppermute x5, starting transfers between devices: 5.88 us -> 6.96 us  [shards(): lax.ppermute(coeffs, AXES, [(i, i ^ 1 << level) for i in range(devices)])]
    ppermute x1, starting transfers between devices: 3.5 us -> 2.86 us  [shards(): from_ring = lax.ppermute(to_ring, AXES, ring)]
    ppermute x1, starting transfers between devices: 3.93 us -> 3.3 us  [shards(): rim_from_ring = lax.ppermute(rim_ring, AXES, ring)]
    ppermute x1, waiting for transfers between devices: 3.69 us -> 4.32 us  [shards(): rim_from_ring = lax.ppermute(rim_ring, AXES, ring)]
    ppermute x5, waiting for transfers between devices: 4.2 us -> 3.62 us  [shards(): lax.ppermute(coeffs, AXES, [(i, i ^ 1 << level) for i in range(devices)])]
  transfers between devices with their start and end apart: 9 -> 9, of which waited for: 4 -> 5; matrix products, arithmetic and copies ran while one was open for 0% -> 0% of each run, Pallas kernels for 12% -> 7%
where the time goes in v3:
time: 30.4 us; the launch traced here: 30.3 us
  starting transfers between devices  13.2 us (43%)
  waiting for transfers between devices  10.8 us (36%)
  Pallas kernels  6.2 us (20%)
    ppermute x5, starting transfers between devices, shards(): lax.ppermute(coeffs, AXES, [(i, i ^ 1 << level) for i in range(devices)])  6.96 us
    ppermute x1, waiting for transfers between devices, shards(): rim_from_ring = lax.ppermute(rim_ring, AXES, ring)  4.32 us
    ppermute x5, waiting for transfers between devices, shards(): lax.ppermute(coeffs, AXES, [(i, i ^ 1 << level) for i in range(devices)])  3.62 us
    ppermute x1, starting transfers between devices, shards(): rim_from_ring = lax.ppermute(rim_ring, AXES, ring)  3.3 us
    ppermute x1, starting transfers between devices, shards(): from_ring = lax.ppermute(to_ring, AXES, ring)  2.86 us
    ppermute x1, waiting for transfers between devices, shards(): from_ring = lax.ppermute(to_ring, AXES, ring)  2.83 us
    pallas_call x6, Pallas kernels, on_chip(): call(*scalars, *[pltpu.with_memory_space_constraint(x, pltpu.VMEM) for x...  2.5 us
    pallas_call x1, Pallas kernels, shards(): pl.pallas_call(local_kernel, out_shape=pltpu.VMEM(*state), in_specs=[pl.B...  2.5 us
  transfers between devices with their start and end apart: 9, of which 5 were waited for; matrix products, arithmetic and copies ran while one was open for 0% of the time, Pallas kernels for 7%

profile of v3, /device:TPU:0, one launch (start us, length us, event | category | flops | bytes accessed | tf_op | source)
XLA Modules:
  0.0 30.3 jit_solution(12550462019034452613)
XLA Ops:
  0.0 0.0 copy-start.3
  0.0 0.0 copy-start
  0.0 2.5 %local.1.own_ref = f32[8,16,128]{2,1,0:T(8,128)S(1)} custom-call(bf16[32,2048]{1,0:T(8,128)(2,1)} %signal_ref.1, bf16[64,2048]{1,0:T(8,128)(2,1)} %basis_hbm.1, bf16[16,9,32,128]{3,2,1,0:T(8,128)(2,1)} %transfer_ref.1, bf16[256,512]{1,0:T(8,128)(2,1)} %constant.22.clone.table_hbm.table_ref), custom_call_target="tpu_custom_call" | custom-call | tf_op jit(solution)/shard_map/local/pallas_call | solution.py:274
  2.5 0.6 %collective-permute-start = (f32[8,16,128]{2,1,0:T(8,128)S(1)}, f32[8,16,128]{2,1,0:T(8,128)S(1)}, u32[]{:S(2)}, u32[]{:S(2)}) collective-permute-start(f32[8,16,128]{2,1,0:T(8,128)S(1)} %local.1.own_ref), channel_id=1, source_target_pairs={{0,1},{1,0},{2,3},{3,2},{4,5},{5,4},{6,7},{7,6},{8,9},{9,8},{10,11... | collective-permute-start | bytes 196616 | tf_op jit(solution)/shard_map/swap_0/ppermute | solution.py:319
  3.1 0.0 copy-done.3
  3.1 0.0 copy-done
  3.1 0.5 %matrices.1.matrices_ref = bf16[5,8,128,128]{3,2,1,0:T(8,128)(2,1)S(1)} custom-call(bf16[16,9,32,128]{3,2,1,0:T(8,128)(2,1)S(1)} %copy-done, bf16[256,512]{1,0:T(8,128)(2,1)S(1)} %copy-done.3), custom_call_target="tpu_custom_call" | custom-call | tf_op jit(solution)/shard_map/matrices/pallas_call | solution.py:245
  3.6 0.4 %collective-permute-done.other_ref = f32[8,16,128]{2,1,0:T(8,128)S(1)} collective-permute-done((f32[8,16,128]{2,1,0:T(8,128)S(1)}, f32[8,16,128]{2,1,0:T(8,128)S(1)}, u32[]{:S(2)}, u32[]{:S(2)}) %collective-permute-start) | collective-permute-done | bytes 65568 | tf_op jit(solution)/shard_map/swap_0/ppermute | solution.py:319
  4.0 0.0 copy-start.2
  4.0 0.3 cross_0.1.own_ref
  4.2 2.9 %collective-permute-start.1 = (f32[8,16,128]{2,1,0:T(8,128)S(1)}, f32[8,16,128]{2,1,0:T(8,128)S(1)}, u32[]{:S(2)}, u32[]{:S(2)}) collective-permute-start(f32[8,16,128]{2,1,0:T(8,128)S(1)} %cross_0.1.own_ref), channel_id=1, source_target_pairs={{0,2},{1,3},{2,0},{3,1},{4,6},{5,7},{6,4},{7,5},{8,10},{9,11},{10,... | collective-permute-start | bytes 196616 | tf_op jit(solution)/shard_map/swap_1/ppermute | solution.py:319
  7.1 0.0 copy-start.1
  7.1 0.0 copy-start.5
  7.1 2.4 %collective-permute-done.1.other_ref = f32[8,16,128]{2,1,0:T(8,128)S(1)} collective-permute-done((f32[8,16,128]{2,1,0:T(8,128)S(1)}, f32[8,16,128]{2,1,0:T(8,128)S(1)}, u32[]{:S(2)}, u32[]{:S(2)}) %collective-permute-start.1) | collective-permute-done | bytes 65568 | tf_op jit(solution)/shard_map/swap_1/ppermute | solution.py:319
  9.6 0.3 cross_1.1.own_ref
  9.8 1.9 %collective-permute-start.2 = (f32[8,16,128]{2,1,0:T(8,128)S(1)}, f32[8,16,128]{2,1,0:T(8,128)S(1)}, u32[]{:S(2)}, u32[]{:S(2)}) collective-permute-start(f32[8,16,128]{2,1,0:T(8,128)S(1)} %cross_1.1.own_ref), channel_id=1, source_target_pairs={{0,4},{1,5},{2,6},{3,7},{4,0},{5,1},{6,2},{7,3},{8,12},{9,13},{10,... | collective-permute-start | bytes 196616 | tf_op jit(solution)/shard_map/swap_2/ppermute | solution.py:319
  11.8 0.0 copy-done.2
  11.8 2.9 %collective-permute-start.6 = (bf16[32,1024]{1,0:T(8,128)(2,1)S(1)}, bf16[32,1024]{1,0:T(8,128)(2,1)S(1)}, u32[]{:S(2)}, u32[]{:S(2)}) collective-permute-start(bf16[32,1024]{1,0:T(8,128)(2,1)S(1)} %get-tuple-element.11), channel_id=1, source_target_pairs={{0,31},{1,2},{2,1},{3,4},{4,3},{5,6},{6,5},{7,8},{8,7},{9,10},{10,... | collective-permute-start | bytes 196616 | tf_op jit(solution)/shard_map/halo_ring/ppermute | solution.py:270
  14.6 0.0 collective-permute-start.5
  14.6 0.0 collective-permute-done.2.other_ref
  14.6 0.3 cross_2.1.own_ref
  14.9 1.5 %collective-permute-start.3 = (f32[8,16,128]{2,1,0:T(8,128)S(1)}, f32[8,16,128]{2,1,0:T(8,128)S(1)}, u32[]{:S(2)}, u32[]{:S(2)}) collective-permute-start(f32[8,16,128]{2,1,0:T(8,128)S(1)} %cross_2.1.own_ref), channel_id=1, source_target_pairs={{0,8},{1,9},{2,10},{3,11},{4,12},{5,13},{6,14},{7,15},{8,0},{9,1},... | collective-permute-start | bytes 196616 | tf_op jit(solution)/shard_map/swap_3/ppermute | solution.py:319
  16.4 2.8 %collective-permute-done.6.ring_ref = bf16[32,1024]{1,0:T(8,128)(2,1)S(1)} collective-permute-done((bf16[32,1024]{1,0:T(8,128)(2,1)S(1)}, bf16[32,1024]{1,0:T(8,128)(2,1)S(1)}, u32[]{:S(2)}, u32[]{:S(2)}) %collective-permute-start.6) | collective-permute-done | bytes 65568 | tf_op jit(solution)/shard_map/halo_ring/ppermute | solution.py:270
  19.2 0.0 collective-permute-done.5.pair_ref
  19.2 0.0 copy-done.1
  19.2 0.0 copy-done.5
  19.2 0.0 copy-start.4
  19.2 1.0 %near.1 = (f32[16,32,128]{2,1,0:T(8,128)S(1)}, f32[32,512]{1,0:T(8,128)S(1)}, f32[32,512]{1,0:T(8,128)S(1)}) custom-call(s32[1]{0:T(128)} %bitcast.index_ref, s32[2,24]{1,0:T(2,128)S(1)} %bitcast.2, bf16[32,2048]{1,0:T(8,128)(2,1)S(1)} %copy-done.2, bf16[32,1024]{1,0:T(8,128)(2,1)S(1)} %collective-permute-done.5.pair_ref, ...), custom_call_target="tpu_custom_call" | custom-call | tf_op jit(solution)/shard_map/near/pallas_call | solution.py:245
  20.2 0.1 collective-permute-start.7
  20.3 3.3 %collective-permute-start.8 = (f32[32,512]{1,0:T(8,128)S(1)}, f32[32,512]{1,0:T(8,128)S(1)}, u32[]{:S(2)}, u32[]{:S(2)}) collective-permute-start(f32[32,512]{1,0:T(8,128)S(1)} %get-tuple-element.10), channel_id=1, source_target_pairs={{0,31},{1,2},{2,1},{3,4},{4,3},{5,6},{6,5},{7,8},{8,7},{9,10},{10,... | collective-permute-start | bytes 196616 | tf_op jit(solution)/shard_map/rim_ring/ppermute | solution.py:315
  23.6 0.0 collective-permute-done.3.other_ref
  23.6 0.3 cross_3.1.own_ref
  23.9 0.1 collective-permute-start.4
  24.0 0.0 collective-permute-done.7.pair_ref
  24.0 4.3 %collective-permute-done.8.ring_ref = f32[32,512]{1,0:T(8,128)S(1)} collective-permute-done((f32[32,512]{1,0:T(8,128)S(1)}, f32[32,512]{1,0:T(8,128)S(1)}, u32[]{:S(2)}, u32[]{:S(2)}) %collective-permute-start.8) | collective-permute-done | bytes 65568 | tf_op jit(solution)/shard_map/rim_ring/ppermute | solution.py:315
  28.3 0.8 %collective-permute-done.4.other_ref = f32[8,16,128]{2,1,0:T(8,128)S(1)} collective-permute-done((f32[8,16,128]{2,1,0:T(8,128)S(1)}, f32[8,16,128]{2,1,0:T(8,128)S(1)}, u32[]{:S(2)}, u32[]{:S(2)}) %collective-permute-start.4) | collective-permute-done | bytes 65568 | tf_op jit(solution)/shard_map/swap_4/ppermute | solution.py:319
  29.1 0.0 copy-done.4
  29.1 1.2 %final.1 = f32[32,2048]{1,0:T(8,128)} custom-call(s32[1]{0:T(128)} %bitcast.index_ref, f32[8,16,128]{2,1,0:T(8,128)S(1)} %cross_3.1.own_ref, f32[8,16,128]{2,1,0:T(8,128)S(1)} %collective-permute-done.4.other_ref, bf16[5,8,128,128]{3,2,1,0:T(8,128)(2,1)S(1)} %matrices.1.matrices_ref, bf16[64,2048]{1,0:T(8,128)(2,1)S(1)} %copy-done.4, ...), custom_call_target="tpu_custom_call" | custom-call | tf_op jit(solution)/shard_map/final/pallas_call | solution.py:328
  (1 shorter events, 0.0 us)
Async XLA Ops:
  0.0 3.1 %copy-start.3 = (bf16[256,512]{1,0:T(8,128)(2,1)S(1)}, bf16[256,512]{1,0:T(8,128)(2,1)}, u32[]{:S(2)}) copy-start(bf16[256,512]{1,0:T(8,128)(2,1)} %constant.22.clone.table_hbm.table_ref) | copy-start | bytes 786436
  0.0 3.1 %copy-start = (bf16[16,9,32,128]{3,2,1,0:T(8,128)(2,1)S(1)}, bf16[16,9,32,128]{3,2,1,0:T(8,128)(2,1)}, u32[]{:S(2)}) copy-start(bf16[16,9,32,128]{3,2,1,0:T(8,128)(2,1)} %transfer_ref.1) | copy-start | bytes 3538948
  2.5 1.5 %collective-permute-start = (f32[8,16,128]{2,1,0:T(8,128)S(1)}, f32[8,16,128]{2,1,0:T(8,128)S(1)}, u32[]{:S(2)}, u32[]{:S(2)}) collective-permute-start(f32[8,16,128]{2,1,0:T(8,128)S(1)} %local.1.own_ref), channel_id=1, source_target_pairs={{0,1},{1,0},{2,3},{3,2},{4,5},{5,4},{6,7},{7,6},{8,9},{9,8},{10,11... | collective-permute-start | bytes 196616 | tf_op jit(solution)/shard_map/swap_0/ppermute | solution.py:319
  4.0 7.8 %copy-start.2 = (bf16[32,2048]{1,0:T(8,128)(2,1)S(1)}, bf16[32,2048]{1,0:T(8,128)(2,1)}, u32[]{:S(2)}) copy-start(bf16[32,2048]{1,0:T(8,128)(2,1)} %signal_ref.1) | copy-start | bytes 393220
  4.2 5.3 %collective-permute-start.1 = (f32[8,16,128]{2,1,0:T(8,128)S(1)}, f32[8,16,128]{2,1,0:T(8,128)S(1)}, u32[]{:S(2)}, u32[]{:S(2)}) collective-permute-start(f32[8,16,128]{2,1,0:T(8,128)S(1)} %cross_0.1.own_ref), channel_id=1, source_target_pairs={{0,2},{1,3},{2,0},{3,1},{4,6},{5,7},{6,4},{7,5},{8,10},{9,11},{10,... | collective-permute-start | bytes 196616 | tf_op jit(solution)/shard_map/swap_1/ppermute | solution.py:319
  7.1 12.1 %copy-start.1 = (bf16[24,128,256]{2,1,0:T(8,128)(2,1)S(1)}, bf16[24,128,256]{2,1,0:T(8,128)(2,1)}, u32[]{:S(2)}) copy-start(bf16[24,128,256]{2,1,0:T(8,128)(2,1)} %blocks_ref.1) | copy-start | bytes 4718596
  7.1 12.1 %copy-start.5 = (s32[24,2]{0,1:T(2,128)S(1)}, s32[24,2]{0,1:T(2,128)}, u32[]{:S(2)}) copy-start(s32[24,2]{0,1:T(2,128)} %param.12) | copy-start | bytes 580
  9.8 4.8 %collective-permute-start.2 = (f32[8,16,128]{2,1,0:T(8,128)S(1)}, f32[8,16,128]{2,1,0:T(8,128)S(1)}, u32[]{:S(2)}, u32[]{:S(2)}) collective-permute-start(f32[8,16,128]{2,1,0:T(8,128)S(1)} %cross_1.1.own_ref), channel_id=1, source_target_pairs={{0,4},{1,5},{2,6},{3,7},{4,0},{5,1},{6,2},{7,3},{8,12},{9,13},{10,... | collective-permute-start | bytes 196616 | tf_op jit(solution)/shard_map/swap_2/ppermute | solution.py:319
  11.8 7.5 %collective-permute-start.6 = (bf16[32,1024]{1,0:T(8,128)(2,1)S(1)}, bf16[32,1024]{1,0:T(8,128)(2,1)S(1)}, u32[]{:S(2)}, u32[]{:S(2)}) collective-permute-start(bf16[32,1024]{1,0:T(8,128)(2,1)S(1)} %get-tuple-element.11), channel_id=1, source_target_pairs={{0,31},{1,2},{2,1},{3,4},{4,3},{5,6},{6,5},{7,8},{8,7},{9,10},{10,... | collective-permute-start | bytes 196616 | tf_op jit(solution)/shard_map/halo_ring/ppermute | solution.py:270
  14.6 4.6 %collective-permute-start.5 = (bf16[32,1024]{1,0:T(8,128)(2,1)S(1)}, bf16[32,1024]{1,0:T(8,128)(2,1)S(1)}, u32[]{:S(2)}, u32[]{:S(2)}) collective-permute-start(bf16[32,1024]{1,0:T(8,128)(2,1)S(1)} %get-tuple-element.12), channel_id=1, source_target_pairs={{0,1},{1,0},{2,3},{3,2},{4,5},{5,4},{6,7},{7,6},{8,9},{9,8},{10,11... | collective-permute-start | bytes 196616 | tf_op jit(solution)/shard_map/halo_pair/ppermute | solution.py:268
  14.9 8.7 %collective-permute-start.3 = (f32[8,16,128]{2,1,0:T(8,128)S(1)}, f32[8,16,128]{2,1,0:T(8,128)S(1)}, u32[]{:S(2)}, u32[]{:S(2)}) collective-permute-start(f32[8,16,128]{2,1,0:T(8,128)S(1)} %cross_2.1.own_ref), channel_id=1, source_target_pairs={{0,8},{1,9},{2,10},{3,11},{4,12},{5,13},{6,14},{7,15},{8,0},{9,1},... | collective-permute-start | bytes 196616 | tf_op jit(solution)/shard_map/swap_3/ppermute | solution.py:319
  19.2 9.9 %copy-start.4 = (bf16[64,2048]{1,0:T(8,128)(2,1)S(1)}, bf16[64,2048]{1,0:T(8,128)(2,1)}, u32[]{:S(2)}) copy-start(bf16[64,2048]{1,0:T(8,128)(2,1)} %basis_ref.1) | copy-start | bytes 786436
  20.2 3.7 %collective-permute-start.7 = (f32[32,512]{1,0:T(8,128)S(1)}, f32[32,512]{1,0:T(8,128)S(1)}, u32[]{:S(2)}, u32[]{:S(2)}) collective-permute-start(f32[32,512]{1,0:T(8,128)S(1)} %get-tuple-element.9), channel_id=1, source_target_pairs={{0,1},{1,0},{2,3},{3,2},{4,5},{5,4},{6,7},{7,6},{8,9},{9,8},{10,11... | collective-permute-start | bytes 196616 | tf_op jit(solution)/shard_map/rim_pair/ppermute | solution.py:313
  20.3 8.0 %collective-permute-start.8 = (f32[32,512]{1,0:T(8,128)S(1)}, f32[32,512]{1,0:T(8,128)S(1)}, u32[]{:S(2)}, u32[]{:S(2)}) collective-permute-start(f32[32,512]{1,0:T(8,128)S(1)} %get-tuple-element.10), channel_id=1, source_target_pairs={{0,31},{1,2},{2,1},{3,4},{4,3},{5,6},{6,5},{7,8},{8,7},{9,10},{10,... | collective-permute-start | bytes 196616 | tf_op jit(solution)/shard_map/rim_ring/ppermute | solution.py:315
  23.9 5.2 %collective-permute-start.4 = (f32[8,16,128]{2,1,0:T(8,128)S(1)}, f32[8,16,128]{2,1,0:T(8,128)S(1)}, u32[]{:S(2)}, u32[]{:S(2)}) collective-permute-start(f32[8,16,128]{2,1,0:T(8,128)S(1)} %cross_3.1.own_ref), channel_id=1, source_target_pairs={{0,16},{1,17},{2,18},{3,19},{4,20},{5,21},{6,22},{7,23},{8,24},{9,... | collective-permute-start | bytes 196616 | tf_op jit(solution)/shard_map/swap_4/ppermute | solution.py:319

commit v4 on v3

--- a/solution.py
+++ b/solution.py
@@ -7,6 +7,7 @@
 from jax.experimental import pallas as pl
 from jax.experimental.pallas import tpu as pltpu
 from jax.sharding import PartitionSpec as P
+
 
 LEAF = 128
 AXES = ("leaf", "sub")
@@ -230,7 +231,7 @@
 SMEM = pl.BlockSpec(memory_space=pltpu.SMEM)
 
 
-def on_chip(kernel, name, outs, scalars, arrays, scratch=(), grant=16 << 20):
+def on_chip(kernel, outs, scalars, arrays, scratch=(), grant=16 << 20):
     single = len(outs) == 2 and not isinstance(outs[1], tuple)
     shapes = tuple(pltpu.VMEM(shape, kind) for shape, kind in ((outs,) if single else outs))
     call = pl.pallas_call(
@@ -240,7 +241,6 @@
         out_specs=VMEM if single else (VMEM,) * len(shapes),
         scratch_shapes=list(scratch),
         compiler_params=pltpu.CompilerParams(vmem_limit_bytes=grant),
-        name=name,
     )
     return call(*scalars, *[pltpu.with_memory_space_constraint(x, pltpu.VMEM) for x in arrays])
 
@@ -264,10 +264,8 @@
     far_end = signal.shape[1] - halo
     to_pair = lax.dynamic_slice_in_dim(signal, jnp.where(odd == 1, 0, far_end), halo, 1)
     to_ring = lax.dynamic_slice_in_dim(signal, jnp.where(odd == 1, far_end, 0), halo, 1)
-    with jax.named_scope("halo_pair"):
-        from_pair = lax.ppermute(to_pair, AXES, pairs)
-    with jax.named_scope("halo_ring"):
-        from_ring = lax.ppermute(to_ring, AXES, ring)
+    from_pair = lax.ppermute(to_pair, AXES, pairs)
+    from_ring = lax.ppermute(to_ring, AXES, ring)
 
     table = jnp.asarray(form_table(rank), BF16)
     state = ((half, rhs, width), F32)
@@ -289,14 +287,12 @@
     cross_levels = levels - local_levels
     matrices = on_chip(
         functools.partial(matrices_kernel, first_level=local_levels),
-        "matrices",
         ((cross_levels, half, width, width), BF16),
         (),
         (transfer, table),
     )
     center, rim_pair, rim_ring = on_chip(
         near_kernel,
-        "near",
         (
             ((boxes, channels, LEAF), F32),
             ((channels, reach * LEAF), F32),
@@ -309,21 +305,14 @@
             pltpu.VMEM((boxes + 2 * reach + 1, channels, LEAF), F32),
         ),
     )
-    with jax.named_scope("rim_pair"):
-        rim_from_pair = lax.ppermute(rim_pair, AXES, pairs)
-    with jax.named_scope("rim_ring"):
-        rim_from_ring = lax.ppermute(rim_ring, AXES, ring)
+    rim_from_pair = lax.ppermute(rim_pair, AXES, pairs)
+    rim_from_ring = lax.ppermute(rim_ring, AXES, ring)
 
     for level in range(cross_levels):
-        with jax.named_scope(f"swap_{level}"):
-            other = lax.ppermute(coeffs, AXES, [(i, i ^ 1 << level) for i in range(devices)])
+        other = lax.ppermute(coeffs, AXES, [(i, i ^ 1 << level) for i in range(devices)])
         if level + 1 < cross_levels:
             coeffs = on_chip(
-                functools.partial(cross_kernel, level=level),
-                f"cross_{level}",
-                state,
-                (index_word,),
-                (coeffs, other, matrices),
+                functools.partial(cross_kernel, level=level), state, (index_word,), (coeffs, other, matrices)
             )
     return pl.pallas_call(
         functools.partial(final_kernel, level=cross_levels - 1),

time: 30.4 us -> 30.4 us (level)
  no operation moved by 1% of the time
where the time goes in v4:
time: 30.4 us; the launch traced here: 30.3 us
  starting transfers between devices  13.2 us (43%)
  waiting for transfers between devices  10.8 us (36%)
  Pallas kernels  6.18 us (20%)
    ppermute x5, starting transfers between devices, shards(): lax.ppermute(coeffs, AXES, [(i, i ^ 1 << level) for i in range(devices)])  6.96 us
    ppermute x1, waiting for transfers between devices, shards(): rim_from_ring = lax.ppermute(rim_ring, AXES, ring)  4.33 us
    ppermute x5, waiting for transfers between devices, shards(): lax.ppermute(coeffs, AXES, [(i, i ^ 1 << level) for i in range(devices)])  3.61 us
    ppermute x1, starting transfers between devices, shards(): rim_from_ring = lax.ppermute(rim_ring, AXES, ring)  3.3 us
    ppermute x1, starting transfers between devices, shards(): from_ring = lax.ppermute(to_ring, AXES, ring)  2.86 us
    ppermute x1, waiting for transfers between devices, shards(): from_ring = lax.ppermute(to_ring, AXES, ring)  2.83 us
    pallas_call x1, Pallas kernels, shards(): pl.pallas_call(local_kernel, out_shape=pltpu.VMEM(*state), in_specs=[pl.B...  2.5 us
    pallas_call x6, Pallas kernels, on_chip(): call(*scalars, *[pltpu.with_memory_space_constraint(x, pltpu.VMEM) for x...  2.49 us
  transfers between devices with their start and end apart: 9, of which 5 were waited for; matrix products, arithmetic and copies ran while one was open for 0% of the time, Pallas kernels for 7%

profile of v4, /device:TPU:0, one launch (start us, length us, event | category | flops | bytes accessed | tf_op | source)
XLA Modules:
  0.0 30.3 jit_solution(12550462019034452613)
XLA Ops:
  0.0 0.0 copy-start.3
  0.0 0.0 copy-start
  0.0 2.5 %local.1.own_ref = f32[8,16,128]{2,1,0:T(8,128)S(1)} custom-call(bf16[32,2048]{1,0:T(8,128)(2,1)} %signal_ref.1, bf16[64,2048]{1,0:T(8,128)(2,1)} %basis_hbm.1, bf16[16,9,32,128]{3,2,1,0:T(8,128)(2,1)} %transfer_ref.1, bf16[256,512]{1,0:T(8,128)(2,1)} %constant.22.clone.table_hbm.table_ref), custom_call_target="tpu_custom_call" | custom-call | tf_op jit(solution)/shard_map/local/pallas_call | solution.py:272
  2.5 0.6 %collective-permute-start = (f32[8,16,128]{2,1,0:T(8,128)S(1)}, f32[8,16,128]{2,1,0:T(8,128)S(1)}, u32[]{:S(2)}, u32[]{:S(2)}) collective-permute-start(f32[8,16,128]{2,1,0:T(8,128)S(1)} %local.1.own_ref), channel_id=1, source_target_pairs={{0,1},{1,0},{2,3},{3,2},{4,5},{5,4},{6,7},{7,6},{8,9},{9,8},{10,11... | collective-permute-start | bytes 196616 | tf_op jit(solution)/shard_map/ppermute | solution.py:312
  3.1 0.0 copy-done.3
  3.1 0.0 copy-done
  3.1 0.5 %shard_map.73.matrices_ref = bf16[5,8,128,128]{3,2,1,0:T(8,128)(2,1)S(1)} custom-call(bf16[16,9,32,128]{3,2,1,0:T(8,128)(2,1)S(1)} %copy-done, bf16[256,512]{1,0:T(8,128)(2,1)S(1)} %copy-done.3), custom_call_target="tpu_custom_call" | custom-call | tf_op jit(solution)/shard_map/pallas_call | solution.py:245
  3.6 0.4 %collective-permute-done.other_ref = f32[8,16,128]{2,1,0:T(8,128)S(1)} collective-permute-done((f32[8,16,128]{2,1,0:T(8,128)S(1)}, f32[8,16,128]{2,1,0:T(8,128)S(1)}, u32[]{:S(2)}, u32[]{:S(2)}) %collective-permute-start) | collective-permute-done | bytes 65568 | tf_op jit(solution)/shard_map/ppermute | solution.py:312
  4.0 0.0 copy-start.2
  4.0 0.3 shard_map.74.own_ref
  4.2 2.9 %collective-permute-start.1 = (f32[8,16,128]{2,1,0:T(8,128)S(1)}, f32[8,16,128]{2,1,0:T(8,128)S(1)}, u32[]{:S(2)}, u32[]{:S(2)}) collective-permute-start(f32[8,16,128]{2,1,0:T(8,128)S(1)} %shard_map.74.own_ref), channel_id=1, source_target_pairs={{0,2},{1,3},{2,0},{3,1},{4,6},{5,7},{6,4},{7,5},{8,10},{9,11},{10,... | collective-permute-start | bytes 196616 | tf_op jit(solution)/shard_map/ppermute | solution.py:312
  7.1 0.0 copy-start.1
  7.1 0.0 copy-start.5
  7.1 2.4 %collective-permute-done.1.other_ref = f32[8,16,128]{2,1,0:T(8,128)S(1)} collective-permute-done((f32[8,16,128]{2,1,0:T(8,128)S(1)}, f32[8,16,128]{2,1,0:T(8,128)S(1)}, u32[]{:S(2)}, u32[]{:S(2)}) %collective-permute-start.1) | collective-permute-done | bytes 65568 | tf_op jit(solution)/shard_map/ppermute | solution.py:312
  9.6 0.3 shard_map.75.own_ref
  9.8 1.9 %collective-permute-start.2 = (f32[8,16,128]{2,1,0:T(8,128)S(1)}, f32[8,16,128]{2,1,0:T(8,128)S(1)}, u32[]{:S(2)}, u32[]{:S(2)}) collective-permute-start(f32[8,16,128]{2,1,0:T(8,128)S(1)} %shard_map.75.own_ref), channel_id=1, source_target_pairs={{0,4},{1,5},{2,6},{3,7},{4,0},{5,1},{6,2},{7,3},{8,12},{9,13},{10,... | collective-permute-start | bytes 196616 | tf_op jit(solution)/shard_map/ppermute | solution.py:312
  11.8 0.0 copy-done.2
  11.8 2.9 %collective-permute-start.6 = (bf16[32,1024]{1,0:T(8,128)(2,1)S(1)}, bf16[32,1024]{1,0:T(8,128)(2,1)S(1)}, u32[]{:S(2)}, u32[]{:S(2)}) collective-permute-start(bf16[32,1024]{1,0:T(8,128)(2,1)S(1)} %get-tuple-element.11), channel_id=1, source_target_pairs={{0,31},{1,2},{2,1},{3,4},{4,3},{5,6},{6,5},{7,8},{8,7},{9,10},{10,... | collective-permute-start | bytes 196616 | tf_op jit(solution)/shard_map/ppermute | solution.py:268
  14.6 0.0 collective-permute-start.5
  14.6 0.0 collective-permute-done.2.other_ref
  14.6 0.3 shard_map.76.own_ref
  14.9 1.5 %collective-permute-start.3 = (f32[8,16,128]{2,1,0:T(8,128)S(1)}, f32[8,16,128]{2,1,0:T(8,128)S(1)}, u32[]{:S(2)}, u32[]{:S(2)}) collective-permute-start(f32[8,16,128]{2,1,0:T(8,128)S(1)} %shard_map.76.own_ref), channel_id=1, source_target_pairs={{0,8},{1,9},{2,10},{3,11},{4,12},{5,13},{6,14},{7,15},{8,0},{9,1},... | collective-permute-start | bytes 196616 | tf_op jit(solution)/shard_map/ppermute | solution.py:312
  16.4 2.8 %collective-permute-done.6.ring_ref = bf16[32,1024]{1,0:T(8,128)(2,1)S(1)} collective-permute-done((bf16[32,1024]{1,0:T(8,128)(2,1)S(1)}, bf16[32,1024]{1,0:T(8,128)(2,1)S(1)}, u32[]{:S(2)}, u32[]{:S(2)}) %collective-permute-start.6) | collective-permute-done | bytes 65568 | tf_op jit(solution)/shard_map/ppermute | solution.py:268
  19.2 0.0 collective-permute-done.5.pair_ref
  19.2 0.0 copy-done.1
  19.2 0.0 copy-done.5
  19.2 0.0 copy-start.4
  19.2 1.0 %shard_map.78 = (f32[16,32,128]{2,1,0:T(8,128)S(1)}, f32[32,512]{1,0:T(8,128)S(1)}, f32[32,512]{1,0:T(8,128)S(1)}) custom-call(s32[1]{0:T(128)} %bitcast.index_ref, s32[2,24]{1,0:T(2,128)S(1)} %bitcast.2, bf16[32,2048]{1,0:T(8,128)(2,1)S(1)} %copy-done.2, bf16[32,1024]{1,0:T(8,128)(2,1)S(1)} %collective-permute-done.5.pair_ref, ...), custom_call_target="tpu_custom_call" | custom-call | tf_op jit(solution)/shard_map/pallas_call | solution.py:245
  20.2 0.1 collective-permute-start.7
  20.3 3.3 %collective-permute-start.8 = (f32[32,512]{1,0:T(8,128)S(1)}, f32[32,512]{1,0:T(8,128)S(1)}, u32[]{:S(2)}, u32[]{:S(2)}) collective-permute-start(f32[32,512]{1,0:T(8,128)S(1)} %get-tuple-element.10), channel_id=1, source_target_pairs={{0,31},{1,2},{2,1},{3,4},{4,3},{5,6},{6,5},{7,8},{8,7},{9,10},{10,... | collective-permute-start | bytes 196616 | tf_op jit(solution)/shard_map/ppermute | solution.py:309
  23.6 0.0 collective-permute-done.3.other_ref
  23.6 0.3 shard_map.77.own_ref
  23.9 0.1 collective-permute-start.4
  24.0 0.0 collective-permute-done.7.pair_ref
  24.0 4.3 %collective-permute-done.8.ring_ref = f32[32,512]{1,0:T(8,128)S(1)} collective-permute-done((f32[32,512]{1,0:T(8,128)S(1)}, f32[32,512]{1,0:T(8,128)S(1)}, u32[]{:S(2)}, u32[]{:S(2)}) %collective-permute-start.8) | collective-permute-done | bytes 65568 | tf_op jit(solution)/shard_map/ppermute | solution.py:309
  28.3 0.8 %collective-permute-done.4.other_ref = f32[8,16,128]{2,1,0:T(8,128)S(1)} collective-permute-done((f32[8,16,128]{2,1,0:T(8,128)S(1)}, f32[8,16,128]{2,1,0:T(8,128)S(1)}, u32[]{:S(2)}, u32[]{:S(2)}) %collective-permute-start.4) | collective-permute-done | bytes 65568 | tf_op jit(solution)/shard_map/ppermute | solution.py:312
  29.1 0.0 copy-done.4
  29.1 1.2 %final.1 = f32[32,2048]{1,0:T(8,128)} custom-call(s32[1]{0:T(128)} %bitcast.index_ref, f32[8,16,128]{2,1,0:T(8,128)S(1)} %shard_map.77.own_ref, f32[8,16,128]{2,1,0:T(8,128)S(1)} %collective-permute-done.4.other_ref, bf16[5,8,128,128]{3,2,1,0:T(8,128)(2,1)S(1)} %shard_map.73.matrices_ref, bf16[64,2048]{1,0:T(8,128)(2,1)S(1)} %copy-done.4, ...), custom_call_target="tpu_custom_call" | custom-call | tf_op jit(solution)/shard_map/final/pallas_call | solution.py:317
  (1 shorter events, 0.0 us)
Async XLA Ops:
  0.0 3.1 %copy-start.3 = (bf16[256,512]{1,0:T(8,128)(2,1)S(1)}, bf16[256,512]{1,0:T(8,128)(2,1)}, u32[]{:S(2)}) copy-start(bf16[256,512]{1,0:T(8,128)(2,1)} %constant.22.clone.table_hbm.table_ref) | copy-start | bytes 786436
  0.0 3.1 %copy-start = (bf16[16,9,32,128]{3,2,1,0:T(8,128)(2,1)S(1)}, bf16[16,9,32,128]{3,2,1,0:T(8,128)(2,1)}, u32[]{:S(2)}) copy-start(bf16[16,9,32,128]{3,2,1,0:T(8,128)(2,1)} %transfer_ref.1) | copy-start | bytes 3538948
  2.5 1.5 %collective-permute-start = (f32[8,16,128]{2,1,0:T(8,128)S(1)}, f32[8,16,128]{2,1,0:T(8,128)S(1)}, u32[]{:S(2)}, u32[]{:S(2)}) collective-permute-start(f32[8,16,128]{2,1,0:T(8,128)S(1)} %local.1.own_ref), channel_id=1, source_target_pairs={{0,1},{1,0},{2,3},{3,2},{4,5},{5,4},{6,7},{7,6},{8,9},{9,8},{10,11... | collective-permute-start | bytes 196616 | tf_op jit(solution)/shard_map/ppermute | solution.py:312
  4.0 7.8 %copy-start.2 = (bf16[32,2048]{1,0:T(8,128)(2,1)S(1)}, bf16[32,2048]{1,0:T(8,128)(2,1)}, u32[]{:S(2)}) copy-start(bf16[32,2048]{1,0:T(8,128)(2,1)} %signal_ref.1) | copy-start | bytes 393220
  4.2 5.3 %collective-permute-start.1 = (f32[8,16,128]{2,1,0:T(8,128)S(1)}, f32[8,16,128]{2,1,0:T(8,128)S(1)}, u32[]{:S(2)}, u32[]{:S(2)}) collective-permute-start(f32[8,16,128]{2,1,0:T(8,128)S(1)} %shard_map.74.own_ref), channel_id=1, source_target_pairs={{0,2},{1,3},{2,0},{3,1},{4,6},{5,7},{6,4},{7,5},{8,10},{9,11},{10,... | collective-permute-start | bytes 196616 | tf_op jit(solution)/shard_map/ppermute | solution.py:312
  7.1 12.1 %copy-start.1 = (bf16[24,128,256]{2,1,0:T(8,128)(2,1)S(1)}, bf16[24,128,256]{2,1,0:T(8,128)(2,1)}, u32[]{:S(2)}) copy-start(bf16[24,128,256]{2,1,0:T(8,128)(2,1)} %blocks_ref.1) | copy-start | bytes 4718596
  7.1 12.1 %copy-start.5 = (s32[24,2]{0,1:T(2,128)S(1)}, s32[24,2]{0,1:T(2,128)}, u32[]{:S(2)}) copy-start(s32[24,2]{0,1:T(2,128)} %param.12) | copy-start | bytes 580
  9.8 4.8 %collective-permute-start.2 = (f32[8,16,128]{2,1,0:T(8,128)S(1)}, f32[8,16,128]{2,1,0:T(8,128)S(1)}, u32[]{:S(2)}, u32[]{:S(2)}) collective-permute-start(f32[8,16,128]{2,1,0:T(8,128)S(1)} %shard_map.75.own_ref), channel_id=1, source_target_pairs={{0,4},{1,5},{2,6},{3,7},{4,0},{5,1},{6,2},{7,3},{8,12},{9,13},{10,... | collective-permute-start | bytes 196616 | tf_op jit(solution)/shard_map/ppermute | solution.py:312
  11.8 7.5 %collective-permute-start.6 = (bf16[32,1024]{1,0:T(8,128)(2,1)S(1)}, bf16[32,1024]{1,0:T(8,128)(2,1)S(1)}, u32[]{:S(2)}, u32[]{:S(2)}) collective-permute-start(bf16[32,1024]{1,0:T(8,128)(2,1)S(1)} %get-tuple-element.11), channel_id=1, source_target_pairs={{0,31},{1,2},{2,1},{3,4},{4,3},{5,6},{6,5},{7,8},{8,7},{9,10},{10,... | collective-permute-start | bytes 196616 | tf_op jit(solution)/shard_map/ppermute | solution.py:268
  14.6 4.6 %collective-permute-start.5 = (bf16[32,1024]{1,0:T(8,128)(2,1)S(1)}, bf16[32,1024]{1,0:T(8,128)(2,1)S(1)}, u32[]{:S(2)}, u32[]{:S(2)}) collective-permute-start(bf16[32,1024]{1,0:T(8,128)(2,1)S(1)} %get-tuple-element.12), channel_id=1, source_target_pairs={{0,1},{1,0},{2,3},{3,2},{4,5},{5,4},{6,7},{7,6},{8,9},{9,8},{10,11... | collective-permute-start | bytes 196616 | tf_op jit(solution)/shard_map/ppermute | solution.py:267
  14.9 8.7 %collective-permute-start.3 = (f32[8,16,128]{2,1,0:T(8,128)S(1)}, f32[8,16,128]{2,1,0:T(8,128)S(1)}, u32[]{:S(2)}, u32[]{:S(2)}) collective-permute-start(f32[8,16,128]{2,1,0:T(8,128)S(1)} %shard_map.76.own_ref), channel_id=1, source_target_pairs={{0,8},{1,9},{2,10},{3,11},{4,12},{5,13},{6,14},{7,15},{8,0},{9,1},... | collective-permute-start | bytes 196616 | tf_op jit(solution)/shard_map/ppermute | solution.py:312
  19.2 9.9 %copy-start.4 = (bf16[64,2048]{1,0:T(8,128)(2,1)S(1)}, bf16[64,2048]{1,0:T(8,128)(2,1)}, u32[]{:S(2)}) copy-start(bf16[64,2048]{1,0:T(8,128)(2,1)} %basis_ref.1) | copy-start | bytes 786436
  20.2 3.7 %collective-permute-start.7 = (f32[32,512]{1,0:T(8,128)S(1)}, f32[32,512]{1,0:T(8,128)S(1)}, u32[]{:S(2)}, u32[]{:S(2)}) collective-permute-start(f32[32,512]{1,0:T(8,128)S(1)} %get-tuple-element.9), channel_id=1, source_target_pairs={{0,1},{1,0},{2,3},{3,2},{4,5},{5,4},{6,7},{7,6},{8,9},{9,8},{10,11... | collective-permute-start | bytes 196616 | tf_op jit(solution)/shard_map/ppermute | solution.py:308
  20.3 8.0 %collective-permute-start.8 = (f32[32,512]{1,0:T(8,128)S(1)}, f32[32,512]{1,0:T(8,128)S(1)}, u32[]{:S(2)}, u32[]{:S(2)}) collective-permute-start(f32[32,512]{1,0:T(8,128)S(1)} %get-tuple-element.10), channel_id=1, source_target_pairs={{0,31},{1,2},{2,1},{3,4},{4,3},{5,6},{6,5},{7,8},{8,7},{9,10},{10,... | collective-permute-start | bytes 196616 | tf_op jit(solution)/shard_map/ppermute | solution.py:309
  23.9 5.2 %collective-permute-start.4 = (f32[8,16,128]{2,1,0:T(8,128)S(1)}, f32[8,16,128]{2,1,0:T(8,128)S(1)}, u32[]{:S(2)}, u32[]{:S(2)}) collective-permute-start(f32[8,16,128]{2,1,0:T(8,128)S(1)} %shard_map.77.own_ref), channel_id=1, source_target_pairs={{0,16},{1,17},{2,18},{3,19},{4,20},{5,21},{6,22},{7,23},{8,24},{9,... | collective-permute-start | bytes 196616 | tf_op jit(solution)/shard_map/ppermute | solution.py:312

commit v5 on v4

--- a/solution.py
+++ b/solution.py
@@ -138,16 +138,35 @@
             out_ref[level, box] = matrices[box]
 
 
-def crossed(own_ref, other_ref, matrices_ref, level, upper, box):
-    own = own_ref[box]
-    other = other_ref[box]
+CODE_STEPS = 256.0
+CODE_MAX = 32767.0
+
+
+def encode(parts):
+    peak = jnp.abs(parts[0])
+    for part in parts[1:]:
+        peak = jnp.maximum(peak, jnp.abs(part))
+    peak = jnp.maximum(jnp.max(peak, axis=1, keepdims=True), 1e-30)
+    code = jnp.ceil(jnp.log2(peak) * CODE_STEPS) + 1.0
+    gain = jnp.exp2(code * (-1.0 / CODE_STEPS)) * CODE_MAX
+    coded = [jnp.round(part * gain) for part in parts] + [jnp.broadcast_to(code, parts[0].shape)]
+    return [part.astype(jnp.int32).astype(jnp.int16) for part in coded]
+
+
+def decode(ref):
+    last = ref.shape[0] - 1
+    gain = jnp.exp2(ref[last].astype(jnp.int32).astype(F32) * (1.0 / CODE_STEPS)) * (1.0 / CODE_MAX)
+    return lambda box: ref[box].astype(jnp.int32).astype(F32) * gain
+
+
+def crossed(own, other, matrix, upper):
     rhs = own.shape[0]
     low = jnp.where(upper, other, own)
     high = jnp.where(upper, own, other)
     first = pick_low(low, half_roll(high))
     second = pick_low(half_roll(low), high)
     rows = jnp.concatenate(split_rows(first) + split_rows(second), axis=0)
-    out = dot(rows, matrices_ref[level, box])
+    out = dot(rows, matrix)
     return pick_low(out[:rhs] + out[rhs : 2 * rhs], out[2 * rhs : 3 * rhs] + out[3 * rhs :])
 
 
@@ -155,10 +174,15 @@
     return lax.axis_index("leaf") * lax.axis_size("sub") + lax.axis_index("sub")
 
 
-def cross_kernel(index_ref, own_ref, other_ref, matrices_ref, out_ref, *, level):
+def cross_kernel(index_ref, own_ref, other_ref, matrices_ref, out_ref, code_ref, *, level):
     upper = (index_ref[0] >> level & 1) == 1
-    for box in range(own_ref.shape[0]):
-        out_ref[box] = crossed(own_ref, other_ref, matrices_ref, level, upper, box)
+    half = own_ref.shape[0]
+    other = decode(other_ref) if level else lambda box: other_ref[box]
+    outs = [crossed(own_ref[box], other(box), matrices_ref[level, box], upper) for box in range(half)]
+    for box, part in enumerate(encode(outs)):
+        code_ref[box] = part
+    for box, part in enumerate(outs):
+        out_ref[box] = part
 
 
 def final_kernel(
@@ -169,8 +193,9 @@
     half, rhs, width = own_ref.shape
     rank = width // 4
     edge = pair_ref.shape[1] // LEAF
+    other = decode(other_ref)
     for box in range(half):
-        pair = crossed(own_ref, other_ref, matrices_ref, level, upper, box)
+        pair = crossed(own_ref[box], other(box), matrices_ref[level, box], upper)
         is_low = lanes_like(pair) < width // 2
         rows = []
         for part in (jnp.where(is_low, pair, 0.0), jnp.where(is_low, 0.0, pair)):
@@ -308,11 +333,15 @@
     rim_from_pair = lax.ppermute(rim_pair, AXES, pairs)
     rim_from_ring = lax.ppermute(rim_ring, AXES, ring)
 
+    sent = coeffs
     for level in range(cross_levels):
-        other = lax.ppermute(coeffs, AXES, [(i, i ^ 1 << level) for i in range(devices)])
+        other = lax.ppermute(sent, AXES, [(i, i ^ 1 << level) for i in range(devices)])
         if level + 1 < cross_levels:
-            coeffs = on_chip(
-                functools.partial(cross_kernel, level=level), state, (index_word,), (coeffs, other, matrices)
+            coeffs, sent = on_chip(
+                functools.partial(cross_kernel, level=level),
+                (state, ((half + 1, rhs, width), jnp.int16)),
+                (index_word,),
+                (coeffs, other, matrices),
             )
     return pl.pallas_call(
         functools.partial(final_kernel, level=cross_levels - 1),

time: 30.4 us -> 28.7 us (0.944)
  waiting for transfers between devices: 10.8 us -> 9.16 us
  starting transfers between devices: 13.2 us -> 12.6 us
  Pallas kernels: 6.18 us -> 6.68 us
    ppermute x5, waiting for transfers between devices: 3.61 us -> 7.02 us  [shards(): lax.ppermute(sent, AXES, [(i, i ^ 1 << level) for i in range(devices)])]
    ppermute x5, starting transfers between devices: 6.96 us -> 3.67 us  [shards(): lax.ppermute(sent, AXES, [(i, i ^ 1 << level) for i in range(devices)])]
    ppermute x1, waiting for transfers between devices: 2.83 us -> 0.01 us  [shards(): from_ring = lax.ppermute(to_ring, AXES, ring)]
    ppermute x1, waiting for transfers between devices: 4.33 us -> 2.13 us  [shards(): rim_from_ring = lax.ppermute(rim_ring, AXES, ring)]
    ppermute x1, starting transfers between devices: 3.3 us -> 4.74 us  [shards(): rim_from_ring = lax.ppermute(rim_ring, AXES, ring)]
    ppermute x1, starting transfers between devices: 2.86 us -> 4.07 us  [shards(): from_ring = lax.ppermute(to_ring, AXES, ring)]
    pallas_call x6, Pallas kernels: 2.49 us -> 2.97 us  [on_chip(): call(*scalars, *[pltpu.with_memory_space_constraint(x, pltpu.VMEM) for x...]
  transfers between devices with their start and end apart: 9 -> 9, of which waited for: 5 -> 4; matrix products, arithmetic and copies ran while one was open for 0% -> 0% of each run, Pallas kernels for 7% -> 9%
where the time goes in v5:
time: 28.7 us; the launch traced here: 28.6 us
  starting transfers between devices  12.6 us (44%)
  waiting for transfers between devices  9.16 us (32%)
  Pallas kernels  6.68 us (23%)
    ppermute x5, waiting for transfers between devices, shards(): lax.ppermute(sent, AXES, [(i, i ^ 1 << level) for i in range(devices)])  7.02 us
    ppermute x1, starting transfers between devices, shards(): rim_from_ring = lax.ppermute(rim_ring, AXES, ring)  4.74 us
    ppermute x1, starting transfers between devices, shards(): from_ring = lax.ppermute(to_ring, AXES, ring)  4.07 us
    ppermute x5, starting transfers between devices, shards(): lax.ppermute(sent, AXES, [(i, i ^ 1 << level) for i in range(devices)])  3.67 us
    pallas_call x6, Pallas kernels, on_chip(): call(*scalars, *[pltpu.with_memory_space_constraint(x, pltpu.VMEM) for x...  2.97 us
    pallas_call x1, Pallas kernels, shards(): pl.pallas_call(local_kernel, out_shape=pltpu.VMEM(*state), in_specs=[pl.B...  2.5 us
    ppermute x1, waiting for transfers between devices, shards(): rim_from_ring = lax.ppermute(rim_ring, AXES, ring)  2.13 us
    pallas_call x1, Pallas kernels, shards(): pl.pallas_call(functools.partial(final_kernel, level=cross_levels - 1), o...  1.21 us
  transfers between devices with their start and end apart: 9, of which 4 were waited for; matrix products, arithmetic and copies ran while one was open for 0% of the time, Pallas kernels for 9%

profile of v5, /device:TPU:0, one launch (start us, length us, event | category | flops | bytes accessed | tf_op | source)
XLA Modules:
  0.0 28.6 jit_solution(6907850033228962679)
XLA Ops:
  0.0 0.0 copy-start.3
  0.0 0.0 copy-start
  0.0 2.5 %local.1.own_ref = f32[8,16,128]{2,1,0:T(8,128)S(1)} custom-call(bf16[32,2048]{1,0:T(8,128)(2,1)} %signal_ref.1, bf16[64,2048]{1,0:T(8,128)(2,1)} %basis_hbm.1, bf16[16,9,32,128]{3,2,1,0:T(8,128)(2,1)} %transfer_ref.1, bf16[256,512]{1,0:T(8,128)(2,1)} %constant.22.clone.table_hbm.table_ref), custom_call_target="tpu_custom_call" | custom-call | tf_op jit(solution)/shard_map/local/pallas_call | solution.py:297
  2.5 0.6 %collective-permute-start = (f32[8,16,128]{2,1,0:T(8,128)S(1)}, f32[8,16,128]{2,1,0:T(8,128)S(1)}, u32[]{:S(2)}, u32[]{:S(2)}) collective-permute-start(f32[8,16,128]{2,1,0:T(8,128)S(1)} %local.1.own_ref), channel_id=1, source_target_pairs={{0,1},{1,0},{2,3},{3,2},{4,5},{5,4},{6,7},{7,6},{8,9},{9,8},{10,11... | collective-permute-start | bytes 196616 | tf_op jit(solution)/shard_map/ppermute | solution.py:338
  3.1 0.0 copy-done.3
  3.1 0.0 copy-done
  3.1 0.5 %shard_map.73.matrices_ref = bf16[5,8,128,128]{3,2,1,0:T(8,128)(2,1)S(1)} custom-call(bf16[16,9,32,128]{3,2,1,0:T(8,128)(2,1)S(1)} %copy-done, bf16[256,512]{1,0:T(8,128)(2,1)S(1)} %copy-done.3), custom_call_target="tpu_custom_call" | custom-call | tf_op jit(solution)/shard_map/pallas_call | solution.py:270
  3.6 0.0 copy-start.2
  3.6 0.4 %collective-permute-done.other_ref = f32[8,16,128]{2,1,0:T(8,128)S(1)} collective-permute-done((f32[8,16,128]{2,1,0:T(8,128)S(1)}, f32[8,16,128]{2,1,0:T(8,128)S(1)}, u32[]{:S(2)}, u32[]{:S(2)}) %collective-permute-start) | collective-permute-done | bytes 65568 | tf_op jit(solution)/shard_map/ppermute | solution.py:338
  4.0 0.4 %shard_map.74 = (f32[8,16,128]{2,1,0:T(8,128)S(1)}, s16[9,16,128]{2,1,0:T(8,128)(2,1)S(1)}) custom-call(s32[1]{0:T(128)} %bitcast.index_ref, f32[8,16,128]{2,1,0:T(8,128)S(1)} %local.1.own_ref, f32[8,16,128]{2,1,0:T(8,128)S(1)} %collective-permute-done.other_ref, bf16[5,8,128,128]{3,2,1,0:T(8,128)(2,1)S(1)} %shard_map.73.matrices_ref), custom_call_target="tpu_custom_call" | custom-call | tf_op jit(solution)/shard_map/pallas_call | solution.py:270
  4.4 2.9 %collective-permute-start.1 = (s16[9,16,128]{2,1,0:T(8,128)(2,1)S(1)}, s16[9,16,128]{2,1,0:T(8,128)(2,1)S(1)}, u32[]{:S(2)}, u32[]{:S(2)}) collective-permute-start(s16[9,16,128]{2,1,0:T(8,128)(2,1)S(1)} %get-tuple-element.17), channel_id=1, source_target_pairs={{0,2},{1,3},{2,0},{3,1},{4,6},{5,7},{6,4},{7,5},{8,10},{9,11},{10,... | collective-permute-start | bytes 110600 | tf_op jit(solution)/shard_map/ppermute | solution.py:338
  7.2 0.0 copy-done.2
  7.3 4.1 %collective-permute-start.6 = (bf16[32,1024]{1,0:T(8,128)(2,1)S(1)}, bf16[32,1024]{1,0:T(8,128)(2,1)S(1)}, u32[]{:S(2)}, u32[]{:S(2)}) collective-permute-start(bf16[32,1024]{1,0:T(8,128)(2,1)S(1)} %get-tuple-element.27), channel_id=1, source_target_pairs={{0,31},{1,2},{2,1},{3,4},{4,3},{5,6},{6,5},{7,8},{8,7},{9,10},{10,... | collective-permute-start | bytes 196616 | tf_op jit(solution)/shard_map/ppermute | solution.py:293
  11.3 0.0 collective-permute-start.5
  11.3 0.0 collective-permute-done.1.other_ref
  11.3 0.0 copy-start.1
  11.3 0.0 copy-start.5
  11.4 0.4 %shard_map.75 = (f32[8,16,128]{2,1,0:T(8,128)S(1)}, s16[9,16,128]{2,1,0:T(8,128)(2,1)S(1)}) custom-call(s32[1]{0:T(128)} %bitcast.index_ref, f32[8,16,128]{2,1,0:T(8,128)S(1)} %get-tuple-element.16.own_ref, s16[9,16,128]{2,1,0:T(8,128)(2,1)S(1)} %collective-permute-done.1.other_ref, bf16[5,8,128,128]{3,2,1,0:T(8,128)(2,1)S(1)} %shard_map.73.matrices_ref), custom_call_target="tpu_custom_call" | custom-call | tf_op jit(solution)/shard_map/pallas_call | solution.py:270
  11.7 0.1 collective-permute-start.2
  11.8 3.9 %collective-permute-done.2.other_ref = s16[9,16,128]{2,1,0:T(8,128)(2,1)S(1)} collective-permute-done((s16[9,16,128]{2,1,0:T(8,128)(2,1)S(1)}, s16[9,16,128]{2,1,0:T(8,128)(2,1)S(1)}, u32[]{:S(2)}, u32[]{:S(2)}) %collective-permute-start.2) | collective-permute-done | bytes 36896 | tf_op jit(solution)/shard_map/ppermute | solution.py:338
  15.8 0.4 %shard_map.76 = (f32[8,16,128]{2,1,0:T(8,128)S(1)}, s16[9,16,128]{2,1,0:T(8,128)(2,1)S(1)}) custom-call(s32[1]{0:T(128)} %bitcast.index_ref, f32[8,16,128]{2,1,0:T(8,128)S(1)} %get-tuple-element.18.own_ref, s16[9,16,128]{2,1,0:T(8,128)(2,1)S(1)} %collective-permute-done.2.other_ref, bf16[5,8,128,128]{3,2,1,0:T(8,128)(2,1)S(1)} %shard_map.73.matrices_ref), custom_call_target="tpu_custom_call" | custom-call | tf_op jit(solution)/shard_map/pallas_call | solution.py:270
  16.2 0.1 collective-permute-start.3
  16.2 0.0 collective-permute-done.6.ring_ref
  16.2 0.0 collective-permute-done.5.pair_ref
  16.3 0.0 copy-done.1
  16.3 0.0 copy-done.5
  16.3 0.0 copy-start.4
  16.3 1.0 %shard_map.78 = (f32[16,32,128]{2,1,0:T(8,128)S(1)}, f32[32,512]{1,0:T(8,128)S(1)}, f32[32,512]{1,0:T(8,128)S(1)}) custom-call(s32[1]{0:T(128)} %bitcast.index_ref, s32[2,24]{1,0:T(2,128)S(1)} %bitcast.2, bf16[32,2048]{1,0:T(8,128)(2,1)S(1)} %copy-done.2, bf16[32,1024]{1,0:T(8,128)(2,1)S(1)} %collective-permute-done.5.pair_ref, ...), custom_call_target="tpu_custom_call" | custom-call | tf_op jit(solution)/shard_map/pallas_call | solution.py:270
  17.3 0.1 collective-permute-start.7
  17.3 4.7 %collective-permute-start.8 = (f32[32,512]{1,0:T(8,128)S(1)}, f32[32,512]{1,0:T(8,128)S(1)}, u32[]{:S(2)}, u32[]{:S(2)}) collective-permute-start(f32[32,512]{1,0:T(8,128)S(1)} %get-tuple-element.26), channel_id=1, source_target_pairs={{0,31},{1,2},{2,1},{3,4},{4,3},{5,6},{6,5},{7,8},{8,7},{9,10},{10,... | collective-permute-start | bytes 196616 | tf_op jit(solution)/shard_map/ppermute | solution.py:334
  22.1 0.0 collective-permute-done.3.other_ref
  22.1 0.4 %shard_map.77 = (f32[8,16,128]{2,1,0:T(8,128)S(1)}, s16[9,16,128]{2,1,0:T(8,128)(2,1)S(1)}) custom-call(s32[1]{0:T(128)} %bitcast.index_ref, f32[8,16,128]{2,1,0:T(8,128)S(1)} %get-tuple-element.20.own_ref, s16[9,16,128]{2,1,0:T(8,128)(2,1)S(1)} %collective-permute-done.3.other_ref, bf16[5,8,128,128]{3,2,1,0:T(8,128)(2,1)S(1)} %shard_map.73.matrices_ref), custom_call_target="tpu_custom_call" | custom-call | tf_op jit(solution)/shard_map/pallas_call | solution.py:270
  22.5 0.1 collective-permute-start.4
  22.5 0.0 collective-permute-done.7.pair_ref
  22.6 2.1 %collective-permute-done.8.ring_ref = f32[32,512]{1,0:T(8,128)S(1)} collective-permute-done((f32[32,512]{1,0:T(8,128)S(1)}, f32[32,512]{1,0:T(8,128)S(1)}, u32[]{:S(2)}, u32[]{:S(2)}) %collective-permute-start.8) | collective-permute-done | bytes 65568 | tf_op jit(solution)/shard_map/ppermute | solution.py:334
  24.7 2.7 %collective-permute-done.4.other_ref = s16[9,16,128]{2,1,0:T(8,128)(2,1)S(1)} collective-permute-done((s16[9,16,128]{2,1,0:T(8,128)(2,1)S(1)}, s16[9,16,128]{2,1,0:T(8,128)(2,1)S(1)}, u32[]{:S(2)}, u32[]{:S(2)}) %collective-permute-start.4) | collective-permute-done | bytes 36896 | tf_op jit(solution)/shard_map/ppermute | solution.py:338
  27.4 0.0 copy-done.4
  27.4 1.2 %final.1 = f32[32,2048]{1,0:T(8,128)} custom-call(s32[1]{0:T(128)} %bitcast.index_ref, f32[8,16,128]{2,1,0:T(8,128)S(1)} %get-tuple-element.22.own_ref, s16[9,16,128]{2,1,0:T(8,128)(2,1)S(1)} %collective-permute-done.4.other_ref, bf16[5,8,128,128]{3,2,1,0:T(8,128)(2,1)S(1)} %shard_map.73.matrices_ref, bf16[64,2048]{1,0:T(8,128)(2,1)S(1)} %copy-done.4, ...), custom_call_target="tpu_custom_call" | custom-call | tf_op jit(solution)/shard_map/final/pallas_call | solution.py:346
  (1 shorter events, 0.0 us)
Async XLA Ops:
  0.0 3.1 %copy-start.3 = (bf16[256,512]{1,0:T(8,128)(2,1)S(1)}, bf16[256,512]{1,0:T(8,128)(2,1)}, u32[]{:S(2)}) copy-start(bf16[256,512]{1,0:T(8,128)(2,1)} %constant.22.clone.table_hbm.table_ref) | copy-start | bytes 786436
  0.0 3.1 %copy-start = (bf16[16,9,32,128]{3,2,1,0:T(8,128)(2,1)S(1)}, bf16[16,9,32,128]{3,2,1,0:T(8,128)(2,1)}, u32[]{:S(2)}) copy-start(bf16[16,9,32,128]{3,2,1,0:T(8,128)(2,1)} %transfer_ref.1) | copy-start | bytes 3538948
  2.5 1.5 %collective-permute-start = (f32[8,16,128]{2,1,0:T(8,128)S(1)}, f32[8,16,128]{2,1,0:T(8,128)S(1)}, u32[]{:S(2)}, u32[]{:S(2)}) collective-permute-start(f32[8,16,128]{2,1,0:T(8,128)S(1)} %local.1.own_ref), channel_id=1, source_target_pairs={{0,1},{1,0},{2,3},{3,2},{4,5},{5,4},{6,7},{7,6},{8,9},{9,8},{10,11... | collective-permute-start | bytes 196616 | tf_op jit(solution)/shard_map/ppermute | solution.py:338
  3.6 3.7 %copy-start.2 = (bf16[32,2048]{1,0:T(8,128)(2,1)S(1)}, bf16[32,2048]{1,0:T(8,128)(2,1)}, u32[]{:S(2)}) copy-start(bf16[32,2048]{1,0:T(8,128)(2,1)} %signal_ref.1) | copy-start | bytes 393220
  4.4 7.0 %collective-permute-start.1 = (s16[9,16,128]{2,1,0:T(8,128)(2,1)S(1)}, s16[9,16,128]{2,1,0:T(8,128)(2,1)S(1)}, u32[]{:S(2)}, u32[]{:S(2)}) collective-permute-start(s16[9,16,128]{2,1,0:T(8,128)(2,1)S(1)} %get-tuple-element.17), channel_id=1, source_target_pairs={{0,2},{1,3},{2,0},{3,1},{4,6},{5,7},{6,4},{7,5},{8,10},{9,11},{10,... | collective-permute-start | bytes 110600 | tf_op jit(solution)/shard_map/ppermute | solution.py:338
  7.3 9.0 %collective-permute-start.6 = (bf16[32,1024]{1,0:T(8,128)(2,1)S(1)}, bf16[32,1024]{1,0:T(8,128)(2,1)S(1)}, u32[]{:S(2)}, u32[]{:S(2)}) collective-permute-start(bf16[32,1024]{1,0:T(8,128)(2,1)S(1)} %get-tuple-element.27), channel_id=1, source_target_pairs={{0,31},{1,2},{2,1},{3,4},{4,3},{5,6},{6,5},{7,8},{8,7},{9,10},{10,... | collective-permute-start | bytes 196616 | tf_op jit(solution)/shard_map/ppermute | solution.py:293
  11.3 4.9 %collective-permute-start.5 = (bf16[32,1024]{1,0:T(8,128)(2,1)S(1)}, bf16[32,1024]{1,0:T(8,128)(2,1)S(1)}, u32[]{:S(2)}, u32[]{:S(2)}) collective-permute-start(bf16[32,1024]{1,0:T(8,128)(2,1)S(1)} %get-tuple-element.28), channel_id=1, source_target_pairs={{0,1},{1,0},{2,3},{3,2},{4,5},{5,4},{6,7},{7,6},{8,9},{9,8},{10,11... | collective-permute-start | bytes 196616 | tf_op jit(solution)/shard_map/ppermute | solution.py:292
  11.3 4.9 %copy-start.1 = (bf16[24,128,256]{2,1,0:T(8,128)(2,1)S(1)}, bf16[24,128,256]{2,1,0:T(8,128)(2,1)}, u32[]{:S(2)}) copy-start(bf16[24,128,256]{2,1,0:T(8,128)(2,1)} %blocks_ref.1) | copy-start | bytes 4718596
  11.3 4.9 %copy-start.5 = (s32[24,2]{0,1:T(2,128)S(1)}, s32[24,2]{0,1:T(2,128)}, u32[]{:S(2)}) copy-start(s32[24,2]{0,1:T(2,128)} %param.12) | copy-start | bytes 580
  11.7 4.0 %collective-permute-start.2 = (s16[9,16,128]{2,1,0:T(8,128)(2,1)S(1)}, s16[9,16,128]{2,1,0:T(8,128)(2,1)S(1)}, u32[]{:S(2)}, u32[]{:S(2)}) collective-permute-start(s16[9,16,128]{2,1,0:T(8,128)(2,1)S(1)} %get-tuple-element.19), channel_id=1, source_target_pairs={{0,4},{1,5},{2,6},{3,7},{4,0},{5,1},{6,2},{7,3},{8,12},{9,13},{10,... | collective-permute-start | bytes 110600 | tf_op jit(solution)/shard_map/ppermute | solution.py:338
  16.2 5.9 %collective-permute-start.3 = (s16[9,16,128]{2,1,0:T(8,128)(2,1)S(1)}, s16[9,16,128]{2,1,0:T(8,128)(2,1)S(1)}, u32[]{:S(2)}, u32[]{:S(2)}) collective-permute-start(s16[9,16,128]{2,1,0:T(8,128)(2,1)S(1)} %get-tuple-element.21), channel_id=1, source_target_pairs={{0,8},{1,9},{2,10},{3,11},{4,12},{5,13},{6,14},{7,15},{8,0},{9,1},... | collective-permute-start | bytes 110600 | tf_op jit(solution)/shard_map/ppermute | solution.py:338
  16.3 11.1 %copy-start.4 = (bf16[64,2048]{1,0:T(8,128)(2,1)S(1)}, bf16[64,2048]{1,0:T(8,128)(2,1)}, u32[]{:S(2)}) copy-start(bf16[64,2048]{1,0:T(8,128)(2,1)} %basis_ref.1) | copy-start | bytes 786436
  17.3 5.3 %collective-permute-start.7 = (f32[32,512]{1,0:T(8,128)S(1)}, f32[32,512]{1,0:T(8,128)S(1)}, u32[]{:S(2)}, u32[]{:S(2)}) collective-permute-start(f32[32,512]{1,0:T(8,128)S(1)} %get-tuple-element.25), channel_id=1, source_target_pairs={{0,1},{1,0},{2,3},{3,2},{4,5},{5,4},{6,7},{7,6},{8,9},{9,8},{10,11... | collective-permute-start | bytes 196616 | tf_op jit(solution)/shard_map/ppermute | solution.py:333
  17.3 7.4 %collective-permute-start.8 = (f32[32,512]{1,0:T(8,128)S(1)}, f32[32,512]{1,0:T(8,128)S(1)}, u32[]{:S(2)}, u32[]{:S(2)}) collective-permute-start(f32[32,512]{1,0:T(8,128)S(1)} %get-tuple-element.26), channel_id=1, source_target_pairs={{0,31},{1,2},{2,1},{3,4},{4,3},{5,6},{6,5},{7,8},{8,7},{9,10},{10,... | collective-permute-start | bytes 196616 | tf_op jit(solution)/shard_map/ppermute | solution.py:334
  22.5 4.9 %collective-permute-start.4 = (s16[9,16,128]{2,1,0:T(8,128)(2,1)S(1)}, s16[9,16,128]{2,1,0:T(8,128)(2,1)S(1)}, u32[]{:S(2)}, u32[]{:S(2)}) collective-permute-start(s16[9,16,128]{2,1,0:T(8,128)(2,1)S(1)} %get-tuple-element.23), channel_id=1, source_target_pairs={{0,16},{1,17},{2,18},{3,19},{4,20},{5,21},{6,22},{7,23},{8,24},{9,... | collective-permute-start | bytes 110600 | tf_op jit(solution)/shard_map/ppermute | solution.py:338

commit v6 on v5

--- a/solution.py
+++ b/solution.py
@@ -2,7 +2,6 @@
 
 import jax
 import jax.numpy as jnp
-import numpy as np
 from jax import lax
 from jax.experimental import pallas as pl
 from jax.experimental.pallas import tpu as pltpu
@@ -41,19 +40,17 @@
     return [top, rest]
 
 
-def form_table(rank):
-    width = 4 * rank
-    table = np.zeros((2 * width, 4 * width), np.float32)
-    unit = np.eye(rank, dtype=np.float32)
-    for group in range(4):
-        child, imag = divmod(group, 2)
-        for box in range(2):
-            for part in range(2):
-                source = box * width + child * 2 * rank + (part ^ imag) * rank
-                target = group * width + box * 2 * rank + part * rank
-                sign = -1.0 if part and not imag else 1.0
-                table[source : source + rank, target : target + rank] = sign * unit
-    return table
+def form_table(rank, rows, columns):
+    bit = rank.bit_length() - 1
+    column = lax.broadcasted_iota(jnp.int32, (rows, columns), 1)
+    row = lax.broadcasted_iota(jnp.int32, (rows, columns), 0)
+    part = (column >> bit) & 1
+    box = (column >> (bit + 1)) & 1
+    imag = (column >> (bit + 2)) & 1
+    child = column >> (bit + 3)
+    source = (box << (bit + 2)) + (child << (bit + 1)) + ((part ^ imag) << bit) + (column & (rank - 1))
+    value = jnp.where(part > imag, -1.0, 1.0)
+    return jnp.where(row == source, value, 0.0).astype(BF16)
 
 
 def level_matrices(blocks, pairs, table):
@@ -86,25 +83,46 @@
 
 
 def local_kernel(
-    signal_hbm, basis_hbm, transfer_hbm, table_hbm, out_ref, signal_ref, basis_ref, transfer_ref, table_ref, arrived
+    index_ref,
+    signal_hbm,
+    basis_hbm,
+    transfer_hbm,
+    out_ref,
+    signal_ref,
+    transfer_ref,
+    table_ref,
+    to_pair_ref,
+    to_ring_ref,
+    basis_ref,
+    arrived,
 ):
-    boxes, levels = transfer_ref.shape[:2]
+    boxes = transfer_ref.shape[0]
+    levels = boxes.bit_length() - 1
     rhs = signal_ref.shape[0] // 2
+    near_levels = pl.ds(0, levels)
+    far_levels = pl.ds(levels, transfer_ref.shape[1] - levels)
     copies = [
         pltpu.make_async_copy(signal_hbm, signal_ref, arrived.at[0]),
         pltpu.make_async_copy(basis_hbm, basis_ref, arrived.at[1]),
-        pltpu.make_async_copy(table_hbm, table_ref, arrived.at[2]),
-        pltpu.make_async_copy(transfer_hbm.at[:, pl.ds(0, levels)], transfer_ref, arrived.at[3]),
+        pltpu.make_async_copy(transfer_hbm.at[:, near_levels], transfer_ref.at[:, near_levels], arrived.at[2]),
+        pltpu.make_async_copy(transfer_hbm.at[:, far_levels], transfer_ref.at[:, far_levels], arrived.at[3]),
     ]
-    for copy in copies:
+    for copy in copies[:3]:
         copy.start()
+    table_ref[...] = form_table(transfer_ref.shape[2], *table_ref.shape)
     for copy in copies[:2]:
         copy.wait()
+    odd = (index_ref[0] & 1) == 1
+    halo = to_pair_ref.shape[1]
+    head = signal_ref[:, :halo]
+    tail = signal_ref[:, signal_ref.shape[1] - halo :]
+    to_pair_ref[...] = jnp.where(odd, head, tail)
+    to_ring_ref[...] = jnp.where(odd, tail, head)
     state = {}
     for box in range(0, boxes, 2):
         state[box] = project_pair(signal_ref, basis_ref, box, box + 1)
-    for copy in copies[2:]:
-        copy.wait()
+    copies[2].wait()
+    copies[3].start()
     table = table_ref[...]
     for level in range(levels):
         bit = 1 << level
@@ -125,17 +143,19 @@
                 state[box + bit] = pick_low(half_roll(done[box]), done[other])
     for box, pair in state.items():
         out_ref[box] = pair
-
-
-def matrices_kernel(transfer_ref, table_ref, out_ref, *, first_level):
+    copies[3].wait()
+
+
+def matrices_kernel(transfer_ref, table_ref, own_ref, lent_ref, *, own_levels, lent_levels):
     boxes = transfer_ref.shape[0]
     half = boxes // 2
     table = table_ref[...]
-    for level in range(out_ref.shape[0]):
-        blocks = [transfer_ref[box, first_level + level] for box in range(boxes)]
-        matrices = level_matrices(blocks, [(box, box + half) for box in range(half)], table)
-        for box in range(half):
-            out_ref[level, box] = matrices[box]
+    for levels, out_ref in ((lent_levels, lent_ref), (own_levels, own_ref)):
+        for place, level in enumerate(levels):
+            blocks = [transfer_ref[box, level] for box in range(boxes)]
+            matrices = level_matrices(blocks, [(box, box + half) for box in range(half)], table)
+            for box in range(half):
+                out_ref[place, box] = matrices[box]
 
 
 CODE_STEPS = 256.0
@@ -146,10 +166,10 @@
     peak = jnp.abs(parts[0])
     for part in parts[1:]:
         peak = jnp.maximum(peak, jnp.abs(part))
-    peak = jnp.maximum(jnp.max(peak, axis=1, keepdims=True), 1e-30)
+    peak = jnp.maximum(peak, 1e-30)
     code = jnp.ceil(jnp.log2(peak) * CODE_STEPS) + 1.0
     gain = jnp.exp2(code * (-1.0 / CODE_STEPS)) * CODE_MAX
-    coded = [jnp.round(part * gain) for part in parts] + [jnp.broadcast_to(code, parts[0].shape)]
+    coded = [jnp.round(part * gain) for part in parts] + [code]
     return [part.astype(jnp.int32).astype(jnp.int16) for part in coded]
 
 
@@ -174,11 +194,11 @@
     return lax.axis_index("leaf") * lax.axis_size("sub") + lax.axis_index("sub")
 
 
-def cross_kernel(index_ref, own_ref, other_ref, matrices_ref, out_ref, code_ref, *, level):
+def cross_kernel(index_ref, own_ref, other_ref, matrices_ref, out_ref, code_ref, *, level, place):
     upper = (index_ref[0] >> level & 1) == 1
     half = own_ref.shape[0]
     other = decode(other_ref) if level else lambda box: other_ref[box]
-    outs = [crossed(own_ref[box], other(box), matrices_ref[level, box], upper) for box in range(half)]
+    outs = [crossed(own_ref[box], other(box), matrices_ref[place, box], upper) for box in range(half)]
     for box, part in enumerate(encode(outs)):
         code_ref[box] = part
     for box, part in enumerate(outs):
@@ -186,36 +206,36 @@
 
 
 def final_kernel(
-    index_ref, own_ref, other_ref, matrices_ref, basis_ref, center_ref, pair_ref, ring_ref, out_ref, *, level
+    index_ref, own_ref, other_ref, matrices_ref, basis_ref, center_ref, pair_ref, ring_ref, out_ref, *, level, place
 ):
     upper = (index_ref[0] >> level & 1) == 1
     odd = (index_ref[0] & 1) == 1
     half, rhs, width = own_ref.shape
     rank = width // 4
-    edge = pair_ref.shape[1] // LEAF
+    edge = pair_ref.shape[0]
     other = decode(other_ref)
+    from_ring = decode(ring_ref)
     for box in range(half):
-        pair = crossed(own_ref[box], other(box), matrices_ref[level, box], upper)
+        pair = crossed(own_ref[box], other(box), matrices_ref[place, box], upper)
         is_low = lanes_like(pair) < width // 2
         rows = []
         for part in (jnp.where(is_low, pair, 0.0), jnp.where(is_low, 0.0, pair)):
             rows += split_rows(part)
         right = []
-        for place in (box, box + half):
-            v = basis_ref[:, pl.ds(place * LEAF, LEAF)]
+        for spot in (box, box + half):
+            v = basis_ref[:, pl.ds(spot * LEAF, LEAF)]
             right.append(jnp.concatenate([v[:rank], v[rank:]], axis=1))
             right.append(jnp.concatenate([-v[rank:], v[:rank]], axis=1))
         out = dot(jnp.concatenate(rows, axis=0), jnp.concatenate(right, axis=0))
-        for k, place in enumerate((box, box + half)):
+        for k, spot in enumerate((box, box + half)):
             far = out[2 * k * rhs : (2 * k + 1) * rhs] + out[(2 * k + 1) * rhs : (2 * k + 2) * rhs]
-            total = center_ref[place] + jnp.concatenate([far[:, :LEAF], far[:, LEAF:]], axis=0)
-            if place < edge:
-                cols = pl.ds(place * LEAF, LEAF)
-                total = total + jnp.where(odd, pair_ref[:, cols], ring_ref[:, cols])
-            if place >= 2 * half - edge:
-                cols = pl.ds((place - 2 * half + edge) * LEAF, LEAF)
-                total = total + jnp.where(odd, ring_ref[:, cols], pair_ref[:, cols])
-            out_ref[:, pl.ds(place * LEAF, LEAF)] = total
+            total = center_ref[spot] + jnp.concatenate([far[:, :LEAF], far[:, LEAF:]], axis=0)
+            if spot < edge:
+                total = total + jnp.where(odd, pair_ref[spot], from_ring(spot))
+            if spot >= 2 * half - edge:
+                rim = spot - 2 * half + edge
+                total = total + jnp.where(odd, from_ring(rim), pair_ref[rim])
+            out_ref[:, pl.ds(spot * LEAF, LEAF)] = total
 
 
 def near_kernel(
@@ -226,7 +246,7 @@
     rhs = channels // 2
     boxes = signal_ref.shape[1] // LEAF
     halo = pair_ref.shape[1] // LEAF
-    edge = to_pair_ref.shape[1] // LEAF
+    edge = to_pair_ref.shape[0]
     for box in range(halo):
         cols = pl.ds(box * LEAF, LEAF)
         window[box] = jnp.where(odd, pair_ref[:, cols], ring_ref[:, cols])
@@ -244,12 +264,14 @@
         sums[col] = sums[col] + jnp.concatenate([real, imag], axis=0)
     for box in range(boxes):
         center_ref[box] = sums[edge + box]
+    to_ring = []
     for box in range(edge):
-        cols = pl.ds(box * LEAF, LEAF)
         before = sums[box]
         after = sums[edge + boxes + box]
-        to_pair_ref[:, cols] = jnp.where(odd, before, after)
-        to_ring_ref[:, cols] = jnp.where(odd, after, before)
+        to_pair_ref[box] = jnp.where(odd, before, after)
+        to_ring.append(jnp.where(odd, after, before))
+    for box, part in enumerate(encode(to_ring)):
+        to_ring_ref[box] = part
 
 
 VMEM = pl.BlockSpec(memory_space=pltpu.VMEM)
@@ -273,55 +295,66 @@
 def shards(signal, row_basis, transfer, column_basis, near_blocks, near_list):
     channels = signal.shape[0]
     rhs = channels // 2
-    boxes, levels, rank, width = transfer.shape
+    boxes, levels, _, width = transfer.shape
     half = boxes // 2
     reach = boxes // 4
     local_levels = boxes.bit_length() - 1
     devices = lax.axis_size("leaf") * lax.axis_size("sub")
     index = device_index()
     index_word = index.astype(jnp.int32).reshape(1)
-    odd = index & 1
 
     pairs = [(i, i ^ 1) for i in range(devices)]
     ring = [(i, (i + 1) % devices if i & 1 else (i - 1) % devices) for i in range(devices)]
 
     halo = 2 * reach * LEAF
-    far_end = signal.shape[1] - halo
-    to_pair = lax.dynamic_slice_in_dim(signal, jnp.where(odd == 1, 0, far_end), halo, 1)
-    to_ring = lax.dynamic_slice_in_dim(signal, jnp.where(odd == 1, far_end, 0), halo, 1)
+    state = ((half, rhs, width), F32)
+    coeffs, signal, transfer, table, to_pair, to_ring = pl.pallas_call(
+        local_kernel,
+        out_shape=(
+            pltpu.VMEM(*state),
+            pltpu.VMEM(signal.shape, BF16),
+            pltpu.VMEM(transfer.shape, BF16),
+            pltpu.VMEM((2 * width, 4 * width), BF16),
+            pltpu.VMEM((channels, halo), BF16),
+            pltpu.VMEM((channels, halo), BF16),
+        ),
+        in_specs=[SMEM] + [pl.BlockSpec(memory_space=pl.ANY)] * 3,
+        out_specs=(VMEM,) * 6,
+        scratch_shapes=[pltpu.VMEM(row_basis.shape, BF16), pltpu.SemaphoreType.DMA((4,))],
+        compiler_params=pltpu.CompilerParams(vmem_limit_bytes=16 << 20),
+        name="local",
+    )(
+        index_word,
+        *[pltpu.with_memory_space_constraint(x, pltpu.HBM) for x in (signal, row_basis, transfer)],
+    )
     from_pair = lax.ppermute(to_pair, AXES, pairs)
     from_ring = lax.ppermute(to_ring, AXES, ring)
 
-    table = jnp.asarray(form_table(rank), BF16)
-    state = ((half, rhs, width), F32)
-    coeffs = pl.pallas_call(
-        local_kernel,
-        out_shape=pltpu.VMEM(*state),
-        in_specs=[pl.BlockSpec(memory_space=pl.ANY)] * 4,
-        out_specs=VMEM,
-        scratch_shapes=[
-            pltpu.VMEM(signal.shape, BF16),
-            pltpu.VMEM(row_basis.shape, BF16),
-            pltpu.VMEM((boxes, local_levels, rank, width), BF16),
-            pltpu.VMEM(table.shape, BF16),
-            pltpu.SemaphoreType.DMA((4,)),
-        ],
-        compiler_params=pltpu.CompilerParams(vmem_limit_bytes=16 << 20),
-        name="local",
-    )(*[pltpu.with_memory_space_constraint(x, pltpu.HBM) for x in (signal, row_basis, transfer, table)])
     cross_levels = levels - local_levels
-    matrices = on_chip(
-        functools.partial(matrices_kernel, first_level=local_levels),
-        ((cross_levels, half, width, width), BF16),
+    crossing = crossings(cross_levels)
+    lent = [bool(sum(crossing[level + 1 :]) & 1) for level in range(cross_levels)]
+    own_levels = [level for level in range(cross_levels) if not lent[level]]
+    lent_levels = [level for level in range(cross_levels) if lent[level]]
+    own_matrices, to_lend = on_chip(
+        functools.partial(
+            matrices_kernel,
+            own_levels=[local_levels + level for level in own_levels],
+            lent_levels=[local_levels + level for level in lent_levels],
+        ),
+        (
+            ((len(own_levels), half, width, width), BF16),
+            ((len(lent_levels), half, width, width), BF16),
+        ),
         (),
         (transfer, table),
     )
+    lent_matrices = lax.ppermute(to_lend, AXES, pairs)
     center, rim_pair, rim_ring = on_chip(
         near_kernel,
         (
             ((boxes, channels, LEAF), F32),
-            ((channels, reach * LEAF), F32),
-            ((channels, reach * LEAF), F32),
+            ((reach, channels, LEAF), F32),
+            ((reach + 1, channels, LEAF), jnp.int16),
         ),
         (index_word, near_list.T),
         (signal, from_pair, from_ring, near_blocks),
@@ -335,16 +368,21 @@
 
     sent = coeffs
     for level in range(cross_levels):
-        other = lax.ppermute(sent, AXES, [(i, i ^ 1 << level) for i in range(devices)])
+        flip = 1 << level | crossing[level]
+        other = lax.ppermute(sent, AXES, [(i, i ^ flip) for i in range(devices)])
+        if crossing[level]:
+            coeffs = lax.ppermute(coeffs, AXES, pairs)
+        matrices, place = (lent_matrices, lent_levels) if lent[level] else (own_matrices, own_levels)
+        place = place.index(level)
         if level + 1 < cross_levels:
             coeffs, sent = on_chip(
-                functools.partial(cross_kernel, level=level),
+                functools.partial(cross_kernel, level=level, place=place),
                 (state, ((half + 1, rhs, width), jnp.int16)),
                 (index_word,),
                 (coeffs, other, matrices),
             )
     return pl.pallas_call(
-        functools.partial(final_kernel, level=cross_levels - 1),
+        functools.partial(final_kernel, level=cross_levels - 1, place=place),
         out_shape=jax.ShapeDtypeStruct((channels, boxes * LEAF), F32),
         in_specs=[SMEM] + [VMEM] * 7,
         out_specs=VMEM,
@@ -359,6 +397,13 @@
     )
 
 
+def crossings(levels):
+    return [int(level - levels in CROSSED) for level in range(levels)]
+
+
+CROSSED = (-3, -1)
+
+
 def solution(mesh):
     return jax.shard_map(
         shards,

time: 28.7 us -> 32.3 us (1.13)
  starting transfers between devices: 12.6 us -> 15.1 us
  waiting for transfers between devices: 9.16 us -> 10.6 us
  Pallas kernels: 6.68 us -> 6.35 us
    ppermute x1, waiting for transfers between devices: 0.01 us -> 2.37 us  [shards(): from_ring = lax.ppermute(to_ring, AXES, ring)]
    ppermute x5 -> x8, starting transfers between devices: 3.67 us -> 5.93 us  [the longest x5 5.22 us: shards(): other = lax.ppermute(sent, AXES, [(i, i ^ flip) for i in range(devices)])]
    ppermute x5 -> x8, waiting for transfers between devices: 7.02 us -> 5.26 us  [the longest x5 5.25 us: shards(): other = lax.ppermute(sent, AXES, [(i, i ^ flip) for i in range(devices)])]
    ppermute x1, waiting for transfers between devices: 2.13 us -> 3 us  [shards(): rim_from_ring = lax.ppermute(rim_ring, AXES, ring)]
    ppermute x1, starting transfers between devices: 4.07 us -> 4.5 us  [shards(): from_ring = lax.ppermute(to_ring, AXES, ring)]
  transfers between devices with their start and end apart: 9 -> 12, of which waited for: 4 -> 6; matrix products, arithmetic and copies ran while one was open for 0% -> 0% of each run, Pallas kernels for 9% -> 7%
where the time goes in v6:
time: 32.3 us; the launch traced here: 32.2 us
  starting transfers between devices  15.1 us (47%)
  waiting for transfers between devices  10.6 us (33%)
  Pallas kernels  6.35 us (20%)
    ppermute x5, waiting for transfers between devices, shards(): other = lax.ppermute(sent, AXES, [(i, i ^ flip) for i in range(devices)])  5.25 us
    ppermute x5, starting transfers between devices, shards(): other = lax.ppermute(sent, AXES, [(i, i ^ flip) for i in range(devices)])  5.22 us
    ppermute x1, starting transfers between devices, shards(): from_ring = lax.ppermute(to_ring, AXES, ring)  4.5 us
    ppermute x1, starting transfers between devices, shards(): rim_from_ring = lax.ppermute(rim_ring, AXES, ring)  4.49 us
    ppermute x1, waiting for transfers between devices, shards(): rim_from_ring = lax.ppermute(rim_ring, AXES, ring)  3 us
    pallas_call x6, Pallas kernels, on_chip(): call(*scalars, *[pltpu.with_memory_space_constraint(x, pltpu.VMEM) for x...  2.71 us
    pallas_call x1, Pallas kernels, shards(): pl.pallas_call(local_kernel, out_shape=(pltpu.VMEM(*state), pltpu.VMEM(si...  2.43 us
    ppermute x1, waiting for transfers between devices, shards(): from_ring = lax.ppermute(to_ring, AXES, ring)  2.37 us
  transfers between devices with their start and end apart: 12, of which 6 were waited for; matrix products, arithmetic and copies ran while one was open for 0% of the time, Pallas kernels for 7%

profile of v6, /device:TPU:0, one launch (start us, length us, event | category | flops | bytes accessed | tf_op | source)
XLA Modules:
  0.0 32.2 jit_solution(10084366240165311712)
XLA Ops:
  0.0 2.4 %local.1 = (f32[8,16,128]{2,1,0:T(8,128)S(1)}, bf16[32,2048]{1,0:T(8,128)(2,1)S(1)}, bf16[16,9,32,128]{3,2,1,0:T(8,128)(2,1)S(1)}, bf16[256,512]{1,0:T(8,128)(2,...) custom-call(s32[1]{0:T(128)} %bitcast.index_ref, bf16[32,2048]{1,0:T(8,128)(2,1)} %signal_hbm.1, ...), custom_call_target="tpu_custom_call" | custom-call | tf_op jit(solution)/shard_map/local/pallas_call | solution.py:311
  2.4 0.5 %shard_map.64 = (bf16[3,8,128,128]{3,2,1,0:T(8,128)(2,1)S(1)}, bf16[2,8,128,128]{3,2,1,0:T(8,128)(2,1)S(1)}) custom-call(bf16[16,9,32,128]{3,2,1,0:T(8,128)(2,1)S(1)} %get-tuple-element.25.transfer_ref, bf16[256,512]{1,0:T(8,128)(2,1)S(1)} %get-tuple-element.26.table_ref), custom_call_target="tpu_custom_call" | custom-call | tf_op jit(solution)/shard_map/pallas_call | solution.py:292
  2.9 0.6 %collective-permute-start.4 = (bf16[2,8,128,128]{3,2,1,0:T(8,128)(2,1)S(1)}, bf16[2,8,128,128]{3,2,1,0:T(8,128)(2,1)S(1)}, u32[]{:S(2)}, u32[]{:S(2)}) collective-permute-start(bf16[2,8,128,128]{3,2,1,0:T(8,128)(2,1)S(1)} %get-tuple-element.32), channel_id=1, source_target_pairs={{0,1},{1,0},{2,3},{3,2},{4,5},{5,4},{6,7},{7,6},{8,9},{9,8},{10,11... | collective-permute-start | bytes 1572872 | tf_op jit(solution)/shard_map/ppermute | solution.py:351
  3.5 0.1 collective-permute-start
  3.6 1.6 %collective-permute-done.other_ref = f32[8,16,128]{2,1,0:T(8,128)S(1)} collective-permute-done((f32[8,16,128]{2,1,0:T(8,128)S(1)}, f32[8,16,128]{2,1,0:T(8,128)S(1)}, u32[]{:S(2)}, u32[]{:S(2)}) %collective-permute-start) | collective-permute-done | bytes 65568 | tf_op jit(solution)/shard_map/ppermute | solution.py:372
  5.1 0.0 copy-start
  5.1 0.0 copy-start.2
  5.1 0.3 shard_map.65
  5.4 2.9 %collective-permute-start.1 = (s16[9,16,128]{2,1,0:T(8,128)(2,1)S(1)}, s16[9,16,128]{2,1,0:T(8,128)(2,1)S(1)}, u32[]{:S(2)}, u32[]{:S(2)}) collective-permute-start(s16[9,16,128]{2,1,0:T(8,128)(2,1)S(1)} %get-tuple-element.29), channel_id=1, source_target_pairs={{0,2},{1,3},{2,0},{3,1},{4,6},{5,7},{6,4},{7,5},{8,10},{9,11},{10,... | collective-permute-start | bytes 110600 | tf_op jit(solution)/shard_map/ppermute | solution.py:372
  8.4 1.9 %collective-permute-done.1.other_ref = s16[9,16,128]{2,1,0:T(8,128)(2,1)S(1)} collective-permute-done((s16[9,16,128]{2,1,0:T(8,128)(2,1)S(1)}, s16[9,16,128]{2,1,0:T(8,128)(2,1)S(1)}, u32[]{:S(2)}, u32[]{:S(2)}) %collective-permute-start.1) | collective-permute-done | bytes 36896 | tf_op jit(solution)/shard_map/ppermute | solution.py:372
  10.3 0.3 shard_map.66
  10.6 0.1 collective-permute-start.2
  10.7 2.1 %collective-permute-start.3 = (s16[9,16,128]{2,1,0:T(8,128)(2,1)S(1)}, s16[9,16,128]{2,1,0:T(8,128)(2,1)S(1)}, u32[]{:S(2)}, u32[]{:S(2)}) collective-permute-start(s16[9,16,128]{2,1,0:T(8,128)(2,1)S(1)} %get-tuple-element.31), channel_id=1, source_target_pairs={{0,5},{1,4},{2,7},{3,6},{4,1},{5,0},{6,3},{7,2},{8,13},{9,12},{10,... | collective-permute-start | bytes 110600 | tf_op jit(solution)/shard_map/ppermute | solution.py:372
  12.8 0.1 collective-permute-start.8
  12.9 4.5 %collective-permute-start.9 = (bf16[32,1024]{1,0:T(8,128)(2,1)S(1)}, bf16[32,1024]{1,0:T(8,128)(2,1)S(1)}, u32[]{:S(2)}, u32[]{:S(2)}) collective-permute-start(bf16[32,1024]{1,0:T(8,128)(2,1)S(1)} %get-tuple-element.39), channel_id=1, source_target_pairs={{0,31},{1,2},{2,1},{3,4},{4,3},{5,6},{6,5},{7,8},{8,7},{9,10},{10,... | collective-permute-start | bytes 196616 | tf_op jit(solution)/shard_map/ppermute | solution.py:331
  17.4 0.0 collective-permute-done.3.other_ref
  17.4 0.0 collective-permute-done.2.own_ref
  17.4 0.0 collective-permute-done.4.matrices_ref
  17.4 0.3 shard_map.67
  17.8 0.1 collective-permute-start.5
  17.8 0.0 collective-permute-done.8.pair_ref
  17.8 2.4 %collective-permute-done.9.ring_ref = bf16[32,1024]{1,0:T(8,128)(2,1)S(1)} collective-permute-done((bf16[32,1024]{1,0:T(8,128)(2,1)S(1)}, bf16[32,1024]{1,0:T(8,128)(2,1)S(1)}, u32[]{:S(2)}, u32[]{:S(2)}) %collective-permute-start.9) | collective-permute-done | bytes 65568 | tf_op jit(solution)/shard_map/ppermute | solution.py:331
  20.2 0.0 copy-done
  20.2 0.0 copy-done.2
  20.2 0.0 copy-start.1
  20.2 1.0 %shard_map.69 = (f32[16,32,128]{2,1,0:T(8,128)S(1)}, f32[4,32,128]{2,1,0:T(8,128)S(1)}, s16[5,32,128]{2,1,0:T(8,128)(2,1)S(1)}) custom-call(s32[1]{0:T(128)} %bitcast.index_ref, s32[2,24]{1,0:T(2,128)S(1)} %bitcast.2, bf16[32,2048]{1,0:T(8,128)(2,1)S(1)} %get-tuple-element.37.signal_ref, bf16[32,1024]{1,0:T(8,128)(2,1)S(1)} %collective-permute-done.8.pair_ref, ...), custom_call_target="tpu_custom_call" | custom-call | tf_op jit(solution)/shard_map/pallas_call | solution.py:292
  21.2 0.1 collective-permute-start.10
  21.3 0.5 %collective-permute-done.5.other_ref = s16[9,16,128]{2,1,0:T(8,128)(2,1)S(1)} collective-permute-done((s16[9,16,128]{2,1,0:T(8,128)(2,1)S(1)}, s16[9,16,128]{2,1,0:T(8,128)(2,1)S(1)}, u32[]{:S(2)}, u32[]{:S(2)}) %collective-permute-start.5) | collective-permute-done | bytes 36896 | tf_op jit(solution)/shard_map/ppermute | solution.py:372
  21.8 0.3 shard_map.68
  22.1 0.1 collective-permute-start.6
  22.2 4.5 %collective-permute-start.11 = (s16[5,32,128]{2,1,0:T(8,128)(2,1)S(1)}, s16[5,32,128]{2,1,0:T(8,128)(2,1)S(1)}, u32[]{:S(2)}, u32[]{:S(2)}) collective-permute-start(s16[5,32,128]{2,1,0:T(8,128)(2,1)S(1)} %get-tuple-element.42), channel_id=1, source_target_pairs={{0,31},{1,2},{2,1},{3,4},{4,3},{5,6},{6,5},{7,8},{8,7},{9,10},{10,... | collective-permute-start | bytes 122888 | tf_op jit(solution)/shard_map/ppermute | solution.py:367
  26.7 0.0 collective-permute-start.7
  26.7 3.0 %collective-permute-done.11.ring_ref = s16[5,32,128]{2,1,0:T(8,128)(2,1)S(1)} collective-permute-done((s16[5,32,128]{2,1,0:T(8,128)(2,1)S(1)}, s16[5,32,128]{2,1,0:T(8,128)(2,1)S(1)}, u32[]{:S(2)}, u32[]{:S(2)}) %collective-permute-start.11) | collective-permute-done | bytes 40992 | tf_op jit(solution)/shard_map/ppermute | solution.py:367
  29.7 0.0 collective-permute-done.10.pair_ref
  29.7 1.3 %collective-permute-done.7.other_ref = s16[9,16,128]{2,1,0:T(8,128)(2,1)S(1)} collective-permute-done((s16[9,16,128]{2,1,0:T(8,128)(2,1)S(1)}, s16[9,16,128]{2,1,0:T(8,128)(2,1)S(1)}, u32[]{:S(2)}, u32[]{:S(2)}) %collective-permute-start.7) | collective-permute-done | bytes 36896 | tf_op jit(solution)/shard_map/ppermute | solution.py:372
  31.0 0.0 collective-permute-done.6.own_ref
  31.0 0.0 copy-done.1
  31.0 1.2 %final.1 = f32[32,2048]{1,0:T(8,128)} custom-call(s32[1]{0:T(128)} %bitcast.index_ref, f32[8,16,128]{2,1,0:T(8,128)S(1)} %collective-permute-done.6.own_ref, s16[9,16,128]{2,1,0:T(8,128)(2,1)S(1)} %collective-permute-done.7.other_ref, bf16[3,8,128,128]{3,2,1,0:T(8,128)(2,1)S(1)} %get-tuple-element.27.matrices_ref, bf16[64,2048]{1,0:T(8,128)(2,1)S(1)} %copy-done.1, ...), custom_call_target="tpu_custom_call" | custom-call | tf_op jit(solution)/shard_map/final/pallas_call | solution.py:384
Async XLA Ops:
  2.9 14.5 %collective-permute-start.4 = (bf16[2,8,128,128]{3,2,1,0:T(8,128)(2,1)S(1)}, bf16[2,8,128,128]{3,2,1,0:T(8,128)(2,1)S(1)}, u32[]{:S(2)}, u32[]{:S(2)}) collective-permute-start(bf16[2,8,128,128]{3,2,1,0:T(8,128)(2,1)S(1)} %get-tuple-element.32), channel_id=1, source_target_pairs={{0,1},{1,0},{2,3},{3,2},{4,5},{5,4},{6,7},{7,6},{8,9},{9,8},{10,11... | collective-permute-start | bytes 1572872 | tf_op jit(solution)/shard_map/ppermute | solution.py:351
  3.5 1.6 %collective-permute-start = (f32[8,16,128]{2,1,0:T(8,128)S(1)}, f32[8,16,128]{2,1,0:T(8,128)S(1)}, u32[]{:S(2)}, u32[]{:S(2)}) collective-permute-start(f32[8,16,128]{2,1,0:T(8,128)S(1)} %get-tuple-element.24.own_ref), channel_id=1, source_target_pairs={{0,1},{1,0},{2,3},{3,2},{4,5},{5,4},{6,7},{7,6},{8,9},{9,8},{10,11... | collective-permute-start | bytes 196616 | tf_op jit(solution)/shard_map/ppermute | solution.py:372
  5.1 15.1 %copy-start = (bf16[24,128,256]{2,1,0:T(8,128)(2,1)S(1)}, bf16[24,128,256]{2,1,0:T(8,128)(2,1)}, u32[]{:S(2)}) copy-start(bf16[24,128,256]{2,1,0:T(8,128)(2,1)} %blocks_ref.1) | copy-start | bytes 4718596
  5.1 15.1 %copy-start.2 = (s32[24,2]{0,1:T(2,128)S(1)}, s32[24,2]{0,1:T(2,128)}, u32[]{:S(2)}) copy-start(s32[24,2]{0,1:T(2,128)} %param.11) | copy-start | bytes 580
  5.4 4.9 %collective-permute-start.1 = (s16[9,16,128]{2,1,0:T(8,128)(2,1)S(1)}, s16[9,16,128]{2,1,0:T(8,128)(2,1)S(1)}, u32[]{:S(2)}, u32[]{:S(2)}) collective-permute-start(s16[9,16,128]{2,1,0:T(8,128)(2,1)S(1)} %get-tuple-element.29), channel_id=1, source_target_pairs={{0,2},{1,3},{2,0},{3,1},{4,6},{5,7},{6,4},{7,5},{8,10},{9,11},{10,... | collective-permute-start | bytes 110600 | tf_op jit(solution)/shard_map/ppermute | solution.py:372
  10.6 6.8 %collective-permute-start.2 = (f32[8,16,128]{2,1,0:T(8,128)S(1)}, f32[8,16,128]{2,1,0:T(8,128)S(1)}, u32[]{:S(2)}, u32[]{:S(2)}) collective-permute-start(f32[8,16,128]{2,1,0:T(8,128)S(1)} %get-tuple-element.30), channel_id=1, source_target_pairs={{0,1},{1,0},{2,3},{3,2},{4,5},{5,4},{6,7},{7,6},{8,9},{9,8},{10,11... | collective-permute-start | bytes 196616 | tf_op jit(solution)/shard_map/ppermute | solution.py:374
  10.7 6.7 %collective-permute-start.3 = (s16[9,16,128]{2,1,0:T(8,128)(2,1)S(1)}, s16[9,16,128]{2,1,0:T(8,128)(2,1)S(1)}, u32[]{:S(2)}, u32[]{:S(2)}) collective-permute-start(s16[9,16,128]{2,1,0:T(8,128)(2,1)S(1)} %get-tuple-element.31), channel_id=1, source_target_pairs={{0,5},{1,4},{2,7},{3,6},{4,1},{5,0},{6,3},{7,2},{8,13},{9,12},{10,... | collective-permute-start | bytes 110600 | tf_op jit(solution)/shard_map/ppermute | solution.py:372
  12.8 5.0 %collective-permute-start.8 = (bf16[32,1024]{1,0:T(8,128)(2,1)S(1)}, bf16[32,1024]{1,0:T(8,128)(2,1)S(1)}, u32[]{:S(2)}, u32[]{:S(2)}) collective-permute-start(bf16[32,1024]{1,0:T(8,128)(2,1)S(1)} %get-tuple-element.38), channel_id=1, source_target_pairs={{0,1},{1,0},{2,3},{3,2},{4,5},{5,4},{6,7},{7,6},{8,9},{9,8},{10,11... | collective-permute-start | bytes 196616 | tf_op jit(solution)/shard_map/ppermute | solution.py:330
  12.9 7.3 %collective-permute-start.9 = (bf16[32,1024]{1,0:T(8,128)(2,1)S(1)}, bf16[32,1024]{1,0:T(8,128)(2,1)S(1)}, u32[]{:S(2)}, u32[]{:S(2)}) collective-permute-start(bf16[32,1024]{1,0:T(8,128)(2,1)S(1)} %get-tuple-element.39), channel_id=1, source_target_pairs={{0,31},{1,2},{2,1},{3,4},{4,3},{5,6},{6,5},{7,8},{8,7},{9,10},{10,... | collective-permute-start | bytes 196616 | tf_op jit(solution)/shard_map/ppermute | solution.py:331
  17.8 4.0 %collective-permute-start.5 = (s16[9,16,128]{2,1,0:T(8,128)(2,1)S(1)}, s16[9,16,128]{2,1,0:T(8,128)(2,1)S(1)}, u32[]{:S(2)}, u32[]{:S(2)}) collective-permute-start(s16[9,16,128]{2,1,0:T(8,128)(2,1)S(1)} %get-tuple-element.34), channel_id=1, source_target_pairs={{0,8},{1,9},{2,10},{3,11},{4,12},{5,13},{6,14},{7,15},{8,0},{9,1},... | collective-permute-start | bytes 110600 | tf_op jit(solution)/shard_map/ppermute | solution.py:372
  20.2 10.7 %copy-start.1 = (bf16[64,2048]{1,0:T(8,128)(2,1)S(1)}, bf16[64,2048]{1,0:T(8,128)(2,1)}, u32[]{:S(2)}) copy-start(bf16[64,2048]{1,0:T(8,128)(2,1)} %basis_ref.1) | copy-start | bytes 786436
  21.2 8.5 %collective-permute-start.10 = (f32[4,32,128]{2,1,0:T(8,128)S(1)}, f32[4,32,128]{2,1,0:T(8,128)S(1)}, u32[]{:S(2)}, u32[]{:S(2)}) collective-permute-start(f32[4,32,128]{2,1,0:T(8,128)S(1)} %get-tuple-element.41), channel_id=1, source_target_pairs={{0,1},{1,0},{2,3},{3,2},{4,5},{5,4},{6,7},{7,6},{8,9},{9,8},{10,11... | collective-permute-start | bytes 196616 | tf_op jit(solution)/shard_map/ppermute | solution.py:366
  22.1 8.9 %collective-permute-start.6 = (f32[8,16,128]{2,1,0:T(8,128)S(1)}, f32[8,16,128]{2,1,0:T(8,128)S(1)}, u32[]{:S(2)}, u32[]{:S(2)}) collective-permute-start(f32[8,16,128]{2,1,0:T(8,128)S(1)} %get-tuple-element.35), channel_id=1, source_target_pairs={{0,1},{1,0},{2,3},{3,2},{4,5},{5,4},{6,7},{7,6},{8,9},{9,8},{10,11... | collective-permute-start | bytes 196616 | tf_op jit(solution)/shard_map/ppermute | solution.py:374
  22.2 7.5 %collective-permute-start.11 = (s16[5,32,128]{2,1,0:T(8,128)(2,1)S(1)}, s16[5,32,128]{2,1,0:T(8,128)(2,1)S(1)}, u32[]{:S(2)}, u32[]{:S(2)}) collective-permute-start(s16[5,32,128]{2,1,0:T(8,128)(2,1)S(1)} %get-tuple-element.42), channel_id=1, source_target_pairs={{0,31},{1,2},{2,1},{3,4},{4,3},{5,6},{6,5},{7,8},{8,7},{9,10},{10,... | collective-permute-start | bytes 122888 | tf_op jit(solution)/shard_map/ppermute | solution.py:367
  26.7 4.3 %collective-permute-start.7 = (s16[9,16,128]{2,1,0:T(8,128)(2,1)S(1)}, s16[9,16,128]{2,1,0:T(8,128)(2,1)S(1)}, u32[]{:S(2)}, u32[]{:S(2)}) collective-permute-start(s16[9,16,128]{2,1,0:T(8,128)(2,1)S(1)} %get-tuple-element.36), channel_id=1, source_target_pairs={{0,17},{1,16},{2,19},{3,18},{4,21},{5,20},{6,23},{7,22},{8,25},{9,... | collective-permute-start | bytes 110600 | tf_op jit(solution)/shard_map/ppermute | solution.py:372

commit v7 on v6

--- a/solution.py
+++ b/solution.py
@@ -87,12 +87,14 @@
     signal_hbm,
     basis_hbm,
     transfer_hbm,
+    list_hbm,
     out_ref,
     signal_ref,
     transfer_ref,
     table_ref,
     to_pair_ref,
     to_ring_ref,
+    list_ref,
     basis_ref,
     arrived,
 ):
@@ -106,6 +108,7 @@
         pltpu.make_async_copy(basis_hbm, basis_ref, arrived.at[1]),
         pltpu.make_async_copy(transfer_hbm.at[:, near_levels], transfer_ref.at[:, near_levels], arrived.at[2]),
         pltpu.make_async_copy(transfer_hbm.at[:, far_levels], transfer_ref.at[:, far_levels], arrived.at[3]),
+        pltpu.make_async_copy(list_hbm, list_ref, arrived.at[4]),
     ]
     for copy in copies[:3]:
         copy.start()
@@ -122,7 +125,8 @@
     for box in range(0, boxes, 2):
         state[box] = project_pair(signal_ref, basis_ref, box, box + 1)
     copies[2].wait()
-    copies[3].start()
+    for copy in copies[3:]:
+        copy.start()
     table = table_ref[...]
     for level in range(levels):
         bit = 1 << level
@@ -143,7 +147,8 @@
                 state[box + bit] = pick_low(half_roll(done[box]), done[other])
     for box, pair in state.items():
         out_ref[box] = pair
-    copies[3].wait()
+    for copy in copies[3:]:
+        copy.wait()
 
 
 def matrices_kernel(transfer_ref, table_ref, own_ref, lent_ref, *, own_levels, lent_levels):
@@ -308,7 +313,7 @@
 
     halo = 2 * reach * LEAF
     state = ((half, rhs, width), F32)
-    coeffs, signal, transfer, table, to_pair, to_ring = pl.pallas_call(
+    coeffs, signal, transfer, table, to_pair, to_ring, slots = pl.pallas_call(
         local_kernel,
         out_shape=(
             pltpu.VMEM(*state),
@@ -317,15 +322,16 @@
             pltpu.VMEM((2 * width, 4 * width), BF16),
             pltpu.VMEM((channels, halo), BF16),
             pltpu.VMEM((channels, halo), BF16),
-        ),
-        in_specs=[SMEM] + [pl.BlockSpec(memory_space=pl.ANY)] * 3,
-        out_specs=(VMEM,) * 6,
-        scratch_shapes=[pltpu.VMEM(row_basis.shape, BF16), pltpu.SemaphoreType.DMA((4,))],
+            pltpu.SMEM(near_list.shape[::-1], jnp.int32),
+        ),
+        in_specs=[SMEM] + [pl.BlockSpec(memory_space=pl.ANY)] * 4,
+        out_specs=(VMEM,) * 6 + (SMEM,),
+        scratch_shapes=[pltpu.VMEM(row_basis.shape, BF16), pltpu.SemaphoreType.DMA((5,))],
         compiler_params=pltpu.CompilerParams(vmem_limit_bytes=16 << 20),
         name="local",
     )(
         index_word,
-        *[pltpu.with_memory_space_constraint(x, pltpu.HBM) for x in (signal, row_basis, transfer)],
+        *[pltpu.with_memory_space_constraint(x, pltpu.HBM) for x in (signal, row_basis, transfer, near_list.T)],
     )
     from_pair = lax.ppermute(to_pair, AXES, pairs)
     from_ring = lax.ppermute(to_ring, AXES, ring)
@@ -356,7 +362,7 @@
             ((reach, channels, LEAF), F32),
             ((reach + 1, channels, LEAF), jnp.int16),
         ),
-        (index_word, near_list.T),
+        (index_word, pltpu.with_memory_space_constraint(slots, pltpu.SMEM)),
         (signal, from_pair, from_ring, near_blocks),
         scratch=(
             pltpu.VMEM((boxes + 4 * reach, channels, LEAF), BF16),
@@ -401,7 +407,7 @@
     return [int(level - levels in CROSSED) for level in range(levels)]
 
 
-CROSSED = (-3, -1)
+CROSSED = (-4, -3, -2, -1)
 
 
 def solution(mesh):

time: 32.3 us -> 31.8 us (0.985)
  Pallas kernels: 6.35 us -> 5.82 us
    ppermute x2 -> x4, starting transfers between devices: 0.16 us -> 1.2 us  [shards(): coeffs = lax.ppermute(coeffs, AXES, pairs)]
    ppermute x5, starting transfers between devices: 5.22 us -> 4.43 us  [shards(): other = lax.ppermute(sent, AXES, [(i, i ^ flip) for i in range(devices)])]
    ppermute x5, waiting for transfers between devices: 5.25 us -> 4.7 us  [shards(): other = lax.ppermute(sent, AXES, [(i, i ^ flip) for i in range(devices)])]
    pallas_call x6, Pallas kernels: 2.71 us -> 2.16 us  [on_chip(): call(*scalars, *[pltpu.with_memory_space_constraint(x, pltpu.VMEM) for x...]
  transfers between devices with their start and end apart: 12 -> 14, of which waited for: 6 -> 6; matrix products, arithmetic and copies ran while one was open for 0% -> 0% of each run, Pallas kernels for 7% -> 4%
where the time goes in v7:
time: 31.8 us; the launch traced here: 31.6 us
  starting transfers between devices  15.3 us (48%)
  waiting for transfers between devices  10.4 us (33%)
  Pallas kernels  5.82 us (18%)
    ppermute x5, waiting for transfers between devices, shards(): other = lax.ppermute(sent, AXES, [(i, i ^ flip) for i in range(devices)])  4.7 us
    ppermute x1, starting transfers between devices, shards(): rim_from_ring = lax.ppermute(rim_ring, AXES, ring)  4.44 us
    ppermute x5, starting transfers between devices, shards(): other = lax.ppermute(sent, AXES, [(i, i ^ flip) for i in range(devices)])  4.43 us
    ppermute x1, starting transfers between devices, shards(): from_ring = lax.ppermute(to_ring, AXES, ring)  4.21 us
    ppermute x1, waiting for transfers between devices, shards(): rim_from_ring = lax.ppermute(rim_ring, AXES, ring)  3.08 us
    ppermute x1, waiting for transfers between devices, shards(): from_ring = lax.ppermute(to_ring, AXES, ring)  2.59 us
    pallas_call x1, Pallas kernels, shards(): pl.pallas_call(local_kernel, out_shape=(pltpu.VMEM(*state), pltpu.VMEM(si...  2.45 us
    pallas_call x6, Pallas kernels, on_chip(): call(*scalars, *[pltpu.with_memory_space_constraint(x, pltpu.VMEM) for x...  2.16 us
  transfers between devices with their start and end apart: 14, of which 6 were waited for; matrix products, arithmetic and copies ran while one was open for 0% of the time, Pallas kernels for 4%

profile of v7, /device:TPU:0, one launch (start us, length us, event | category | flops | bytes accessed | tf_op | source)
XLA Modules:
  0.0 31.6 jit_solution(11617240820262657)
XLA Ops:
  0.0 2.4 %local.1 = (f32[8,16,128]{2,1,0:T(8,128)S(1)}, bf16[32,2048]{1,0:T(8,128)(2,1)S(1)}, bf16[16,9,32,128]{3,2,1,0:T(8,128)(2,1)S(1)}, bf16[256,512]{1,0:T(8,128)(2,...) custom-call(s32[1]{0:T(128)} %bitcast.index_ref, ...), custom_call_target="tpu_custom_call" | custom-call | tf_op jit(solution)/shard_map/local/pallas_call | solution.py:316
  2.5 0.5 %shard_map.64 = (bf16[3,8,128,128]{3,2,1,0:T(8,128)(2,1)S(1)}, bf16[2,8,128,128]{3,2,1,0:T(8,128)(2,1)S(1)}) custom-call(bf16[16,9,32,128]{3,2,1,0:T(8,128)(2,1)S(1)} %get-tuple-element.26.transfer_ref, bf16[256,512]{1,0:T(8,128)(2,1)S(1)} %get-tuple-element.27.table_ref), custom_call_target="tpu_custom_call" | custom-call | tf_op jit(solution)/shard_map/pallas_call | solution.py:297
  3.0 0.6 %collective-permute-start.3 = (bf16[2,8,128,128]{3,2,1,0:T(8,128)(2,1)S(1)}, bf16[2,8,128,128]{3,2,1,0:T(8,128)(2,1)S(1)}, u32[]{:S(2)}, u32[]{:S(2)}) collective-permute-start(bf16[2,8,128,128]{3,2,1,0:T(8,128)(2,1)S(1)} %get-tuple-element.31), channel_id=1, source_target_pairs={{0,1},{1,0},{2,3},{3,2},{4,5},{5,4},{6,7},{7,6},{8,9},{9,8},{10,11... | collective-permute-start | bytes 1572872 | tf_op jit(solution)/shard_map/ppermute | solution.py:357
  3.5 0.1 collective-permute-start
  3.6 1.6 %collective-permute-done.other_ref = f32[8,16,128]{2,1,0:T(8,128)S(1)} collective-permute-done((f32[8,16,128]{2,1,0:T(8,128)S(1)}, f32[8,16,128]{2,1,0:T(8,128)S(1)}, u32[]{:S(2)}, u32[]{:S(2)}) %collective-permute-start) | collective-permute-done | bytes 65568 | tf_op jit(solution)/shard_map/ppermute | solution.py:378
  5.2 0.0 copy-start
  5.2 0.3 shard_map.65
  5.5 0.4 %collective-permute-start.1 = (f32[8,16,128]{2,1,0:T(8,128)S(1)}, f32[8,16,128]{2,1,0:T(8,128)S(1)}, u32[]{:S(2)}, u32[]{:S(2)}) collective-permute-start(f32[8,16,128]{2,1,0:T(8,128)S(1)} %get-tuple-element.29), channel_id=1, source_target_pairs={{0,1},{1,0},{2,3},{3,2},{4,5},{5,4},{6,7},{7,6},{8,9},{9,8},{10,11... | collective-permute-start | bytes 196616 | tf_op jit(solution)/shard_map/ppermute | solution.py:380
  5.9 2.6 %collective-permute-start.2 = (s16[9,16,128]{2,1,0:T(8,128)(2,1)S(1)}, s16[9,16,128]{2,1,0:T(8,128)(2,1)S(1)}, u32[]{:S(2)}, u32[]{:S(2)}) collective-permute-start(s16[9,16,128]{2,1,0:T(8,128)(2,1)S(1)} %get-tuple-element.30), channel_id=1, source_target_pairs={{0,3},{1,2},{2,1},{3,0},{4,7},{5,6},{6,5},{7,4},{8,11},{9,10},{10,... | collective-permute-start | bytes 110600 | tf_op jit(solution)/shard_map/ppermute | solution.py:378
  8.5 1.7 %collective-permute-done.2.other_ref = s16[9,16,128]{2,1,0:T(8,128)(2,1)S(1)} collective-permute-done((s16[9,16,128]{2,1,0:T(8,128)(2,1)S(1)}, s16[9,16,128]{2,1,0:T(8,128)(2,1)S(1)}, u32[]{:S(2)}, u32[]{:S(2)}) %collective-permute-start.2) | collective-permute-done | bytes 36896 | tf_op jit(solution)/shard_map/ppermute | solution.py:378
  10.2 0.0 collective-permute-done.1.own_ref
  10.2 0.0 collective-permute-done.3.matrices_ref
  10.2 0.3 shard_map.66
  10.5 0.2 collective-permute-start.4
  10.7 1.7 %collective-permute-start.5 = (s16[9,16,128]{2,1,0:T(8,128)(2,1)S(1)}, s16[9,16,128]{2,1,0:T(8,128)(2,1)S(1)}, u32[]{:S(2)}, u32[]{:S(2)}) collective-permute-start(s16[9,16,128]{2,1,0:T(8,128)(2,1)S(1)} %get-tuple-element.33), channel_id=1, source_target_pairs={{0,5},{1,4},{2,7},{3,6},{4,1},{5,0},{6,3},{7,2},{8,13},{9,12},{10,... | collective-permute-start | bytes 110600 | tf_op jit(solution)/shard_map/ppermute | solution.py:378
  12.4 0.4 %collective-permute-start.10 = (bf16[32,1024]{1,0:T(8,128)(2,1)S(1)}, bf16[32,1024]{1,0:T(8,128)(2,1)S(1)}, u32[]{:S(2)}, u32[]{:S(2)}) collective-permute-start(bf16[32,1024]{1,0:T(8,128)(2,1)S(1)} %get-tuple-element.40), channel_id=1, source_target_pairs={{0,1},{1,0},{2,3},{3,2},{4,5},{5,4},{6,7},{7,6},{8,9},{9,8},{10,11... | collective-permute-start | bytes 196616 | tf_op jit(solution)/shard_map/ppermute | solution.py:336
  12.8 4.2 %collective-permute-start.11 = (bf16[32,1024]{1,0:T(8,128)(2,1)S(1)}, bf16[32,1024]{1,0:T(8,128)(2,1)S(1)}, u32[]{:S(2)}, u32[]{:S(2)}) collective-permute-start(bf16[32,1024]{1,0:T(8,128)(2,1)S(1)} %get-tuple-element.41), channel_id=1, source_target_pairs={{0,31},{1,2},{2,1},{3,4},{4,3},{5,6},{6,5},{7,8},{8,7},{9,10},{10,... | collective-permute-start | bytes 196616 | tf_op jit(solution)/shard_map/ppermute | solution.py:337
  17.0 0.0 collective-permute-done.5.other_ref
  17.0 0.0 collective-permute-done.4.own_ref
  17.0 0.3 shard_map.67
  17.3 0.1 collective-permute-start.6
  17.4 0.1 collective-permute-start.7
  17.5 0.0 collective-permute-done.10.pair_ref
  17.5 2.6 %collective-permute-done.11.ring_ref = bf16[32,1024]{1,0:T(8,128)(2,1)S(1)} collective-permute-done((bf16[32,1024]{1,0:T(8,128)(2,1)S(1)}, bf16[32,1024]{1,0:T(8,128)(2,1)S(1)}, u32[]{:S(2)}, u32[]{:S(2)}) %collective-permute-start.11) | collective-permute-done | bytes 65568 | tf_op jit(solution)/shard_map/ppermute | solution.py:337
  20.1 0.0 copy-done
  20.1 0.0 copy-start.1
  20.1 0.4 %shard_map.69 = (f32[16,32,128]{2,1,0:T(8,128)S(1)}, f32[4,32,128]{2,1,0:T(8,128)S(1)}, s16[5,32,128]{2,1,0:T(8,128)(2,1)S(1)}) custom-call(s32[1]{0:T(128)} %bitcast.index_ref, s32[2,24]{1,0:T(2,128)S(4)} %get-tuple-element.38.list_ref, bf16[32,2048]{1,0:T(8,128)(2,1)S(1)} %get-tuple-element.39.signal_ref, ...), custom_call_target="tpu_custom_call" | custom-call | tf_op jit(solution)/shard_map/pallas_call | solution.py:297
  20.5 0.1 collective-permute-start.12
  20.6 0.2 collective-permute-done.7.other_ref
  20.9 0.0 collective-permute-done.6.own_ref
  20.9 0.3 shard_map.68
  21.2 0.5 %collective-permute-start.8 = (f32[8,16,128]{2,1,0:T(8,128)S(1)}, f32[8,16,128]{2,1,0:T(8,128)S(1)}, u32[]{:S(2)}, u32[]{:S(2)}) collective-permute-start(f32[8,16,128]{2,1,0:T(8,128)S(1)} %get-tuple-element.36), channel_id=1, source_target_pairs={{0,1},{1,0},{2,3},{3,2},{4,5},{5,4},{6,7},{7,6},{8,9},{9,8},{10,11... | collective-permute-start | bytes 196616 | tf_op jit(solution)/shard_map/ppermute | solution.py:380
  21.7 4.4 %collective-permute-start.13 = (s16[5,32,128]{2,1,0:T(8,128)(2,1)S(1)}, s16[5,32,128]{2,1,0:T(8,128)(2,1)S(1)}, u32[]{:S(2)}, u32[]{:S(2)}) collective-permute-start(s16[5,32,128]{2,1,0:T(8,128)(2,1)S(1)} %get-tuple-element.44), channel_id=1, source_target_pairs={{0,31},{1,2},{2,1},{3,4},{4,3},{5,6},{6,5},{7,8},{8,7},{9,10},{10,... | collective-permute-start | bytes 122888 | tf_op jit(solution)/shard_map/ppermute | solution.py:373
  26.1 0.0 collective-permute-start.9
  26.1 3.1 %collective-permute-done.13.ring_ref = s16[5,32,128]{2,1,0:T(8,128)(2,1)S(1)} collective-permute-done((s16[5,32,128]{2,1,0:T(8,128)(2,1)S(1)}, s16[5,32,128]{2,1,0:T(8,128)(2,1)S(1)}, u32[]{:S(2)}, u32[]{:S(2)}) %collective-permute-start.13) | collective-permute-done | bytes 40992 | tf_op jit(solution)/shard_map/ppermute | solution.py:373
  29.2 0.0 collective-permute-done.12.pair_ref
  29.2 1.2 %collective-permute-done.9.other_ref = s16[9,16,128]{2,1,0:T(8,128)(2,1)S(1)} collective-permute-done((s16[9,16,128]{2,1,0:T(8,128)(2,1)S(1)}, s16[9,16,128]{2,1,0:T(8,128)(2,1)S(1)}, u32[]{:S(2)}, u32[]{:S(2)}) %collective-permute-start.9) | collective-permute-done | bytes 36896 | tf_op jit(solution)/shard_map/ppermute | solution.py:378
  30.4 0.0 collective-permute-done.8.own_ref
  30.4 0.0 copy-done.1
  30.4 1.2 %final.1 = f32[32,2048]{1,0:T(8,128)} custom-call(s32[1]{0:T(128)} %bitcast.index_ref, f32[8,16,128]{2,1,0:T(8,128)S(1)} %collective-permute-done.8.own_ref, s16[9,16,128]{2,1,0:T(8,128)(2,1)S(1)} %collective-permute-done.9.other_ref, bf16[3,8,128,128]{3,2,1,0:T(8,128)(2,1)S(1)} %get-tuple-element.28.matrices_ref, bf16[64,2048]{1,0:T(8,128)(2,1)S(1)} %copy-done.1, ...), custom_call_target="tpu_custom_call" | custom-call | tf_op jit(solution)/shard_map/final/pallas_call | solution.py:390
Async XLA Ops:
  3.0 7.3 %collective-permute-start.3 = (bf16[2,8,128,128]{3,2,1,0:T(8,128)(2,1)S(1)}, bf16[2,8,128,128]{3,2,1,0:T(8,128)(2,1)S(1)}, u32[]{:S(2)}, u32[]{:S(2)}) collective-permute-start(bf16[2,8,128,128]{3,2,1,0:T(8,128)(2,1)S(1)} %get-tuple-element.31), channel_id=1, source_target_pairs={{0,1},{1,0},{2,3},{3,2},{4,5},{5,4},{6,7},{7,6},{8,9},{9,8},{10,11... | collective-permute-start | bytes 1572872 | tf_op jit(solution)/shard_map/ppermute | solution.py:357
  3.5 1.6 %collective-permute-start = (f32[8,16,128]{2,1,0:T(8,128)S(1)}, f32[8,16,128]{2,1,0:T(8,128)S(1)}, u32[]{:S(2)}, u32[]{:S(2)}) collective-permute-start(f32[8,16,128]{2,1,0:T(8,128)S(1)} %get-tuple-element.25.own_ref), channel_id=1, source_target_pairs={{0,1},{1,0},{2,3},{3,2},{4,5},{5,4},{6,7},{7,6},{8,9},{9,8},{10,11... | collective-permute-start | bytes 196616 | tf_op jit(solution)/shard_map/ppermute | solution.py:378
  5.2 14.9 %copy-start = (bf16[24,128,256]{2,1,0:T(8,128)(2,1)S(1)}, bf16[24,128,256]{2,1,0:T(8,128)(2,1)}, u32[]{:S(2)}) copy-start(bf16[24,128,256]{2,1,0:T(8,128)(2,1)} %blocks_ref.1) | copy-start | bytes 4718596
  5.5 4.8 %collective-permute-start.1 = (f32[8,16,128]{2,1,0:T(8,128)S(1)}, f32[8,16,128]{2,1,0:T(8,128)S(1)}, u32[]{:S(2)}, u32[]{:S(2)}) collective-permute-start(f32[8,16,128]{2,1,0:T(8,128)S(1)} %get-tuple-element.29), channel_id=1, source_target_pairs={{0,1},{1,0},{2,3},{3,2},{4,5},{5,4},{6,7},{7,6},{8,9},{9,8},{10,11... | collective-permute-start | bytes 196616 | tf_op jit(solution)/shard_map/ppermute | solution.py:380
  5.9 4.3 %collective-permute-start.2 = (s16[9,16,128]{2,1,0:T(8,128)(2,1)S(1)}, s16[9,16,128]{2,1,0:T(8,128)(2,1)S(1)}, u32[]{:S(2)}, u32[]{:S(2)}) collective-permute-start(s16[9,16,128]{2,1,0:T(8,128)(2,1)S(1)} %get-tuple-element.30), channel_id=1, source_target_pairs={{0,3},{1,2},{2,1},{3,0},{4,7},{5,6},{6,5},{7,4},{8,11},{9,10},{10,... | collective-permute-start | bytes 110600 | tf_op jit(solution)/shard_map/ppermute | solution.py:378
  10.5 6.5 %collective-permute-start.4 = (f32[8,16,128]{2,1,0:T(8,128)S(1)}, f32[8,16,128]{2,1,0:T(8,128)S(1)}, u32[]{:S(2)}, u32[]{:S(2)}) collective-permute-start(f32[8,16,128]{2,1,0:T(8,128)S(1)} %get-tuple-element.32), channel_id=1, source_target_pairs={{0,1},{1,0},{2,3},{3,2},{4,5},{5,4},{6,7},{7,6},{8,9},{9,8},{10,11... | collective-permute-start | bytes 196616 | tf_op jit(solution)/shard_map/ppermute | solution.py:380
  10.7 6.3 %collective-permute-start.5 = (s16[9,16,128]{2,1,0:T(8,128)(2,1)S(1)}, s16[9,16,128]{2,1,0:T(8,128)(2,1)S(1)}, u32[]{:S(2)}, u32[]{:S(2)}) collective-permute-start(s16[9,16,128]{2,1,0:T(8,128)(2,1)S(1)} %get-tuple-element.33), channel_id=1, source_target_pairs={{0,5},{1,4},{2,7},{3,6},{4,1},{5,0},{6,3},{7,2},{8,13},{9,12},{10,... | collective-permute-start | bytes 110600 | tf_op jit(solution)/shard_map/ppermute | solution.py:378
  12.4 5.1 %collective-permute-start.10 = (bf16[32,1024]{1,0:T(8,128)(2,1)S(1)}, bf16[32,1024]{1,0:T(8,128)(2,1)S(1)}, u32[]{:S(2)}, u32[]{:S(2)}) collective-permute-start(bf16[32,1024]{1,0:T(8,128)(2,1)S(1)} %get-tuple-element.40), channel_id=1, source_target_pairs={{0,1},{1,0},{2,3},{3,2},{4,5},{5,4},{6,7},{7,6},{8,9},{9,8},{10,11... | collective-permute-start | bytes 196616 | tf_op jit(solution)/shard_map/ppermute | solution.py:336
  12.8 7.3 %collective-permute-start.11 = (bf16[32,1024]{1,0:T(8,128)(2,1)S(1)}, bf16[32,1024]{1,0:T(8,128)(2,1)S(1)}, u32[]{:S(2)}, u32[]{:S(2)}) collective-permute-start(bf16[32,1024]{1,0:T(8,128)(2,1)S(1)} %get-tuple-element.41), channel_id=1, source_target_pairs={{0,31},{1,2},{2,1},{3,4},{4,3},{5,6},{6,5},{7,8},{8,7},{9,10},{10,... | collective-permute-start | bytes 196616 | tf_op jit(solution)/shard_map/ppermute | solution.py:337
  17.3 3.5 %collective-permute-start.6 = (f32[8,16,128]{2,1,0:T(8,128)S(1)}, f32[8,16,128]{2,1,0:T(8,128)S(1)}, u32[]{:S(2)}, u32[]{:S(2)}) collective-permute-start(f32[8,16,128]{2,1,0:T(8,128)S(1)} %get-tuple-element.34), channel_id=1, source_target_pairs={{0,1},{1,0},{2,3},{3,2},{4,5},{5,4},{6,7},{7,6},{8,9},{9,8},{10,11... | collective-permute-start | bytes 196616 | tf_op jit(solution)/shard_map/ppermute | solution.py:380
  17.4 3.4 %collective-permute-start.7 = (s16[9,16,128]{2,1,0:T(8,128)(2,1)S(1)}, s16[9,16,128]{2,1,0:T(8,128)(2,1)S(1)}, u32[]{:S(2)}, u32[]{:S(2)}) collective-permute-start(s16[9,16,128]{2,1,0:T(8,128)(2,1)S(1)} %get-tuple-element.35), channel_id=1, source_target_pairs={{0,9},{1,8},{2,11},{3,10},{4,13},{5,12},{6,15},{7,14},{8,1},{9,0},... | collective-permute-start | bytes 110600 | tf_op jit(solution)/shard_map/ppermute | solution.py:378
  20.1 10.3 %copy-start.1 = (bf16[64,2048]{1,0:T(8,128)(2,1)S(1)}, bf16[64,2048]{1,0:T(8,128)(2,1)}, u32[]{:S(2)}) copy-start(bf16[64,2048]{1,0:T(8,128)(2,1)} %basis_ref.1) | copy-start | bytes 786436
  20.5 8.6 %collective-permute-start.12 = (f32[4,32,128]{2,1,0:T(8,128)S(1)}, f32[4,32,128]{2,1,0:T(8,128)S(1)}, u32[]{:S(2)}, u32[]{:S(2)}) collective-permute-start(f32[4,32,128]{2,1,0:T(8,128)S(1)} %get-tuple-element.43), channel_id=1, source_target_pairs={{0,1},{1,0},{2,3},{3,2},{4,5},{5,4},{6,7},{7,6},{8,9},{9,8},{10,11... | collective-permute-start | bytes 196616 | tf_op jit(solution)/shard_map/ppermute | solution.py:372
  21.2 9.2 %collective-permute-start.8 = (f32[8,16,128]{2,1,0:T(8,128)S(1)}, f32[8,16,128]{2,1,0:T(8,128)S(1)}, u32[]{:S(2)}, u32[]{:S(2)}) collective-permute-start(f32[8,16,128]{2,1,0:T(8,128)S(1)} %get-tuple-element.36), channel_id=1, source_target_pairs={{0,1},{1,0},{2,3},{3,2},{4,5},{5,4},{6,7},{7,6},{8,9},{9,8},{10,11... | collective-permute-start | bytes 196616 | tf_op jit(solution)/shard_map/ppermute | solution.py:380
  21.7 7.5 %collective-permute-start.13 = (s16[5,32,128]{2,1,0:T(8,128)(2,1)S(1)}, s16[5,32,128]{2,1,0:T(8,128)(2,1)S(1)}, u32[]{:S(2)}, u32[]{:S(2)}) collective-permute-start(s16[5,32,128]{2,1,0:T(8,128)(2,1)S(1)} %get-tuple-element.44), channel_id=1, source_target_pairs={{0,31},{1,2},{2,1},{3,4},{4,3},{5,6},{6,5},{7,8},{8,7},{9,10},{10,... | collective-permute-start | bytes 122888 | tf_op jit(solution)/shard_map/ppermute | solution.py:373
  26.1 4.3 %collective-permute-start.9 = (s16[9,16,128]{2,1,0:T(8,128)(2,1)S(1)}, s16[9,16,128]{2,1,0:T(8,128)(2,1)S(1)}, u32[]{:S(2)}, u32[]{:S(2)}) collective-permute-start(s16[9,16,128]{2,1,0:T(8,128)(2,1)S(1)} %get-tuple-element.37), channel_id=1, source_target_pairs={{0,17},{1,16},{2,19},{3,18},{4,21},{5,20},{6,23},{7,22},{8,25},{9,... | collective-permute-start | bytes 110600 | tf_op jit(solution)/shard_map/ppermute | solution.py:378
